TPU v7x, 128 devices: a whole 4x4x4 slice. The times are simulated.
128 devices in a mesh: tm: 8 (over y, core), ep: 16 (over x, z).
Axes of the slice: x: 4, y: 4, z: 4, core: 2. Of those that a mesh axis runs over, the one named last changes fastest.
Arguments:
- observations: bfloat16 [1024, 128, 1024], P('ep', 'tm'), may hold values from -6 to 6
- input_weight: bfloat16 [1024, 2048], replicated, may hold values from -0.1875 to 0.1875
- hidden_weight: bfloat16 [512, 2048], replicated, may hold values from -0.25 to 0.25
- gate_bias: float32 [2048], replicated, may hold values from -3 to 3
- forget_bias: float32 [512], replicated, may hold values from 0 to 5
- episode_ids: int32 [2048], P('ep'), may hold values from 0 to 63
- start_steps: int32 [2048], P('ep'), may hold values from 0 to 127
- priorities: int32 [2048], P('ep'), may hold values from 20 to 999
Outputs:
- train_rows: bfloat16 [2048, 128, 1024], P('ep', 'tm')
- start_state: bfloat16 [2048, 2, 512], P('ep')
- sample_weights: bfloat16 [2048], P('ep')
Inputs may be any that keep to these rules, and one draw needn't show every extreme that they name: `episode_ids`: slot index inside the storage shard that sampled the sequence.
All inputs are finite; a program needn't handle non-finite values.
Results may differ from a plain program's by a relative error of at most 0.009.
Values may be sent and summed in bfloat16 or wider, within the bound.
No kernel may reach another device: no remote copies, remote signals or barrier semaphores. Data moves between devices by JAX's collectives and lax.ppermute only.
A program may use at most 64 MiB of HBM per device.

v0:
```python
import jax
import jax.numpy as jnp
from jax import lax
from jax.sharding import Mesh
from jax.sharding import PartitionSpec as P

STEPS = 128
BURN = 40
UNROLL = 80
EP = ("ep_0", "ep_1")


IMPORTANCE = 0.6


def split_up(x, dim, devices):
    before, after = (x.shape[:dim], x.shape[dim + 1 :])
    return jnp.moveaxis(x.reshape(*before, devices, -1, *after), dim, 0)


def sum_at_owner(x, axis, dim):
    devices = lax.axis_size(axis)
    tiles = lax.all_to_all(split_up(x, dim, devices), axis, 0, 0, tiled=True)
    return jnp.sum(tiles.astype(jnp.float32), axis=0)


def one_axis_at_a_time(x, axes):
    for axis in axes:
        x = lax.pmax(x, axis)
    return x


def sent_together(arrays, axis, split_dim, concat_dim, along):
    columns = [a.reshape(*a.shape[:along], -1) for a in arrays]
    both = jnp.concatenate(columns, axis=along)
    whole, at, gathered = (
        lax.all_to_all(both, axis, split_axis=split_dim, concat_axis=concat_dim, tiled=True),
        0,
        [],
    )
    for a, column in zip(arrays, columns):
        piece = whole[..., at : at + column.shape[along]]
        gathered.append(piece.reshape(*piece.shape[:along], *a.shape[along:]))
        at += column.shape[along]
    return tuple(gathered)


def joined_along(tiles, dim):
    tiles = jnp.moveaxis(tiles, 0, dim)
    lengths = tiles.shape
    return tiles.reshape(*lengths[:dim], lengths[dim] * lengths[dim + 1], *lengths[dim + 2 :])


def sent_to_all(x, axis):
    copies = jnp.broadcast_to(x, (lax.axis_size(axis), *x.shape))
    return lax.all_to_all(copies, axis, split_axis=0, concat_axis=0, tiled=True)


def collect(x, axis, dim):
    return joined_along(sent_to_all(x, axis), dim)


def lstm_step(state_pair, projected, hidden_weight, gate_bias, forget_bias):
    hidden, cell_state = state_pair
    hidden_width = hidden.shape[-1]
    gate_sum = (
        projected
        + jnp.dot(hidden.astype(jnp.bfloat16), hidden_weight, preferred_element_type=jnp.float32)
        + gate_bias
    )
    ingate = gate_sum[:, :hidden_width]
    forget = gate_sum[:, hidden_width : 2 * hidden_width]
    candidate = gate_sum[:, 2 * hidden_width : 3 * hidden_width]
    outgate = gate_sum[:, 3 * hidden_width :]
    cell_state = jax.nn.sigmoid(forget + forget_bias) * cell_state + jax.nn.sigmoid(
        ingate
    ) * jnp.tanh(candidate)
    hidden = jax.nn.sigmoid(outgate) * jnp.tanh(cell_state)
    return (hidden, cell_state)


def body(
    observations,
    input_weight,
    hidden_weight,
    gate_bias,
    forget_bias,
    episode_ids,
    start_steps,
    priorities,
):
    shard_steps = observations.shape[1]
    seq_count = episode_ids.shape[0]
    hidden_width = hidden_weight.shape[0]
    time_shards = lax.axis_size("tm")
    position = lax.axis_index("tm")
    stored_rows = observations[episode_ids]
    local_steps = position * shard_steps + jnp.arange(shard_steps, dtype=jnp.int32)
    offsets = (local_steps[None, :] - start_steps[:, None]) % STEPS
    own_count = seq_count // time_shards
    whole_slots = lax.all_to_all(stored_rows, "tm", split_axis=0, concat_axis=1, tiled=True)
    own_starts = lax.dynamic_slice_in_dim(start_steps, position * own_count, own_count)
    burn_steps = (own_starts[None, :] + jnp.arange(BURN, dtype=jnp.int32)[:, None]) % STEPS
    own_index = jnp.broadcast_to(jnp.arange(own_count, dtype=jnp.int32)[None, :], burn_steps.shape)
    burn_inputs = whole_slots[own_index, burn_steps]
    burn_projected = jnp.dot(
        burn_inputs.reshape(BURN * own_count, burn_inputs.shape[2]),
        input_weight,
        preferred_element_type=jnp.float32,
    ).reshape(BURN, own_count, -1)

    def warm(state_pair, projected_now):
        return (lstm_step(state_pair, projected_now, hidden_weight, gate_bias, forget_bias), None)

    blank_own = jnp.zeros((own_count, hidden_width), jnp.float32)
    (own_hidden, own_cell), _ = lax.scan(warm, (blank_own, blank_own), burn_projected, unroll=4)
    own_pair = jnp.stack([own_hidden, own_cell], axis=1)
    final_pair = lax.dynamic_update_slice_in_dim(
        jnp.zeros((seq_count, 2, hidden_width), jnp.float32), own_pair, position * own_count, 0
    )
    start_state = sum_at_owner(final_pair.astype(jnp.bfloat16), "tm", 2).astype(jnp.bfloat16)
    train_mask = (offsets - BURN) % STEPS < UNROLL
    sent_rows = jnp.where(train_mask[:, :, None], stored_rows, jnp.zeros((), jnp.bfloat16))
    raw_weight = jnp.exp(-IMPORTANCE * jnp.log(priorities.astype(jnp.float32))).astype(jnp.bfloat16)
    peak_weight = one_axis_at_a_time(jnp.max(raw_weight.astype(jnp.float32)), EP)
    outgoing = (raw_weight.astype(jnp.float32) / peak_weight).astype(jnp.bfloat16)
    moved_rows, moved_state, moved_weights = sent_together(
        (sent_rows, start_state, outgoing), EP, 0, 0, 1
    )
    moved_state = collect(moved_state, "tm", 2)
    return (moved_rows, moved_state, moved_weights)


def solution(mesh):
    torus = Mesh(mesh.devices.reshape(mesh.shape["tm"], 4, 4), ("tm", "ep_0", "ep_1"))
    return jax.shard_map(
        body,
        mesh=torus,
        in_specs=(P(EP, "tm", None), P(), P(), P(), P(), P(EP), P(EP), P(EP)),
        out_specs=(P(EP, "tm", None), P(EP, None, None), P(EP)),
        check_vma=False,
    )
```

profile of v0, /device:TPU:1, one launch (start us, length us, event | category | flops | bytes accessed | tf_op | source)
XLA Modules:
  0.0 274.5 jit_solution(11965095968492109559)
XLA Ops:
  2.2 2.8 %gather_fusion = bf16[128,16,1024]{2,1,0:T(8,128)(2,1)} fusion(bf16[64,16,1024]{2,1,0:T(8,128)(2,1)S(1)} %copy-done, s32[1024]{0:T(1024)S(1)} %pad_clamp_fusion), kind=kCustom, calls=%fused_computation | custom fusion | bytes 8389120 | tf_op jit(solution)/shard_map/gather | solution.py:97
  5.1 6.1 %all-to-all-start = ((bf16[128,16,1024]{2,1,0:T(8,128)(2,1)}), bf16[128,16,1024]{2,1,0:T(8,128)(2,1)}, u32[]{:S(2)}, u32[]{:S(2)}) async-start(bf16[128,16,1024]{2,1,0:T(8,128)(2,1)} %gather_fusion), calls=%async_computation | async-start | bytes 8388608 | tf_op jit(solution)/shard_map/all_to_all | solution.py:101
  11.8 10.0 %pmax.14 = f32[]{:T(128)} all-reduce(bf16[]{:T(256)} %convert_reduce_fusion), channel_id=1, replica_groups=mesh['tm'=8,'ep_0'=4,'ep_1'=4] {'ep_0'}, use_global_device_ids=true, to_apply=%region_4.5 | all-reduce | flops 1 | bytes 6 | tf_op jit(solution)/shard_map/pmax | solution.py:29
  22.1 37.9 %all-to-all-done = bf16[128,16,1024]{2,1,0:T(8,128)(2,1)} async-done(((bf16[128,16,1024]{2,1,0:T(8,128)(2,1)}), bf16[128,16,1024]{2,1,0:T(8,128)(2,1)}, u32[]{:S(2)}, u32[]{:S(2)}) %all-to-all-start) | async-done | bytes 4194336 | tf_op jit(solution)/shard_map/all_to_all | solution.py:101
  59.9 5.0 %copy.28 = bf16[8,16,16,1024]{3,2,0,1:T(8,128)(2,1)} copy(bf16[8,16,16,1024]{3,2,1,0:T(8,128)(2,1)} %bitcast) | data formatting | bytes 8388608 | tf_op jit(solution)/shard_map/all_to_all | solution.py:101
  64.9 15.3 %gather_fusion.1 = bf16[640,1024]{1,0:T(8,128)(2,1)} fusion(bf16[16,128,1024]{2,1,0:T(8,128)(2,1)} %bitcast.61, s32[640]{0:T(1024)S(1)} %reshape.199), kind=kCustom, calls=%fused_computation.1 | custom fusion | bytes 2626560 | tf_op jit(solution)/shard_map/gather | solution.py:105
  80.3 7.8 %fusion.75 = f32[10,4,16,2048]{3,2,1,0:T(8,128)} fusion(bf16[10,4,16,1024]{3,2,1,0:T(8,128)(2,1)} %bitcast.67, bf16[1024,2048]{1,0:T(8,128)(2,1)} %param.11), kind=kOutput, calls=%fused_computation.100 | convolution fusion | flops 2684354560 | bytes 10747904 | tf_op jit(solution)/shard_map/dot_general | solution.py:106
  88.1 81.5 %while.13 = (s32[]{:T(128)}, bf16[16,512]{1,0:T(8,128)(2,1)S(1)}, f32[16,512]{1,0:T(8,128)S(1)}, f32[10,4,16,2048]{3,2,1,0:T(8,128)}, bf16[512,2048]{1,0:T(8,128...) while((s32[]{:T(128)}, bf16[16,512]{1,0:T(8,128)(2,1)S(1)}, ...), condition=%wide.region_1.2_spmd.clone, body=%wide.region_0.1_spmd.clone.sunk | while | flops 134987776 | bytes 10395840 | solution.py:116
  96.3 2.0 fusion.116
  104.4 2.0 fusion.116
  112.6 2.0 fusion.116
  120.8 2.0 fusion.116
  128.9 2.0 fusion.116
  137.1 2.0 fusion.116
  145.2 2.0 fusion.116
  172.3 3.5 %all-to-all-start.1 = ((bf16[8,128,2,64]{1,3,2,0:T(8,128)(2,1)}), bf16[8,128,2,64]{1,3,2,0:T(8,128)(2,1)S(1)}, u32[]{:S(2)}, u32[]{:S(2)}) async-start(bf16[8,128,2,64]{1,3,2,0:T(8,128)(2,1)} %copy.30), calls=%async_computation.1 | async-start | bytes 524288 | tf_op jit(solution)/shard_map/all_to_all | solution.py:23
  175.8 3.8 %broadcast_select_fusion = bf16[128,16,1024]{2,1,0:T(8,128)(2,1)} fusion(bf16[128,16,1024]{2,1,0:T(8,128)(2,1)} %gather_fusion, pred[128,16]{1,0:T(8,128)(4,1)S(1)} %fusion.79), kind=kLoop, calls=%fused_computation.102 | loop fusion | flops 2097152 | bytes 8390656 | tf_op jit(solution)/shard_map/jit(_where)/select_n | solution.py:123
  179.6 10.4 %pmax.15 = f32[]{:T(128)} all-reduce(f32[]{:T(128)} %pmax.14), channel_id=1, replica_groups=mesh['tm'=8,'ep_0'=4,'ep_1'=4] {'ep_1'}, use_global_device_ids=true, to_apply=%region_5.6 | all-reduce | flops 1 | bytes 8 | tf_op jit(solution)/shard_map/pmax | solution.py:29
  190.0 7.4 %select_n.64 = bf16[16,8,16384]{2,1,0:T(8,128)(2,1)} reshape(bf16[128,16,1024]{2,1,0:T(8,128)(2,1)} %broadcast_select_fusion) | data formatting | bytes 8388608 | tf_op jit(solution)/shard_map/jit(_where)/select_n | solution.py:123
  198.6 2.4 pad_maximum_fusion
  201.0 53.7 %all_to_all.37 = bf16[16,8,16513]{2,1,0:T(8,128)(2,1)S(1)} all-to-all(bf16[16,8,16513]{2,1,0:T(8,128)(2,1)S(1)} %pad_maximum_fusion), channel_id=1, replica_groups=mesh['tm'=8,'ep_0'=4,'ep_1'=4] {'ep_0','ep_1'}, dimensions={0} | all-to-all | bytes 8454656 | tf_op jit(solution)/shard_map/all_to_all | solution.py:37
  257.5 7.5 %all-to-all-start.3 = ((bf16[8,128,2,64]{1,3,2,0:T(8,128)(2,1)}), bf16[8,128,2,64]{1,3,2,0:T(8,128)(2,1)S(1)}, u32[]{:S(2)}, u32[]{:S(2)}) async-start(bf16[8,128,2,64]{1,3,2,0:T(8,128)(2,1)} %broadcast_in_dim.32), calls=%async_computation.3 | async-start | bytes 524288 | tf_op jit(solution)/shard_map/all_to_all | solution.py:56
  265.0 2.5 slice.116
  267.5 4.8 %copy.39 = bf16[16,8,16,1024]{3,2,1,0:T(8,128)(2,1)} copy(bf16[16,8,16,1024]{3,1,2,0:T(8,128)(2,1)S(1)} %bitcast.65) | data formatting | bytes 8388608
  (113 shorter events, 78.7 us)
Async XLA Ops:
  0.6 1.6 copy-start
  5.1 6.1 %copy-start.5 = (s32[128]{0:T(128)S(1)}, s32[128]{0:T(128)}, u32[]{:S(2)}) copy-start(s32[128]{0:T(128)} %param.17) | copy-start | bytes 1540
  5.1 16.7 %copy-start.4 = (s32[128]{0:T(128)S(1)}, s32[128]{0:T(128)}, u32[]{:S(2)}) copy-start(s32[128]{0:T(128)} %param.16) | copy-start | bytes 1540
  5.1 54.9 %all-to-all-start = ((bf16[128,16,1024]{2,1,0:T(8,128)(2,1)}), bf16[128,16,1024]{2,1,0:T(8,128)(2,1)}, u32[]{:S(2)}, u32[]{:S(2)}) async-start(bf16[128,16,1024]{2,1,0:T(8,128)(2,1)} %gather_fusion), calls=%async_computation | async-start | bytes 8388608 | tf_op jit(solution)/shard_map/all_to_all | solution.py:101
  80.3 7.8 %copy-start.2 = (f32[2048]{0:T(1024)S(1)}, f32[2048]{0:T(1024)}, u32[]{:S(2)}) copy-start(f32[2048]{0:T(1024)} %param.13) | copy-start | bytes 24580
  80.3 7.8 %copy-start.3 = (f32[512]{0:T(512)S(1)}, f32[512]{0:T(512)}, u32[]{:S(2)}) copy-start(f32[512]{0:T(512)} %param.14) | copy-start | bytes 6148
  172.3 25.9 %all-to-all-start.1 = ((bf16[8,128,2,64]{1,3,2,0:T(8,128)(2,1)}), bf16[8,128,2,64]{1,3,2,0:T(8,128)(2,1)S(1)}, u32[]{:S(2)}, u32[]{:S(2)}) async-start(bf16[8,128,2,64]{1,3,2,0:T(8,128)(2,1)} %copy.30), calls=%async_computation.1 | async-start | bytes 524288 | tf_op jit(solution)/shard_map/all_to_all | solution.py:23
  254.6 2.0 copy-start.1
  257.5 16.1 %all-to-all-start.3 = ((bf16[8,128,2,64]{1,3,2,0:T(8,128)(2,1)}), bf16[8,128,2,64]{1,3,2,0:T(8,128)(2,1)S(1)}, u32[]{:S(2)}, u32[]{:S(2)}) async-start(bf16[8,128,2,64]{1,3,2,0:T(8,128)(2,1)} %broadcast_in_dim.32), calls=%async_computation.3 | async-start | bytes 524288 | tf_op jit(solution)/shard_map/all_to_all | solution.py:56
where the time goes:
time: 277 us; the launch traced here: 275 us
  matrix products  87.2 us (31%)
  blocking collectives  74 us (27%)
  local copies, waits for them, and re-layouts  46.9 us (17%)
  waiting for transfers between devices  37.9 us (14%)
  starting transfers between devices  17.1 us (6%)
  other arithmetic  10.3 us (4%)
    dot_general x40, matrix products, lstm_step(): jnp.dot(hidden.astype(jnp.bfloat16), hidden_weight, preferred_element_typ...  79.3 us
    all_to_all x1, blocking collectives, sent_together(): lax.all_to_all(both, axis, split_axis=split_dim, concat_axis=concat_dim,...  53.7 us
    all_to_all x1, waiting for transfers between devices, body(): lax.all_to_all(stored_rows, 'tm', split_axis=0, concat_axis=1, tiled=True)  37.9 us
    pmax x2, blocking collectives, one_axis_at_a_time(): x = lax.pmax(x, axis)  20.3 us
    gather x1, local copies, waits for them, and re-layouts, body(): burn_inputs = whole_slots[own_index, burn_steps]  15.3 us
    unnamed x14, local copies, waits for them, and re-layouts  8.41 us
    dot_general x1, matrix products, body(): jnp.dot(burn_inputs.reshape(BURN * own_count, burn_inputs.shape[2]), inpu...  7.84 us
    all_to_all x1, starting transfers between devices, sent_to_all(): return lax.all_to_all(copies, axis, split_axis=0, concat_axis=0, tiled=True)  7.54 us
  transfers between devices with their start and end apart: 3, of which 1 were waited for; matrix products, arithmetic and copies ran while one was open for 8% of the time, Pallas kernels for 0%

commit v1 on v0

v1 whole, which is shorter than its diff:
```python
import functools

import jax
import jax.numpy as jnp
from jax import lax
from jax.experimental import pallas as pl
from jax.experimental.pallas import tpu as pltpu
from jax.sharding import Mesh
from jax.sharding import PartitionSpec as P

STEPS = 128
BURN = 40
UNROLL = 80
SPAN = 4
EP = ("ep_0", "ep_1")
IMPORTANCE = 0.6


def sigmoid(x):
    return 0.5 * jnp.tanh(0.5 * x) + 0.5


def burn_in_kernel(
    starts, x_hbm, win_hbm, wh_hbm, off_ref, bias_ref, out_ref, xs, win, wh, hot, proj, xsem, wsem, hsem
):
    shards, count, rows, _ = x_hbm.shape
    hidden_width = wh.shape[0]
    win_copy = pltpu.make_async_copy(win_hbm, win, wsem)
    wh_copy = pltpu.make_async_copy(wh_hbm, wh, hsem)
    for s in range(count):
        first = starts[s] // rows
        for j in range(SPAN):
            pltpu.make_async_copy(
                x_hbm.at[(first + j) % shards, s],
                xs.at[pl.ds((s * SPAN + j) * rows, rows)],
                xsem,
            ).start()
    win_copy.start()
    wh_copy.start()
    span = SPAN * rows
    column = lax.broadcasted_iota(jnp.int32, (count, count * span), 1)
    sequence = lax.broadcasted_iota(jnp.int32, (count, count * span), 0)
    gap = column - sequence * span - off_ref[...]
    for t in range(BURN):
        hot[t * count : (t + 1) * count, :] = jnp.where(gap == t, 1.0, 0.0).astype(jnp.bfloat16)
    pltpu.make_async_copy(xs, xs, xsem).wait()
    x = jnp.dot(hot[...], xs[...], preferred_element_type=jnp.float32).astype(jnp.bfloat16)
    win_copy.wait()
    proj[...] = jnp.dot(x, win[...], preferred_element_type=jnp.float32) + bias_ref[...]
    wh_copy.wait()

    def step(t, state_pair):
        hidden, cell_state = state_pair
        projected = proj[pl.ds(pl.multiple_of(t * count, count), count), :]
        gate_sum = projected + jnp.dot(hidden, wh[...], preferred_element_type=jnp.float32)
        ingate = sigmoid(gate_sum[:, :hidden_width])
        forget = sigmoid(gate_sum[:, hidden_width : 2 * hidden_width])
        candidate = jnp.tanh(gate_sum[:, 2 * hidden_width : 3 * hidden_width])
        outgate = sigmoid(gate_sum[:, 3 * hidden_width :])
        cell_state = forget * cell_state + ingate * candidate
        return ((outgate * jnp.tanh(cell_state)).astype(jnp.bfloat16), cell_state)

    blank = (
        jnp.zeros((count, hidden_width), jnp.bfloat16),
        jnp.zeros((count, hidden_width), jnp.float32),
    )
    hidden, cell_state = lax.fori_loop(0, BURN, step, blank, unroll=4)
    out_ref[0] = hidden
    out_ref[1] = cell_state.astype(jnp.bfloat16)


def burn_in(starts, x, input_weight, hidden_weight, bias):
    _, count, rows, width = x.shape
    hidden_width = hidden_weight.shape[0]
    hbm = pl.BlockSpec(memory_space=pltpu.HBM)
    vmem = pl.BlockSpec(memory_space=pltpu.VMEM)
    return pl.pallas_call(
        burn_in_kernel,
        out_shape=jax.ShapeDtypeStruct((2, count, hidden_width), jnp.bfloat16),
        in_specs=[pl.BlockSpec(memory_space=pltpu.SMEM), hbm, hbm, hbm, vmem, vmem],
        out_specs=vmem,
        scratch_shapes=[
            pltpu.VMEM((count * SPAN * rows, width), jnp.bfloat16),
            pltpu.VMEM(input_weight.shape, jnp.bfloat16),
            pltpu.VMEM(hidden_weight.shape, jnp.bfloat16),
            pltpu.VMEM((BURN * count, count * SPAN * rows), jnp.bfloat16),
            pltpu.VMEM((BURN * count, 4 * hidden_width), jnp.float32),
            pltpu.SemaphoreType.DMA,
            pltpu.SemaphoreType.DMA,
            pltpu.SemaphoreType.DMA,
        ],
        compiler_params=pltpu.CompilerParams(vmem_limit_bytes=32 * 1024 * 1024),
        cost_estimate=pl.CostEstimate(
            flops=30_000_000_000, bytes_accessed=8 * 1024 * 1024, transcendentals=0
        ),
        name="burn_in",
    )(starts, x, input_weight, hidden_weight, (starts % rows)[:, None], bias)


def body(
    observations,
    input_weight,
    hidden_weight,
    gate_bias,
    forget_bias,
    episode_ids,
    start_steps,
    priorities,
):
    shard_steps, width = observations.shape[1:]
    seq_count = episode_ids.shape[0]
    hidden_width = hidden_weight.shape[0]
    time_shards = lax.axis_size("tm")
    learners = lax.axis_size(EP)
    position = lax.axis_index("tm")
    own_count = seq_count // time_shards
    per_learner = seq_count // learners
    stored_rows = observations[episode_ids]
    slots = lax.all_to_all(stored_rows, "tm", split_axis=0, concat_axis=0, tiled=True)
    slots = slots.reshape(time_shards, own_count, shard_steps, width)

    local_steps = position * shard_steps + jnp.arange(shard_steps, dtype=jnp.int32)
    offsets = (local_steps[None, :] - start_steps[:, None] - BURN) % STEPS
    sent_rows = jnp.where((offsets < UNROLL)[:, :, None], stored_rows, jnp.zeros((), jnp.bfloat16))
    moved_rows = lax.all_to_all(sent_rows, EP, split_axis=0, concat_axis=0, tiled=True)

    own_starts = lax.dynamic_slice_in_dim(start_steps, position * own_count, own_count)
    blank = jnp.zeros((hidden_width,), jnp.float32)
    bias = gate_bias + jnp.concatenate([blank, forget_bias, blank, blank])
    own_pair = burn_in(own_starts, slots, input_weight, hidden_weight, bias[None, :])
    own_pair = jnp.swapaxes(own_pair, 0, 1)

    pairs = lax.all_gather(own_pair, "tm", axis=0, tiled=True)
    pairs = pairs.reshape(learners, per_learner, 2, hidden_width)
    raw_weight = jnp.exp(-IMPORTANCE * jnp.log(priorities.astype(jnp.float32))).astype(jnp.bfloat16)
    peak = jnp.broadcast_to(jnp.max(raw_weight), (learners, 1))
    extra = jnp.concatenate([raw_weight.reshape(learners, per_learner), peak], axis=1)
    extra = jnp.pad(extra, ((0, 0), (0, 2 * hidden_width - per_learner - 1)))
    both = jnp.concatenate([pairs, extra.reshape(learners, 1, 2, hidden_width)], axis=1)
    both = lax.all_to_all(both, EP, split_axis=0, concat_axis=0, tiled=True)
    start_state = both[:, :per_learner].reshape(seq_count, 2, hidden_width)
    extra = both[:, per_learner, 0, : per_learner + 1].astype(jnp.float32)
    weights = (extra[:, :per_learner] / jnp.max(extra[:, per_learner])).astype(jnp.bfloat16)
    return (moved_rows, start_state, weights.reshape(seq_count))


def solution(mesh):
    torus = Mesh(mesh.devices.reshape(mesh.shape["tm"], 4, 4), ("tm", "ep_0", "ep_1"))
    return jax.shard_map(
        body,
        mesh=torus,
        in_specs=(P(EP, "tm", None), P(), P(), P(), P(), P(EP), P(EP), P(EP)),
        out_specs=(P(EP, "tm", None), P(EP, None, None), P(EP)),
        check_vma=False,
    )
```

time: 277 us -> 155 us (0.56)
  matrix products: 87.2 us -> 0 us
  blocking collectives: 74 us -> 32.5 us
  local copies, waits for them, and re-layouts: 46.9 us -> 14.5 us
  waiting for transfers between devices: 37.9 us -> 61.3 us
  Pallas kernels: 0 us -> 21.5 us
  starting transfers between devices: 17.1 us -> 13.7 us
    dot_general x41 -> x0, matrix products: 87.2 us -> none  [the longest x40 79.3 us: lstm_step(): jnp.dot(hidden.astype(jnp.bfloat16), hidden_weight, preferred_element_typ...]
    all_to_all x1, blocking collectives: 53.7 us -> 18.6 us  [body(): both = lax.all_to_all(both, EP, split_axis=0, concat_axis=0, tiled=True)]
    all_to_all x3 -> x2, waiting for transfers between devices: 37.9 us -> 61.3 us  [the longest x1 44.8 us: body(): lax.all_to_all(stored_rows, 'tm', split_axis=0, concat_axis=0, tiled=True)]
    pallas_call x0 -> x1, Pallas kernels: none -> 21.5 us  [burn_in(): pl.pallas_call(burn_in_kernel, out_shape=jax.ShapeDtypeStruct((2, count,...]
    pmax x2 -> x0, blocking collectives: 20.3 us -> none  [one_axis_at_a_time(): x = lax.pmax(x, axis)]
    gather x1 -> x0, local copies, waits for them, and re-layouts: 15.3 us -> none  [body(): burn_inputs = whole_slots[own_index, burn_steps]]
    all_gather x0 -> x1, blocking collectives: none -> 13.9 us  [body(): pairs = lax.all_gather(own_pair, 'tm', axis=0, tiled=True)]
    select_n x1 -> x0, local copies, waits for them, and re-layouts: 7.41 us -> none  [body(): jnp.where(train_mask[:, :, None], stored_rows, jnp.zeros((), jnp.bfloat16))]
  transfers between devices with their start and end apart: 3 -> 2, of which waited for: 1 -> 2; matrix products, arithmetic and copies ran while one was open for 8% -> 4% of each run, Pallas kernels for 0% -> 14%
where the time goes in v1:
time: 155 us; the launch traced here: 152 us
  waiting for transfers between devices  61.3 us (40%)
  blocking collectives  32.5 us (21%)
  Pallas kernels  21.5 us (14%)
  local copies, waits for them, and re-layouts  14.5 us (9%)
  starting transfers between devices  13.7 us (9%)
  other arithmetic  7.82 us (5%)
    all_to_all x1, waiting for transfers between devices, body(): lax.all_to_all(stored_rows, 'tm', split_axis=0, concat_axis=0, tiled=True)  44.8 us
    pallas_call x1, Pallas kernels, burn_in(): pl.pallas_call(burn_in_kernel, out_shape=jax.ShapeDtypeStruct((2, count,...  21.5 us
    all_to_all x1, blocking collectives, body(): both = lax.all_to_all(both, EP, split_axis=0, concat_axis=0, tiled=True)  18.6 us
    all_to_all x1, waiting for transfers between devices, body(): lax.all_to_all(sent_rows, EP, split_axis=0, concat_axis=0, tiled=True)  16.4 us
    all_gather x1, blocking collectives, body(): pairs = lax.all_gather(own_pair, 'tm', axis=0, tiled=True)  13.9 us
    unnamed x15, local copies, waits for them, and re-layouts  9.62 us
    all_to_all x1, starting transfers between devices, body(): lax.all_to_all(sent_rows, EP, split_axis=0, concat_axis=0, tiled=True)  7.65 us
    all_to_all x1, starting transfers between devices, body(): lax.all_to_all(stored_rows, 'tm', split_axis=0, concat_axis=0, tiled=True)  6.09 us
  transfers between devices with their start and end apart: 2, of which 2 were waited for; matrix products, arithmetic and copies ran while one was open for 4% of the time, Pallas kernels for 14%

profile of v1, /device:TPU:1, one launch (start us, length us, event | category | flops | bytes accessed | tf_op | source)
XLA Modules:
  0.0 152.1 jit_solution(11554906951487724846)
XLA Ops:
  0.6 0.8 compare_select_fusion
  1.5 0.8 copy-done
  2.2 2.8 %gather_fusion = bf16[128,16,1024]{2,1,0:T(8,128)(2,1)} fusion(bf16[64,16,1024]{2,1,0:T(8,128)(2,1)S(1)} %copy-done, s32[1024]{0:T(1024)S(1)} %pad_clamp_fusion), kind=kCustom, calls=%fused_computation | custom fusion | bytes 8389120 | tf_op jit(solution)/shard_map/gather | solution.py:118
  5.1 6.1 %all-to-all-start.1 = ((bf16[128,16,1024]{2,1,0:T(8,128)(2,1)}), bf16[128,16,1024]{2,1,0:T(8,128)(2,1)}, u32[]{:S(2)}, u32[]{:S(2)}) async-start(bf16[128,16,1024]{2,1,0:T(8,128)(2,1)} %gather_fusion), calls=%async_computation.1 | async-start | bytes 8388608 | tf_op jit(solution)/shard_map/all_to_all | solution.py:119
  11.2 0.1 fusion.1
  11.3 3.8 %broadcast_select_fusion = bf16[128,16,1024]{2,1,0:T(8,128)(2,1)} fusion(bf16[128,16,1024]{2,1,0:T(8,128)(2,1)} %gather_fusion, pred[128,16]{1,0:T(8,128)(4,1)S(1)} %fusion.1), kind=kLoop, calls=%fused_computation.1 | loop fusion | flops 2097152 | bytes 8390656 | tf_op jit(solution)/shard_map/jit(_where)/select_n | solution.py:124
  15.1 44.8 %all-to-all-done.1 = bf16[128,16,1024]{2,1,0:T(8,128)(2,1)} async-done(((bf16[128,16,1024]{2,1,0:T(8,128)(2,1)}), bf16[128,16,1024]{2,1,0:T(8,128)(2,1)}, u32[]{:S(2)}, u32[]{:S(2)}) %all-to-all-start.1) | async-done | bytes 4194336 | tf_op jit(solution)/shard_map/all_to_all | solution.py:119
  59.9 7.6 %all-to-all-start = ((bf16[128,16,1024]{2,1,0:T(8,128)(2,1)}), bf16[128,16,1024]{2,1,0:T(8,128)(2,1)}, u32[]{:S(2)}, u32[]{:S(2)}) async-start(bf16[128,16,1024]{2,1,0:T(8,128)(2,1)} %broadcast_select_fusion), calls=%async_computation | async-start | bytes 8388608 | tf_op jit(solution)/shard_map/all_to_all | solution.py:125
  67.6 0.1 reshape.73
  67.9 0.6 fusion.6
  68.5 0.6 fusion.2
  69.3 2.2 %copy-done.1 = bf16[1024,2048]{1,0:T(8,128)(2,1)S(1)} copy-done((bf16[1024,2048]{1,0:T(8,128)(2,1)S(1)}, bf16[1024,2048]{1,0:T(8,128)(2,1)}, u32[]{:S(2)}) %copy-start.1) | copy-done | bytes 4194328
  71.5 1.6 %copy-done.2 = bf16[512,2048]{1,0:T(8,128)(2,1)S(1)} copy-done((bf16[512,2048]{1,0:T(8,128)(2,1)S(1)}, bf16[512,2048]{1,0:T(8,128)(2,1)}, u32[]{:S(2)}) %copy-start.2) | copy-done | bytes 2097176
  73.0 21.5 %burn_in.1 = bf16[2,16,512]{2,1,0:T(8,128)(2,1)S(1)} custom-call(s32[16]{0:T(128)S(1)} %get-tuple-element.4.starts, bf16[8,16,16,1024]{3,2,1,0:T(8,128)(2,1)} %bitcast.x_hbm, bf16[1024,2048]{1,0:T(8,128)(2,1)S(1)} %copy-done.1, bf16[512,2048]{1,0:T(8,128)(2,1)S(1)} %copy-done.2, s32[16,1]{1,0:T(8,128)S(1)} %copy.19.off_ref, f32[1,2048]{1,0:T(1,128)S(1)} %bitcast.10), custom_call_target="tpu_custom_call" | custom-call | flops 30000001024 | bytes 8388608 | tf_op jit(solution)/shard_map/burn_in/pallas_call | solution.py:77
  94.6 13.9 %all_gather.3 = bf16[128,2,512]{2,0,1:T(8,128)(2,1)S(1)} all-gather(bf16[16,2,512]{2,0,1:T(8,128)(2,1)S(1)} %bitcast.9), channel_id=1, replica_groups=mesh['tm'=8,'ep_0'=4,'ep_1'=4] {'tm'}, dimensions={0}, use_global_device_ids=true | all-gather | bytes 294912 | tf_op jit(solution)/shard_map/all_gather | solution.py:133
  108.5 0.3 copy.20
  108.8 0.4 pad_maximum_fusion
  109.2 16.4 %all-to-all-done = bf16[128,16,1024]{2,1,0:T(8,128)(2,1)} async-done(((bf16[128,16,1024]{2,1,0:T(8,128)(2,1)}), bf16[128,16,1024]{2,1,0:T(8,128)(2,1)}, u32[]{:S(2)}, u32[]{:S(2)}) %all-to-all-start) | async-done | bytes 4194336 | tf_op jit(solution)/shard_map/all_to_all | solution.py:125
  125.6 18.6 %all_to_all.15 = bf16[16,9,2,512]{3,2,1,0:T(2,128)(2,1)S(1)} all-to-all(bf16[16,9,2,512]{3,2,1,0:T(2,128)(2,1)S(1)} %pad_maximum_fusion), channel_id=1, replica_groups=mesh['tm'=8,'ep_0'=4,'ep_1'=4] {'ep_0','ep_1'}, dimensions={0} | all-to-all | bytes 589824 | tf_op jit(solution)/shard_map/all_to_all | solution.py:140
  144.2 0.7 slice_reduce_fusion
  144.9 0.6 fusion.3
  145.5 0.6 reshape.76
  146.1 1.0 slice.18
  147.1 5.0 %copy.23 = bf16[128,16,1024]{2,1,0:T(8,128)(2,1)} copy(bf16[128,16,1024]{2,1,0:T(8,128)(2,1)} %all-to-all-done) | data formatting | bytes 8388608
  (21 shorter events, 0.3 us)
Async XLA Ops:
  0.6 1.6 %copy-start = (bf16[64,16,1024]{2,1,0:T(8,128)(2,1)S(1)}, bf16[64,16,1024]{2,1,0:T(8,128)(2,1)}, u32[]{:S(2)}) copy-start(bf16[64,16,1024]{2,1,0:T(8,128)(2,1)} %param.8) | copy-start | bytes 6291460
  5.1 6.1 %copy-start.5 = (s32[128]{0:T(128)S(1)}, s32[128]{0:T(128)}, u32[]{:S(2)}) copy-start(s32[128]{0:T(128)} %param.14) | copy-start | bytes 1540
  5.1 54.9 %all-to-all-start.1 = ((bf16[128,16,1024]{2,1,0:T(8,128)(2,1)}), bf16[128,16,1024]{2,1,0:T(8,128)(2,1)}, u32[]{:S(2)}, u32[]{:S(2)}) async-start(bf16[128,16,1024]{2,1,0:T(8,128)(2,1)} %gather_fusion), calls=%async_computation.1 | async-start | bytes 8388608 | tf_op jit(solution)/shard_map/all_to_all | solution.py:119
  15.1 52.5 %copy-start.6 = (s32[128]{0:T(128)S(1)}, s32[128]{0:T(128)}, u32[]{:S(2)}) copy-start(s32[128]{0:T(128)} %param.15) | copy-start | bytes 1540
  15.1 54.1 %copy-start.3 = (f32[2048]{0:T(1024)S(1)}, f32[2048]{0:T(1024)}, u32[]{:S(2)}) copy-start(f32[2048]{0:T(1024)} %param.11) | copy-start | bytes 24580
  15.1 54.1 %copy-start.4 = (f32[512]{0:T(512)S(1)}, f32[512]{0:T(512)}, u32[]{:S(2)}) copy-start(f32[512]{0:T(512)} %param.12) | copy-start | bytes 6148
  59.9 65.6 %all-to-all-start = ((bf16[128,16,1024]{2,1,0:T(8,128)(2,1)}), bf16[128,16,1024]{2,1,0:T(8,128)(2,1)}, u32[]{:S(2)}, u32[]{:S(2)}) async-start(bf16[128,16,1024]{2,1,0:T(8,128)(2,1)} %broadcast_select_fusion), calls=%async_computation | async-start | bytes 8388608 | tf_op jit(solution)/shard_map/all_to_all | solution.py:125
  69.3 2.2 %copy-start.1 = (bf16[1024,2048]{1,0:T(8,128)(2,1)S(1)}, bf16[1024,2048]{1,0:T(8,128)(2,1)}, u32[]{:S(2)}) copy-start(bf16[1024,2048]{1,0:T(8,128)(2,1)} %win_hbm.1) | copy-start | bytes 12582916
  71.4 1.6 %copy-start.2 = (bf16[512,2048]{1,0:T(8,128)(2,1)S(1)}, bf16[512,2048]{1,0:T(8,128)(2,1)}, u32[]{:S(2)}) copy-start(bf16[512,2048]{1,0:T(8,128)(2,1)} %wh_hbm.1) | copy-start | bytes 6291460

commit v2 on v1

v2 whole, which is shorter than its diff:
```python
import functools

import jax
import jax.numpy as jnp
from jax import lax
from jax.experimental import pallas as pl
from jax.experimental.pallas import tpu as pltpu
from jax.sharding import Mesh
from jax.sharding import PartitionSpec as P

STEPS = 128
BURN = 40
UNROLL = 80
ROOM = 128
EP = ("ep_0", "ep_1")
IMPORTANCE = 0.6
MIB = 1024 * 1024
SMEM = pl.BlockSpec(memory_space=pltpu.SMEM)
VMEM = pl.BlockSpec(memory_space=pltpu.VMEM)
HBM = pl.BlockSpec(memory_space=pltpu.HBM)


def sigmoid(x):
    return 0.5 * jnp.tanh(0.5 * x) + 0.5


def iota(shape, dim):
    return lax.broadcasted_iota(jnp.int32, shape, dim)


def one_hot(hit):
    return jnp.where(hit, 1.0, 0.0).astype(jnp.bfloat16)


def f32_dot(a, b):
    return jnp.dot(a, b, preferred_element_type=jnp.float32)


def pack_kernel(base, place, ids, starts_ref, obs, *rest):
    outs, rows_of = rest[:-1], rest[-1]
    shards, count = starts_ref.shape
    shard_steps = obs.shape[1]
    lanes = count * shard_steps
    spread = one_hot(iota((count, lanes), 1) // shard_steps == iota((count, lanes), 0))
    starts = f32_dot(starts_ref[...].astype(jnp.bfloat16), spread).astype(jnp.int32)
    step = place[0] * shard_steps + iota((shards, lanes), 1) % shard_steps
    within = ((step - starts) & (STEPS - 1)) < BURN
    before = one_hot(iota((lanes, lanes), 0) < iota((lanes, lanes), 1))
    slot = f32_dot(one_hot(within), before).astype(jnp.int32) - base
    slot = jnp.where(within, slot, -1)
    for k in range(shards):
        for i in range(count):
            rows_of[k, i * shard_steps : (i + 1) * shard_steps, :] = obs[ids[k, i]]
    for k in range(shards):
        hot = one_hot(iota((ROOM, lanes), 0) == slot[k : k + 1, :])
        outs[k][...] = f32_dot(hot, rows_of[k]).astype(jnp.bfloat16)


def pack(base, position, ids, starts, observations):
    shards, count = ids.shape
    _, shard_steps, width = observations.shape
    return pl.pallas_call(
        functools.partial(pack_kernel, base),
        out_shape=[jax.ShapeDtypeStruct((ROOM, width), jnp.bfloat16)] * shards,
        in_specs=[SMEM, SMEM, VMEM, VMEM],
        out_specs=[VMEM] * shards,
        scratch_shapes=[pltpu.VMEM((shards, count * shard_steps, width), jnp.bfloat16)],
        compiler_params=pltpu.CompilerParams(vmem_limit_bytes=24 * MIB),
        cost_estimate=pl.CostEstimate(flops=10**9, bytes_accessed=4 * MIB, transcendentals=0),
        name="pack_rows",
    )(position.reshape(1), ids, starts, observations)


def masked_kernel(place, ids_hbm, starts_hbm, obs, out, ids, starts, sem):
    block = pl.program_id(0)

    @pl.when(block == 0)
    def _():
        ids_copy = pltpu.make_async_copy(ids_hbm, ids, sem.at[0])
        starts_copy = pltpu.make_async_copy(starts_hbm, starts, sem.at[1])
        ids_copy.start()
        starts_copy.start()
        ids_copy.wait()
        starts_copy.wait()

    count, shard_steps, width = out.shape
    step = place[0] * shard_steps + iota((shard_steps, width), 0)
    for i in range(count):
        g = block * count + i
        keep = ((step - starts[g] - BURN) & (STEPS - 1)) < UNROLL
        out[i] = jnp.where(keep, obs[ids[g]], jnp.zeros((), jnp.bfloat16))


def masked(position, ids, starts, observations):
    _, shard_steps, width = observations.shape
    count = 8
    return pl.pallas_call(
        masked_kernel,
        grid=(ids.shape[0] // count,),
        out_shape=jax.ShapeDtypeStruct((ids.shape[0], shard_steps, width), jnp.bfloat16),
        in_specs=[SMEM, HBM, HBM, VMEM],
        out_specs=pl.BlockSpec((count, shard_steps, width), lambda b: (b, 0, 0)),
        scratch_shapes=[
            pltpu.SMEM(ids.shape, jnp.int32),
            pltpu.SMEM(starts.shape, jnp.int32),
            pltpu.SemaphoreType.DMA((2,)),
        ],
        compiler_params=pltpu.CompilerParams(vmem_limit_bytes=60 * MIB),
        cost_estimate=pl.CostEstimate(flops=10**8, bytes_accessed=6 * MIB, transcendentals=0),
        name="masked_rows",
    )(position.reshape(1), ids, starts, observations)


def copy_kernel(rows, out):
    out[...] = rows[...]


def copied(rows):
    _, shard_steps, width = rows.shape
    block = pl.BlockSpec((16, shard_steps, width), lambda b: (b, 0, 0))
    return pl.pallas_call(
        copy_kernel,
        grid=(rows.shape[0] // 16,),
        out_shape=jax.ShapeDtypeStruct(rows.shape, rows.dtype),
        in_specs=[block],
        out_specs=block,
        compiler_params=pltpu.CompilerParams(vmem_limit_bytes=48 * MIB),
        cost_estimate=pl.CostEstimate(flops=10**9, bytes_accessed=8 * MIB, transcendentals=0),
        name="copy_rows",
    )(rows)


def burn_in_kernel(rounds, *refs):
    parts, refs = refs[: 8 * rounds], refs[8 * rounds :]
    columns, (win_hbm, wh_hbm, bias_ref, out_ref), refs = refs[:rounds], refs[rounds : rounds + 4], refs[rounds + 4 :]
    xs, hots, (win, wh, proj, xsem, wsem, hsem) = refs[:rounds], refs[rounds : 2 * rounds], refs[2 * rounds :]
    copies, _, count, hidden_width = out_ref.shape
    win_copy = pltpu.make_async_copy(win_hbm, win, wsem)
    wh_copy = pltpu.make_async_copy(wh_hbm, wh, hsem)
    row_copies = [
        pltpu.make_async_copy(part, xs[n // 8].at[pl.ds((n % 8) * ROOM, ROOM)], xsem.at[n])
        for n, part in enumerate(parts)
    ]
    for copy in row_copies:
        copy.start()
    win_copy.start()
    wh_copy.start()
    lane = iota((count, 8 * ROOM), 1)
    for hot, column in zip(hots, columns):
        for t in range(BURN):
            at = slice(t * count, (t + 1) * count)
            hot[at, :] = one_hot(lane == column[at, :])
    for copy in row_copies:
        copy.wait()
    x = sum(f32_dot(hot[...], rows[...]) for hot, rows in zip(hots, xs)).astype(jnp.bfloat16)
    win_copy.wait()
    proj[...] = f32_dot(x, win[...]) + bias_ref[...]
    wh_copy.wait()

    half = hidden_width // 2

    def step(t, state_pair):
        hiddens, cells = state_pair
        row = pl.ds(pl.multiple_of(t * count, count), count)
        blocks = [[pl.ds(gate * hidden_width + q * half, half) for gate in range(4)] for q in range(2)]
        sums = [[proj[row, block] for block in part] for part in blocks]
        for k in range(2):
            for q in range(2):
                for gate in range(4):
                    weight = wh[k * half : (k + 1) * half, blocks[q][gate]]
                    sums[q][gate] = sums[q][gate] + f32_dot(hiddens[k], weight)
        new_hiddens, new_cells = [], []
        for (ingate, forget, candidate, outgate), cell_state in zip(sums, cells):
            cell_state = sigmoid(forget) * cell_state + sigmoid(ingate) * jnp.tanh(candidate)
            new_cells.append(cell_state)
            new_hiddens.append((sigmoid(outgate) * jnp.tanh(cell_state)).astype(jnp.bfloat16))
        return (tuple(new_hiddens), tuple(new_cells))

    blank = ((jnp.zeros((count, half), jnp.bfloat16),) * 2, (jnp.zeros((count, half), jnp.float32),) * 2)
    hiddens, cells = lax.fori_loop(0, BURN, step, blank, unroll=8)
    hidden = jnp.concatenate(hiddens, axis=1)
    cell_state = jnp.concatenate(cells, axis=1)
    for n in range(copies):
        out_ref[n, 0] = hidden
        out_ref[n, 1] = cell_state.astype(jnp.bfloat16)


def burn_in(parts, columns, input_weight, hidden_weight, bias):
    rounds = len(columns)
    shards = len(parts) // rounds
    width = input_weight.shape[0]
    hidden_width = hidden_weight.shape[0]
    total = columns[0].shape[0]
    count = total // BURN
    return pl.pallas_call(
        functools.partial(burn_in_kernel, rounds),
        out_shape=jax.ShapeDtypeStruct((shards, 2, count, hidden_width), jnp.bfloat16),
        in_specs=[HBM] * len(parts) + [VMEM] * rounds + [HBM, HBM, VMEM],
        out_specs=VMEM,
        scratch_shapes=[pltpu.VMEM((shards * ROOM, width), jnp.bfloat16)] * rounds
        + [pltpu.VMEM((total, shards * ROOM), jnp.bfloat16)] * rounds
        + [
            pltpu.VMEM(input_weight.shape, jnp.bfloat16),
            pltpu.VMEM(hidden_weight.shape, jnp.bfloat16),
            pltpu.VMEM((total, 4 * hidden_width), jnp.float32),
            pltpu.SemaphoreType.DMA((len(parts),)),
            pltpu.SemaphoreType.DMA,
            pltpu.SemaphoreType.DMA,
        ],
        compiler_params=pltpu.CompilerParams(vmem_limit_bytes=32 * MIB),
        cost_estimate=pl.CostEstimate(
            flops=30_000_000_000, bytes_accessed=8 * MIB, transcendentals=0
        ),
        name="burn_in",
    )(*parts, *columns, input_weight, hidden_weight, bias)


def order_kernel(pairs, rank, raw, out):
    shards, _, count, hidden_width = pairs.shape
    total = shards * count
    column = iota((total, total), 1)
    hot = one_hot((column % count) * shards + column // count == rank[...])
    for n in range(2):
        state = pairs[:, n].reshape(total, hidden_width)
        out[:, n * hidden_width : (n + 1) * hidden_width] = f32_dot(hot, state).astype(jnp.bfloat16)
    lane = iota((total, 128), 1)
    tail = jnp.where(lane == 0, raw[...], jnp.where(lane == 1, jnp.max(raw[...]), 0.0))
    out[:, 2 * hidden_width :] = tail.astype(jnp.bfloat16)


def ordered(pairs, rank, raw):
    total = rank.shape[0]
    return pl.pallas_call(
        order_kernel,
        out_shape=jax.ShapeDtypeStruct((total, 2 * pairs.shape[3] + 128), jnp.bfloat16),
        in_specs=[VMEM] * 3,
        out_specs=VMEM,
        compiler_params=pltpu.CompilerParams(vmem_limit_bytes=8 * MIB),
        cost_estimate=pl.CostEstimate(flops=10**8, bytes_accessed=MIB, transcendentals=0),
        name="learner_order",
    )(pairs, rank[:, None], raw[:, None])


def rows_in_shard(starts, shard, shard_steps):
    part = (shard - starts // shard_steps) % (STEPS // shard_steps)
    first = part * shard_steps - starts % shard_steps
    return jnp.clip(jnp.minimum(BURN, first + shard_steps) - jnp.maximum(first, 0), 0, shard_steps)


def body(
    observations,
    input_weight,
    hidden_weight,
    gate_bias,
    forget_bias,
    episode_ids,
    start_steps,
    priorities,
):
    shard_steps, _ = observations.shape[1:]
    seq_count = episode_ids.shape[0]
    hidden_width = hidden_weight.shape[0]
    shards = lax.axis_size("tm")
    learners = lax.axis_size(EP)
    position = lax.axis_index("tm").astype(jnp.int32)
    own_count = seq_count // shards
    per_learner = seq_count // learners

    index = jnp.arange(seq_count, dtype=jnp.int32)
    key = start_steps * seq_count + index
    rank = jnp.sum((key[None, :] < key[:, None]).astype(jnp.int32), axis=1)
    turn = jnp.arange(shards, dtype=jnp.int32)
    dealt = jnp.arange(own_count, dtype=jnp.int32)[None, :] * shards + ((position + turn) % shards)[:, None]
    chosen = rank[None, None, :] == dealt[:, :, None]
    ids = jnp.sum(jnp.where(chosen, episode_ids, 0), axis=2)
    starts = jnp.sum(jnp.where(chosen, start_steps, 0), axis=2)

    def exchanged(base):
        sent = pack(base, position, ids, starts, observations)
        parts = [sent[0]]
        for k in range(1, shards):
            ring = [(i, (i + k) % shards) for i in range(shards)]
            parts.append(lax.ppermute(sent[k], "tm", ring))
        return parts

    parts = exchanged(0)
    sent_rows = masked(position, episode_ids, start_steps, observations)
    moved_rows = lax.all_to_all(sent_rows, EP, split_axis=0, concat_axis=0, tiled=True)

    own = starts[0]
    step = jnp.arange(BURN, dtype=jnp.int32)[:, None]
    shard = (own + step) % STEPS // shard_steps
    earlier = jnp.arange(own_count)[None, None, :] < jnp.arange(own_count)[None, :, None]
    ahead = jnp.sum(
        jnp.where(earlier, rows_in_shard(own[None, None, :], shard[:, :, None], shard_steps), 0), axis=2
    )
    first = jnp.maximum((own % shard_steps + step) // shard_steps * shard_steps - own % shard_steps, 0)
    slot = ahead + step - first
    sender = (position - shard) % shards
    column = (sender * ROOM + slot % ROOM).reshape(BURN * own_count, 1)
    late = (slot >= ROOM).reshape(BURN * own_count, 1)
    pair_rows = jnp.sum(rows_in_shard(starts[None], turn[:, None, None], shard_steps), axis=2)
    crowded = jnp.max(pair_rows) > ROOM

    blank = jnp.zeros((hidden_width,), jnp.float32)
    bias = (gate_bias + jnp.concatenate([blank, forget_bias, blank, blank]))[None, :]

    def usual():
        return burn_in(parts, [column], input_weight, hidden_weight, bias)

    def two_rounds():
        columns = [jnp.where(late, -1, column), jnp.where(late, column, -1)]
        more = exchanged(ROOM)
        return burn_in(parts + more, columns, input_weight, hidden_weight, bias)

    pairs = lax.cond(crowded, two_rounds, usual)
    pairs, moved_rows = lax.optimization_barrier((pairs, moved_rows))
    pairs = lax.all_to_all(pairs, "tm", split_axis=0, concat_axis=0, tiled=True)
    moved_rows = copied(moved_rows)
    raw_weight = jnp.exp(-IMPORTANCE * jnp.log(priorities.astype(jnp.float32))).astype(jnp.bfloat16)
    both = ordered(pairs, rank, raw_weight.astype(jnp.float32))
    both = both.reshape(learners, per_learner, both.shape[1])
    both = lax.all_to_all(both, EP, split_axis=0, concat_axis=0, tiled=True)
    start_state = both[:, :, : 2 * hidden_width].reshape(seq_count, 2, hidden_width)
    raw = both[:, :, 2 * hidden_width].astype(jnp.float32)
    peak = jnp.max(both[:, :, 2 * hidden_width + 1]).astype(jnp.float32)
    weights = (raw / peak).astype(jnp.bfloat16)
    return (moved_rows, start_state, weights.reshape(seq_count))


def solution(mesh):
    torus = Mesh(mesh.devices.reshape(mesh.shape["tm"], 4, 4), ("tm", "ep_0", "ep_1"))
    return jax.shard_map(
        body,
        mesh=torus,
        in_specs=(P(EP, "tm", None), P(), P(), P(), P(), P(EP), P(EP), P(EP)),
        out_specs=(P(EP, "tm", None), P(EP, None, None), P(EP)),
        check_vma=False,
    )
```

time: 155 us -> 116 us (0.75)
  blocking collectives: 32.5 us -> 0 us
  waiting for transfers between devices: 61.3 us -> 31.9 us
  starting transfers between devices: 13.7 us -> 34.8 us
  Pallas kernels: 21.5 us -> 39.7 us
  local copies, waits for them, and re-layouts: 14.5 us -> 2.44 us
  other arithmetic: 7.82 us -> 2.71 us
    all_to_all x1 -> x2, waiting for transfers between devices: 44.8 us -> 7.33 us  [the longest x1 6.23 us: body(): pairs = lax.all_to_all(pairs, 'tm', split_axis=0, concat_axis=0, tiled=True)]
    all_to_all x1 -> x0, blocking collectives: 18.6 us -> none  [body(): both = lax.all_to_all(both, EP, split_axis=0, concat_axis=0, tiled=True)]
    pallas_call x1 -> x5, Pallas kernels: 21.5 us -> 39.7 us  [the longest x1 20.7 us: burn_in(): pl.pallas_call(functools.partial(burn_in_kernel, rounds), out_shape=jax.S...]
    ppermute x0 -> x7, waiting for transfers between devices: none -> 17.8 us  [exchanged(): parts.append(lax.ppermute(sent[k], 'tm', ring))]
    all_gather x1 -> x0, blocking collectives: 13.9 us -> none  [body(): pairs = lax.all_gather(own_pair, 'tm', axis=0, tiled=True)]
    all_to_all x1 -> x2, starting transfers between devices: 6.09 us -> 17.9 us  [the longest x1 11 us: body(): both = lax.all_to_all(both, EP, split_axis=0, concat_axis=0, tiled=True)]
    all_to_all x1, waiting for transfers between devices: 16.4 us -> 6.78 us  [body(): lax.all_to_all(sent_rows, EP, split_axis=0, concat_axis=0, tiled=True)]
    unnamed x15 -> x10, local copies, waits for them, and re-layouts: 9.62 us -> 0.03 us
  transfers between devices with their start and end apart: 2 -> 10, of which waited for: 2 -> 7; matrix products, arithmetic and copies ran while one was open for 4% -> 2% of each run, Pallas kernels for 14% -> 27%
where the time goes in v2:
time: 116 us; the launch traced here: 114 us
  Pallas kernels  39.7 us (34%)
  starting transfers between devices  34.8 us (30%)
  waiting for transfers between devices  31.9 us (28%)
  other arithmetic  2.71 us (2%)
  local copies, waits for them, and re-layouts  2.44 us (2%)
  between operations  2.16 us (2%)
    pallas_call x1, Pallas kernels, burn_in(): pl.pallas_call(functools.partial(burn_in_kernel, rounds), out_shape=jax.S...  20.7 us
    ppermute x7, waiting for transfers between devices, exchanged(): parts.append(lax.ppermute(sent[k], 'tm', ring))  17.8 us
    all_to_all x1, starting transfers between devices, body(): both = lax.all_to_all(both, EP, split_axis=0, concat_axis=0, tiled=True)  11 us
    all_to_all x1, starting transfers between devices, body(): lax.all_to_all(sent_rows, EP, split_axis=0, concat_axis=0, tiled=True)  8.61 us
    ppermute x7, starting transfers between devices, exchanged(): parts.append(lax.ppermute(sent[k], 'tm', ring))  8.32 us
    pallas_call x1, Pallas kernels, masked(): pl.pallas_call(masked_kernel, grid=(ids.shape[0] // count,), out_shape=ja...  8.26 us
    all_to_all x1, starting transfers between devices, body(): pairs = lax.all_to_all(pairs, 'tm', split_axis=0, concat_axis=0, tiled=True)  6.95 us
    all_to_all x1, waiting for transfers between devices, body(): lax.all_to_all(sent_rows, EP, split_axis=0, concat_axis=0, tiled=True)  6.78 us
  transfers between devices with their start and end apart: 10, of which 7 were waited for; matrix products, arithmetic and copies ran while one was open for 2% of the time, Pallas kernels for 27%

profile of v2, /device:TPU:1, one launch (start us, length us, event | category | flops | bytes accessed | tf_op | source)
XLA Modules:
  0.0 113.9 jit_solution(13204440448206037944)
XLA Ops:
  0.6 8.3 %masked_rows.1 = bf16[128,16,1024]{2,1,0:T(8,128)(2,1)} custom-call(s32[1]{0:T(128)} %bitcast.1.place, s32[128]{0:T(128)} %ids_hbm.1, s32[128]{0:T(128)} %starts_hbm.1, bf16[64,16,1024]{2,1,0:T(8,128)(2,1)} %obs.3), custom_call_target="tpu_custom_call" | custom-call | flops 100000000 | bytes 6291456 | tf_op jit(solution)/shard_map/masked_rows/pallas_call | solution.py:97
  8.9 8.6 %all-to-all-start = ((bf16[128,16,1024]{2,1,0:T(8,128)(2,1)}), bf16[128,16,1024]{2,1,0:T(8,128)(2,1)}, u32[]{:S(2)}, u32[]{:S(2)}) async-start(bf16[128,16,1024]{2,1,0:T(8,128)(2,1)} %masked_rows.1), calls=%async_computation | async-start | bytes 8388608 | tf_op jit(solution)/shard_map/all_to_all | solution.py:288
  18.3 3.1 %pack_rows.3 = (bf16[128,1024]{1,0:T(8,128)(2,1)}, bf16[128,1024]{1,0:T(8,128)(2,1)S(1)}, bf16[128,1024]{1,0:T(8,128)(2,1)S(1)}, bf16[128,1024]{1,0:T(8,128)(2,1...) custom-call(s32[1]{0:T(128)} %bitcast.1.place, ...), custom_call_target="tpu_custom_call" | custom-call | flops 1000000000 | bytes 4194304 | tf_op jit(solution)/shard_map/pack_rows/pallas_call | solution.py:62
  21.4 2.1 %collective-permute-start.7 = (bf16[128,1024]{1,0:T(8,128)(2,1)S(1)}, bf16[128,1024]{1,0:T(8,128)(2,1)S(1)}, u32[]{:S(2)}, u32[]{:S(2)}) collective-permute-start(bf16[128,1024]{1,0:T(8,128)(2,1)S(1)} %get-tuple-element.115), channel_id=1, source_target_pairs={{0,16},{16,32},{32,48},{48,64},{64,80},{80,96},{96,112},{112,0},{1... | collective-permute-start | bytes 786440 | tf_op jit(solution)/shard_map/ppermute | solution.py:283
  23.5 1.3 %collective-permute-start.8 = (bf16[128,1024]{1,0:T(8,128)(2,1)S(1)}, bf16[128,1024]{1,0:T(8,128)(2,1)S(1)}, u32[]{:S(2)}, u32[]{:S(2)}) collective-permute-start(bf16[128,1024]{1,0:T(8,128)(2,1)S(1)} %get-tuple-element.116), channel_id=1, source_target_pairs={{0,32},{16,48},{32,64},{48,80},{64,96},{80,112},{96,0},{112,16},{1... | collective-permute-start | bytes 786440 | tf_op jit(solution)/shard_map/ppermute | solution.py:283
  24.8 1.6 %collective-permute-start.9 = (bf16[128,1024]{1,0:T(8,128)(2,1)S(1)}, bf16[128,1024]{1,0:T(8,128)(2,1)S(1)}, u32[]{:S(2)}, u32[]{:S(2)}) collective-permute-start(bf16[128,1024]{1,0:T(8,128)(2,1)S(1)} %get-tuple-element.117), channel_id=1, source_target_pairs={{0,48},{16,64},{32,80},{48,96},{64,112},{80,0},{96,16},{112,32},{1... | collective-permute-start | bytes 786440 | tf_op jit(solution)/shard_map/ppermute | solution.py:283
  26.8 2.0 %collective-permute-start.11 = (bf16[128,1024]{1,0:T(8,128)(2,1)S(1)}, bf16[128,1024]{1,0:T(8,128)(2,1)S(1)}, u32[]{:S(2)}, u32[]{:S(2)}) collective-permute-start(bf16[128,1024]{1,0:T(8,128)(2,1)S(1)} %get-tuple-element.119), channel_id=1, source_target_pairs={{0,80},{16,96},{32,112},{48,0},{64,16},{80,32},{96,48},{112,64},{1... | collective-permute-start | bytes 786440 | tf_op jit(solution)/shard_map/ppermute | solution.py:283
  29.7 0.9 collective-permute-start.12
  30.6 6.3 %collective-permute-done.8 = bf16[128,1024]{1,0:T(8,128)(2,1)S(1)} collective-permute-done((bf16[128,1024]{1,0:T(8,128)(2,1)S(1)}, bf16[128,1024]{1,0:T(8,128)(2,1)S(1)}, u32[]{:S(2)}, u32[]{:S(2)}) %collective-permute-start.8) | collective-permute-done | bytes 262176 | tf_op jit(solution)/shard_map/ppermute | solution.py:283
  37.1 0.6 reduce_max.18
  38.5 1.9 %collective-permute-done.9 = bf16[128,1024]{1,0:T(8,128)(2,1)S(1)} collective-permute-done((bf16[128,1024]{1,0:T(8,128)(2,1)S(1)}, bf16[128,1024]{1,0:T(8,128)(2,1)S(1)}, u32[]{:S(2)}, u32[]{:S(2)}) %collective-permute-start.9) | collective-permute-done | bytes 262176 | tf_op jit(solution)/shard_map/ppermute | solution.py:283
  40.3 9.0 %collective-permute-done.10 = bf16[128,1024]{1,0:T(8,128)(2,1)S(1)} collective-permute-done((bf16[128,1024]{1,0:T(8,128)(2,1)S(1)}, bf16[128,1024]{1,0:T(8,128)(2,1)S(1)}, u32[]{:S(2)}, u32[]{:S(2)}) %collective-permute-start.10) | collective-permute-done | bytes 262176 | tf_op jit(solution)/shard_map/ppermute | solution.py:283
  50.0 21.1 %conditional.1 = (bf16[8,2,16,512]{3,2,1,0:T(8,128)(2,1)}) conditional(s32[]{:T(128)} %convert_element_type.29, (bf16[128,1024]{1,0:T(8,128)(2,1)}, bf16[128,1024]{1,0:T(8,128)(2,1)S(1)}, bf16[128,1024]{1,0:T(8,128)(2,1)S(1)}, bf16[128,1024]{1,0:T(8,128)(2,1)S(1)}, bf16[128,1024]{1,0:T(8,128)(2,1)S(1)}, /*index=5*/bf16[128,1024]{1,0:T(8,128)(2,1)S(1)}, ...), branch_computations={%region_6.7_spmd, %region_7.8_spmd} | conditional | flops 31000002560 | bytes 26239176 | solution.py:316
  50.2 20.7 %burn_in.2 = bf16[8,2,16,512]{3,2,1,0:T(8,128)(2,1)} custom-call(bf16[128,1024]{1,0:T(8,128)(2,1)} %get-tuple-element.64.refs_0_, bf16[128,1024]{1,0:T(8,128)(2,1)S(1)} %get-tuple-element.65.refs_1_, bf16[128,1024]{1,0:T(8,128)(2,1)S(1)} %get-tuple-element.66.refs_2_, bf16[128,1024]{1,0:T(8,128)(2,1)S(1)} %get-tuple-element.67.refs_3_, ...), custom_call_target="tpu_custom_call" | custom-call | flops 30000001024 | bytes 8388608 | tf_op jit(solution)/shard_map/cond/branch_0_fun/burn_in/pallas_call | solution.py:195
  71.1 6.8 %all-to-all-done.rows = bf16[128,16,1024]{2,1,0:T(8,128)(2,1)} async-done(((bf16[128,16,1024]{2,1,0:T(8,128)(2,1)}), bf16[128,16,1024]{2,1,0:T(8,128)(2,1)}, u32[]{:S(2)}, u32[]{:S(2)}) %all-to-all-start) | async-done | bytes 4194336 | tf_op jit(solution)/shard_map/all_to_all | solution.py:288
  77.9 6.9 %all-to-all-start.1 = ((bf16[8,2,16,512]{3,2,1,0:T(8,128)(2,1)}), bf16[8,2,16,512]{3,2,1,0:T(8,128)(2,1)S(1)}, u32[]{:S(2)}, u32[]{:S(2)}) async-start(bf16[8,2,16,512]{3,2,1,0:T(8,128)(2,1)} %get-tuple-element.223), calls=%async_computation.1 | async-start | bytes 524288 | tf_op jit(solution)/shard_map/all_to_all | solution.py:318
  85.1 6.2 %all-to-all-done.1.pairs = bf16[8,2,16,512]{3,2,1,0:T(8,128)(2,1)S(1)} async-done(((bf16[8,2,16,512]{3,2,1,0:T(8,128)(2,1)}), bf16[8,2,16,512]{3,2,1,0:T(8,128)(2,1)S(1)}, u32[]{:S(2)}, u32[]{:S(2)}) %all-to-all-start.1) | async-done | bytes 262176 | tf_op jit(solution)/shard_map/all_to_all | solution.py:318
  91.3 1.0 learner_order.1
  92.3 11.0 %all-to-all-start.2 = ((bf16[16,8,1152]{2,1,0:T(8,128)(2,1)}), bf16[16,8,1152]{2,1,0:T(8,128)(2,1)S(1)}, u32[]{:S(2)}, u32[]{:S(2)}) async-start(bf16[16,8,1152]{2,1,0:T(8,128)(2,1)} %bitcast.7), calls=%async_computation.2 | async-start | bytes 589824 | tf_op jit(solution)/shard_map/all_to_all | solution.py:323
  103.3 6.6 %copy_rows.1 = bf16[128,16,1024]{2,1,0:T(8,128)(2,1)} custom-call(bf16[128,16,1024]{2,1,0:T(8,128)(2,1)} %all-to-all-done.rows), custom_call_target="tpu_custom_call" | custom-call | flops 1000000000 | bytes 8388608 | tf_op jit(solution)/shard_map/copy_rows/pallas_call | solution.py:121
  109.9 1.1 all-to-all-done.2
  111.0 0.9 reshape.589
  111.9 0.7 slice_reduce_fusion
  113.3 0.6 convert_element_type.35
  (49 shorter events, 3.3 us)
Async XLA Ops:
  8.9 8.7 %copy-start.2 = (s32[128]{0:T(128)S(1)}, s32[128]{0:T(128)}, u32[]{:S(2)}) copy-start(s32[128]{0:T(128)} %starts_hbm.1) | copy-start | bytes 1540
  8.9 9.0 %copy-start.1 = (s32[128]{0:T(128)S(1)}, s32[128]{0:T(128)}, u32[]{:S(2)}) copy-start(s32[128]{0:T(128)} %ids_hbm.1) | copy-start | bytes 1540
  8.9 29.5 %copy-start = (f32[2048]{0:T(1024)S(1)}, f32[2048]{0:T(1024)}, u32[]{:S(2)}) copy-start(f32[2048]{0:T(1024)} %param.13) | copy-start | bytes 24580
  8.9 29.5 %copy-start.3 = (f32[512]{0:T(512)S(1)}, f32[512]{0:T(512)}, u32[]{:S(2)}) copy-start(f32[512]{0:T(512)} %param.14) | copy-start | bytes 6148
  8.9 68.9 %all-to-all-start = ((bf16[128,16,1024]{2,1,0:T(8,128)(2,1)}), bf16[128,16,1024]{2,1,0:T(8,128)(2,1)}, u32[]{:S(2)}, u32[]{:S(2)}) async-start(bf16[128,16,1024]{2,1,0:T(8,128)(2,1)} %masked_rows.1), calls=%async_computation | async-start | bytes 8388608 | tf_op jit(solution)/shard_map/all_to_all | solution.py:288
  21.4 8.3 %collective-permute-start.7 = (bf16[128,1024]{1,0:T(8,128)(2,1)S(1)}, bf16[128,1024]{1,0:T(8,128)(2,1)S(1)}, u32[]{:S(2)}, u32[]{:S(2)}) collective-permute-start(bf16[128,1024]{1,0:T(8,128)(2,1)S(1)} %get-tuple-element.115), channel_id=1, source_target_pairs={{0,16},{16,32},{32,48},{48,64},{64,80},{80,96},{96,112},{112,0},{1... | collective-permute-start | bytes 786440 | tf_op jit(solution)/shard_map/ppermute | solution.py:283
  23.5 13.4 %collective-permute-start.8 = (bf16[128,1024]{1,0:T(8,128)(2,1)S(1)}, bf16[128,1024]{1,0:T(8,128)(2,1)S(1)}, u32[]{:S(2)}, u32[]{:S(2)}) collective-permute-start(bf16[128,1024]{1,0:T(8,128)(2,1)S(1)} %get-tuple-element.116), channel_id=1, source_target_pairs={{0,32},{16,48},{32,64},{48,80},{64,96},{80,112},{96,0},{112,16},{1... | collective-permute-start | bytes 786440 | tf_op jit(solution)/shard_map/ppermute | solution.py:283
  24.8 15.5 %collective-permute-start.9 = (bf16[128,1024]{1,0:T(8,128)(2,1)S(1)}, bf16[128,1024]{1,0:T(8,128)(2,1)S(1)}, u32[]{:S(2)}, u32[]{:S(2)}) collective-permute-start(bf16[128,1024]{1,0:T(8,128)(2,1)S(1)} %get-tuple-element.117), channel_id=1, source_target_pairs={{0,48},{16,64},{32,80},{48,96},{64,112},{80,0},{96,16},{112,32},{1... | collective-permute-start | bytes 786440 | tf_op jit(solution)/shard_map/ppermute | solution.py:283
  26.4 23.0 %collective-permute-start.10 = (bf16[128,1024]{1,0:T(8,128)(2,1)S(1)}, bf16[128,1024]{1,0:T(8,128)(2,1)S(1)}, u32[]{:S(2)}, u32[]{:S(2)}) collective-permute-start(bf16[128,1024]{1,0:T(8,128)(2,1)S(1)} %get-tuple-element.118), channel_id=1, source_target_pairs={{0,64},{16,80},{32,96},{48,112},{64,0},{80,16},{96,32},{112,48},{1... | collective-permute-start | bytes 786440 | tf_op jit(solution)/shard_map/ppermute | solution.py:283
  26.8 23.2 %collective-permute-start.11 = (bf16[128,1024]{1,0:T(8,128)(2,1)S(1)}, bf16[128,1024]{1,0:T(8,128)(2,1)S(1)}, u32[]{:S(2)}, u32[]{:S(2)}) collective-permute-start(bf16[128,1024]{1,0:T(8,128)(2,1)S(1)} %get-tuple-element.119), channel_id=1, source_target_pairs={{0,80},{16,96},{32,112},{48,0},{64,16},{80,32},{96,48},{112,64},{1... | collective-permute-start | bytes 786440 | tf_op jit(solution)/shard_map/ppermute | solution.py:283
  29.7 20.3 %collective-permute-start.12 = (bf16[128,1024]{1,0:T(8,128)(2,1)S(1)}, bf16[128,1024]{1,0:T(8,128)(2,1)S(1)}, u32[]{:S(2)}, u32[]{:S(2)}) collective-permute-start(bf16[128,1024]{1,0:T(8,128)(2,1)S(1)} %get-tuple-element.120), channel_id=1, source_target_pairs={{0,96},{16,112},{32,0},{48,16},{64,32},{80,48},{96,64},{112,80},{1... | collective-permute-start | bytes 786440 | tf_op jit(solution)/shard_map/ppermute | solution.py:283
  36.9 13.1 %collective-permute-start.13 = (bf16[128,1024]{1,0:T(8,128)(2,1)S(1)}, bf16[128,1024]{1,0:T(8,128)(2,1)}, u32[]{:S(2)}, u32[]{:S(2)}) collective-permute-start(bf16[128,1024]{1,0:T(8,128)(2,1)S(1)} %get-tuple-element.121), channel_id=1, source_target_pairs={{0,112},{16,0},{32,16},{48,32},{64,48},{80,64},{96,80},{112,96},{1... | collective-permute-start | bytes 786440 | tf_op jit(solution)/shard_map/ppermute | solution.py:283
  50.0 35.0 %copy-start.10 = (s32[128]{0:T(128)S(1)}, s32[128]{0:T(128)}, u32[]{:S(2)}) copy-start(s32[128]{0:T(128)} %param.17) | copy-start | bytes 1540
  77.9 13.4 %all-to-all-start.1 = ((bf16[8,2,16,512]{3,2,1,0:T(8,128)(2,1)}), bf16[8,2,16,512]{3,2,1,0:T(8,128)(2,1)S(1)}, u32[]{:S(2)}, u32[]{:S(2)}) async-start(bf16[8,2,16,512]{3,2,1,0:T(8,128)(2,1)} %get-tuple-element.223), calls=%async_computation.1 | async-start | bytes 524288 | tf_op jit(solution)/shard_map/all_to_all | solution.py:318
  92.3 18.7 %all-to-all-start.2 = ((bf16[16,8,1152]{2,1,0:T(8,128)(2,1)}), bf16[16,8,1152]{2,1,0:T(8,128)(2,1)S(1)}, u32[]{:S(2)}, u32[]{:S(2)}) async-start(bf16[16,8,1152]{2,1,0:T(8,128)(2,1)} %bitcast.7), calls=%async_computation.2 | async-start | bytes 589824 | tf_op jit(solution)/shard_map/all_to_all | solution.py:323

commit v3 on v2

--- a/solution.py
+++ b/solution.py
@@ -36,8 +36,7 @@
     return jnp.dot(a, b, preferred_element_type=jnp.float32)
 
 
-def pack_kernel(base, place, ids, starts_ref, obs, *rest):
-    outs, rows_of = rest[:-1], rest[-1]
+def pack_kernel(base, place, ids, starts_ref, obs, out, rows_of, packed, sem):
     shards, count = starts_ref.shape
     shard_steps = obs.shape[1]
     lanes = count * shard_steps
@@ -51,9 +50,11 @@
     for k in range(shards):
         for i in range(count):
             rows_of[k, i * shard_steps : (i + 1) * shard_steps, :] = obs[ids[k, i]]
+        hot = one_hot(iota((ROOM, lanes), 0) == slot[k : k + 1, :])
+        packed[k] = f32_dot(hot, rows_of[k]).astype(jnp.bfloat16)
+        pltpu.make_async_copy(packed.at[k], out.at[k], sem.at[k]).start()
     for k in range(shards):
-        hot = one_hot(iota((ROOM, lanes), 0) == slot[k : k + 1, :])
-        outs[k][...] = f32_dot(hot, rows_of[k]).astype(jnp.bfloat16)
+        pltpu.make_async_copy(packed.at[k], out.at[k], sem.at[k]).wait()
 
 
 def pack(base, position, ids, starts, observations):
@@ -61,91 +62,96 @@
     _, shard_steps, width = observations.shape
     return pl.pallas_call(
         functools.partial(pack_kernel, base),
-        out_shape=[jax.ShapeDtypeStruct((ROOM, width), jnp.bfloat16)] * shards,
+        out_shape=jax.ShapeDtypeStruct((shards, ROOM, width), jnp.bfloat16),
         in_specs=[SMEM, SMEM, VMEM, VMEM],
-        out_specs=[VMEM] * shards,
-        scratch_shapes=[pltpu.VMEM((shards, count * shard_steps, width), jnp.bfloat16)],
+        out_specs=HBM,
+        scratch_shapes=[
+            pltpu.VMEM((shards, count * shard_steps, width), jnp.bfloat16),
+            pltpu.VMEM((shards, ROOM, width), jnp.bfloat16),
+            pltpu.SemaphoreType.DMA((shards,)),
+        ],
         compiler_params=pltpu.CompilerParams(vmem_limit_bytes=24 * MIB),
         cost_estimate=pl.CostEstimate(flops=10**9, bytes_accessed=4 * MIB, transcendentals=0),
         name="pack_rows",
     )(position.reshape(1), ids, starts, observations)
 
 
-def masked_kernel(place, ids_hbm, starts_hbm, obs, out, ids, starts, sem):
-    block = pl.program_id(0)
-
-    @pl.when(block == 0)
-    def _():
-        ids_copy = pltpu.make_async_copy(ids_hbm, ids, sem.at[0])
-        starts_copy = pltpu.make_async_copy(starts_hbm, starts, sem.at[1])
-        ids_copy.start()
-        starts_copy.start()
-        ids_copy.wait()
-        starts_copy.wait()
-
-    count, shard_steps, width = out.shape
+def masked_kernel(place, blocks, ids, starts, obs, *refs):
+    outs, (held, sem) = refs[:-2], refs[-2:]
+    count, shard_steps, width = outs[0].shape
     step = place[0] * shard_steps + iota((shard_steps, width), 0)
-    for i in range(count):
-        g = block * count + i
-        keep = ((step - starts[g] - BURN) & (STEPS - 1)) < UNROLL
-        out[i] = jnp.where(keep, obs[ids[g]], jnp.zeros((), jnp.bfloat16))
-
-
-def masked(position, ids, starts, observations):
+    copies = [pltpu.make_async_copy(held.at[n], out, sem.at[n]) for n, out in enumerate(outs)]
+    for n in range(len(outs)):
+        for i in range(count):
+            g = blocks[n] * count + i
+            keep = ((step - starts[g] - BURN) & (STEPS - 1)) < UNROLL
+            held[n, i] = jnp.where(keep, obs[ids[g]], jnp.zeros((), jnp.bfloat16))
+        copies[n].start()
+    for copy in copies:
+        copy.wait()
+
+
+def masked(position, blocks, ids, starts, observations):
     _, shard_steps, width = observations.shape
-    count = 8
+    learners = blocks.shape[0]
+    block = (ids.shape[0] // learners, shard_steps, width)
     return pl.pallas_call(
         masked_kernel,
-        grid=(ids.shape[0] // count,),
-        out_shape=jax.ShapeDtypeStruct((ids.shape[0], shard_steps, width), jnp.bfloat16),
-        in_specs=[SMEM, HBM, HBM, VMEM],
-        out_specs=pl.BlockSpec((count, shard_steps, width), lambda b: (b, 0, 0)),
+        out_shape=[jax.ShapeDtypeStruct(block, jnp.bfloat16)] * learners,
+        in_specs=[SMEM, SMEM, SMEM, SMEM, VMEM],
+        out_specs=[HBM] * learners,
         scratch_shapes=[
-            pltpu.SMEM(ids.shape, jnp.int32),
-            pltpu.SMEM(starts.shape, jnp.int32),
-            pltpu.SemaphoreType.DMA((2,)),
+            pltpu.VMEM((learners, *block), jnp.bfloat16),
+            pltpu.SemaphoreType.DMA((learners,)),
         ],
         compiler_params=pltpu.CompilerParams(vmem_limit_bytes=60 * MIB),
         cost_estimate=pl.CostEstimate(flops=10**8, bytes_accessed=6 * MIB, transcendentals=0),
         name="masked_rows",
-    )(position.reshape(1), ids, starts, observations)
-
-
-def copy_kernel(rows, out):
-    out[...] = rows[...]
-
-
-def copied(rows):
-    _, shard_steps, width = rows.shape
-    block = pl.BlockSpec((16, shard_steps, width), lambda b: (b, 0, 0))
-    return pl.pallas_call(
-        copy_kernel,
-        grid=(rows.shape[0] // 16,),
-        out_shape=jax.ShapeDtypeStruct(rows.shape, rows.dtype),
-        in_specs=[block],
-        out_specs=block,
-        compiler_params=pltpu.CompilerParams(vmem_limit_bytes=48 * MIB),
+    )(position.reshape(1), blocks, ids, starts, observations)
+
+
+def place_kernel(blocks, *refs):
+    rows, (out, sem) = refs[:-2], refs[-2:]
+    count = rows[0].shape[0]
+    copies = [
+        pltpu.make_async_copy(block, out.at[pl.ds(blocks[n] * count, count)], sem.at[n])
+        for n, block in enumerate(rows)
+    ]
+    for copy in copies:
+        copy.start()
+    for copy in copies:
+        copy.wait()
+
+
+def placed(rows, blocks):
+    count, shard_steps, width = rows[0].shape
+    return pl.pallas_call(
+        place_kernel,
+        out_shape=jax.ShapeDtypeStruct((len(rows) * count, shard_steps, width), rows[0].dtype),
+        in_specs=[SMEM] + [VMEM] * len(rows),
+        out_specs=HBM,
+        scratch_shapes=[pltpu.SemaphoreType.DMA((len(rows),))],
+        compiler_params=pltpu.CompilerParams(vmem_limit_bytes=8 * MIB),
         cost_estimate=pl.CostEstimate(flops=10**9, bytes_accessed=8 * MIB, transcendentals=0),
-        name="copy_rows",
-    )(rows)
+        name="place_rows",
+    )(blocks, *rows)
 
 
 def burn_in_kernel(rounds, *refs):
-    parts, refs = refs[: 8 * rounds], refs[8 * rounds :]
+    parts, refs = refs[:rounds], refs[rounds:]
     columns, (win_hbm, wh_hbm, bias_ref, out_ref), refs = refs[:rounds], refs[rounds : rounds + 4], refs[rounds + 4 :]
     xs, hots, (win, wh, proj, xsem, wsem, hsem) = refs[:rounds], refs[rounds : 2 * rounds], refs[2 * rounds :]
     copies, _, count, hidden_width = out_ref.shape
     win_copy = pltpu.make_async_copy(win_hbm, win, wsem)
     wh_copy = pltpu.make_async_copy(wh_hbm, wh, hsem)
     row_copies = [
-        pltpu.make_async_copy(part, xs[n // 8].at[pl.ds((n % 8) * ROOM, ROOM)], xsem.at[n])
-        for n, part in enumerate(parts)
+        pltpu.make_async_copy(part, rows, xsem.at[n]) for n, (part, rows) in enumerate(zip(parts, xs))
     ]
     for copy in row_copies:
         copy.start()
     win_copy.start()
     wh_copy.start()
-    lane = iota((count, 8 * ROOM), 1)
+    lane = iota((count, xs[0].shape[0]), 1)
     for hot, column in zip(hots, columns):
         for t in range(BURN):
             at = slice(t * count, (t + 1) * count)
@@ -187,7 +193,7 @@
 
 def burn_in(parts, columns, input_weight, hidden_weight, bias):
     rounds = len(columns)
-    shards = len(parts) // rounds
+    shards = parts[0].shape[0] // ROOM
     width = input_weight.shape[0]
     hidden_width = hidden_weight.shape[0]
     total = columns[0].shape[0]
@@ -238,7 +244,30 @@
         compiler_params=pltpu.CompilerParams(vmem_limit_bytes=8 * MIB),
         cost_estimate=pl.CostEstimate(flops=10**8, bytes_accessed=MIB, transcendentals=0),
         name="learner_order",
-    )(pairs, rank[:, None], raw[:, None])
+    )(pairs, rank, raw)
+
+
+def weights_kernel(received, out):
+    total = received.shape[0]
+    raw = received[...].astype(jnp.float32)
+    lane = iota(raw.shape, 1)
+    peak = jnp.max(jnp.where(lane == 1, raw, 0.0))
+    weight = jnp.sum(jnp.where(lane == 0, raw, 0.0), axis=1, keepdims=True) / peak
+    weight = jnp.where(iota((total, total), 0) == iota((total, total), 1), weight, 0.0)
+    out[...] = jnp.sum(weight, axis=0, keepdims=True).astype(jnp.bfloat16)
+
+
+def normalized(received):
+    total, lanes = received.shape
+    return pl.pallas_call(
+        weights_kernel,
+        grid=(1,),
+        out_shape=jax.ShapeDtypeStruct((1, total), jnp.bfloat16),
+        in_specs=[pl.BlockSpec((total, 128), lambda n: (0, lanes // 128 - 1))],
+        out_specs=pl.BlockSpec((1, total), lambda n: (0, 0)),
+        compiler_params=pltpu.CompilerParams(vmem_limit_bytes=4 * MIB),
+        name="weights",
+    )(received)[0]
 
 
 def rows_in_shard(starts, shard, shard_steps):
@@ -257,7 +286,7 @@
     start_steps,
     priorities,
 ):
-    shard_steps, _ = observations.shape[1:]
+    shard_steps, width = observations.shape[1:]
     seq_count = episode_ids.shape[0]
     hidden_width = hidden_weight.shape[0]
     shards = lax.axis_size("tm")
@@ -270,24 +299,35 @@
     key = start_steps * seq_count + index
     rank = jnp.sum((key[None, :] < key[:, None]).astype(jnp.int32), axis=1)
     turn = jnp.arange(shards, dtype=jnp.int32)
-    dealt = jnp.arange(own_count, dtype=jnp.int32)[None, :] * shards + ((position + turn) % shards)[:, None]
+    dealt = jnp.arange(own_count, dtype=jnp.int32)[None, :] * shards + turn[:, None]
     chosen = rank[None, None, :] == dealt[:, :, None]
     ids = jnp.sum(jnp.where(chosen, episode_ids, 0), axis=2)
     starts = jnp.sum(jnp.where(chosen, start_steps, 0), axis=2)
 
     def exchanged(base):
         sent = pack(base, position, ids, starts, observations)
-        parts = [sent[0]]
-        for k in range(1, shards):
-            ring = [(i, (i + k) % shards) for i in range(shards)]
-            parts.append(lax.ppermute(sent[k], "tm", ring))
-        return parts
-
-    parts = exchanged(0)
-    sent_rows = masked(position, episode_ids, start_steps, observations)
-    moved_rows = lax.all_to_all(sent_rows, EP, split_axis=0, concat_axis=0, tiled=True)
-
-    own = starts[0]
+        rows = lax.all_to_all(sent, "tm", split_axis=0, concat_axis=0, tiled=True)
+        return rows.reshape(shards * ROOM, width)
+
+    along, across = lax.axis_size("ep_0"), lax.axis_size("ep_1")
+    offsets = jnp.arange(learners, dtype=jnp.int32)
+    here = [lax.axis_index(axis).astype(jnp.int32) for axis in EP]
+
+    def block_at(sign):
+        first = (here[0] + sign * (offsets // across)) % along
+        return first * across + (here[1] + sign * (offsets % across)) % across
+
+    rows_in = exchanged(0)
+    sent_rows = masked(position, block_at(1), episode_ids, start_steps, observations)
+    moved_rows = [sent_rows[0]]
+    for n in range(1, learners):
+        ring = [
+            (i, (i // across + n // across) % along * across + (i + n) % across)
+            for i in range(learners)
+        ]
+        moved_rows.append(lax.ppermute(sent_rows[n], EP, ring))
+
+    own = lax.dynamic_index_in_dim(starts, position, 0, keepdims=False)
     step = jnp.arange(BURN, dtype=jnp.int32)[:, None]
     shard = (own + step) % STEPS // shard_steps
     earlier = jnp.arange(own_count)[None, None, :] < jnp.arange(own_count)[None, :, None]
@@ -296,36 +336,34 @@
     )
     first = jnp.maximum((own % shard_steps + step) // shard_steps * shard_steps - own % shard_steps, 0)
     slot = ahead + step - first
-    sender = (position - shard) % shards
-    column = (sender * ROOM + slot % ROOM).reshape(BURN * own_count, 1)
-    late = (slot >= ROOM).reshape(BURN * own_count, 1)
+    column = (shard * ROOM + slot % ROOM).reshape(BURN * own_count, 1)
+    second = (slot >= ROOM).reshape(BURN * own_count, 1)
     pair_rows = jnp.sum(rows_in_shard(starts[None], turn[:, None, None], shard_steps), axis=2)
     crowded = jnp.max(pair_rows) > ROOM
 
     blank = jnp.zeros((hidden_width,), jnp.float32)
     bias = (gate_bias + jnp.concatenate([blank, forget_bias, blank, blank]))[None, :]
 
+    raw_weight = jnp.exp(-IMPORTANCE * jnp.log(priorities.astype(jnp.float32))).astype(jnp.bfloat16)
+    raw_column = raw_weight.astype(jnp.float32)[:, None]
+    column, rank_column, raw_column = lax.optimization_barrier((column, rank[:, None], raw_column))
+
     def usual():
-        return burn_in(parts, [column], input_weight, hidden_weight, bias)
+        return burn_in([rows_in], [column], input_weight, hidden_weight, bias)
 
     def two_rounds():
-        columns = [jnp.where(late, -1, column), jnp.where(late, column, -1)]
-        more = exchanged(ROOM)
-        return burn_in(parts + more, columns, input_weight, hidden_weight, bias)
+        columns = [jnp.where(second, -1, column), jnp.where(second, column, -1)]
+        return burn_in([rows_in, exchanged(ROOM)], columns, input_weight, hidden_weight, bias)
 
     pairs = lax.cond(crowded, two_rounds, usual)
-    pairs, moved_rows = lax.optimization_barrier((pairs, moved_rows))
     pairs = lax.all_to_all(pairs, "tm", split_axis=0, concat_axis=0, tiled=True)
-    moved_rows = copied(moved_rows)
-    raw_weight = jnp.exp(-IMPORTANCE * jnp.log(priorities.astype(jnp.float32))).astype(jnp.bfloat16)
-    both = ordered(pairs, rank, raw_weight.astype(jnp.float32))
+    moved_rows = placed(moved_rows, block_at(-1))
+    both = ordered(pairs, rank_column, raw_column)
     both = both.reshape(learners, per_learner, both.shape[1])
     both = lax.all_to_all(both, EP, split_axis=0, concat_axis=0, tiled=True)
     start_state = both[:, :, : 2 * hidden_width].reshape(seq_count, 2, hidden_width)
-    raw = both[:, :, 2 * hidden_width].astype(jnp.float32)
-    peak = jnp.max(both[:, :, 2 * hidden_width + 1]).astype(jnp.float32)
-    weights = (raw / peak).astype(jnp.bfloat16)
-    return (moved_rows, start_state, weights.reshape(seq_count))
+    weights = normalized(both.reshape(seq_count, both.shape[2]))
+    return (moved_rows, start_state, weights)
 
 
 def solution(mesh):

time: 116 us -> 121 us (1.043)
  starting transfers between devices: 34.8 us -> 45.2 us
  Pallas kernels: 39.7 us -> 32.6 us
    ppermute x7 -> x15, starting transfers between devices: 8.32 us -> 28.5 us  [body(): moved_rows.append(lax.ppermute(sent_rows[n], EP, ring))]
    ppermute x7 -> x15, waiting for transfers between devices: 17.8 us -> 31.1 us  [body(): moved_rows.append(lax.ppermute(sent_rows[n], EP, ring))]
    pallas_call x3 -> x4, Pallas kernels: 17.9 us -> 10.4 us  [the longest x1 3.43 us: pack(): pl.pallas_call(functools.partial(pack_kernel, base), out_shape=jax.ShapeD...]
    all_to_all x1, waiting for transfers between devices: 6.78 us -> 0.01 us  [exchanged(): rows = lax.all_to_all(sent, 'tm', split_axis=0, concat_axis=0, tiled=True)]
    all_to_all x1, starting transfers between devices: 11 us -> 4.27 us  [body(): both = lax.all_to_all(both, EP, split_axis=0, concat_axis=0, tiled=True)]
    all_to_all x1, waiting for transfers between devices: 6.23 us -> 0.01 us  [body(): pairs = lax.all_to_all(pairs, 'tm', split_axis=0, concat_axis=0, tiled=True)]
    all_to_all x1, starting transfers between devices: 8.61 us -> 6.1 us  [exchanged(): rows = lax.all_to_all(sent, 'tm', split_axis=0, concat_axis=0, tiled=True)]
    unnamed x10 -> x18, local copies, waits for them, and re-layouts: 0.03 us -> 1.45 us
  transfers between devices with their start and end apart: 10 -> 18, of which waited for: 7 -> 6; matrix products, arithmetic and copies ran while one was open for 2% -> 2% of each run, Pallas kernels for 27% -> 24%
where the time goes in v3:
time: 121 us; the launch traced here: 119 us
  starting transfers between devices  45.2 us (37%)
  Pallas kernels  32.6 us (27%)
  waiting for transfers between devices  32.6 us (27%)
  other arithmetic  3.75 us (3%)
  local copies, waits for them, and re-layouts  3.24 us (3%)
  between operations  1.56 us (1%)
    ppermute x15, waiting for transfers between devices, body(): moved_rows.append(lax.ppermute(sent_rows[n], EP, ring))  31.1 us
    ppermute x15, starting transfers between devices, body(): moved_rows.append(lax.ppermute(sent_rows[n], EP, ring))  28.5 us
    pallas_call x1, Pallas kernels, burn_in(): pl.pallas_call(functools.partial(burn_in_kernel, rounds), out_shape=jax.S...  21.3 us
    all_to_all x1, starting transfers between devices, body(): pairs = lax.all_to_all(pairs, 'tm', split_axis=0, concat_axis=0, tiled=True)  6.27 us
    all_to_all x1, starting transfers between devices, exchanged(): rows = lax.all_to_all(sent, 'tm', split_axis=0, concat_axis=0, tiled=True)  6.1 us
    all_to_all x1, starting transfers between devices, body(): both = lax.all_to_all(both, EP, split_axis=0, concat_axis=0, tiled=True)  4.27 us
    pallas_call x1, Pallas kernels, pack(): pl.pallas_call(functools.partial(pack_kernel, base), out_shape=jax.ShapeD...  3.43 us
    pallas_call x1, Pallas kernels, placed(): pl.pallas_call(place_kernel, out_shape=jax.ShapeDtypeStruct((len(rows) *...  3.42 us
  transfers between devices with their start and end apart: 18, of which 6 were waited for; matrix products, arithmetic and copies ran while one was open for 2% of the time, Pallas kernels for 24%

profile of v3, /device:TPU:1, one launch (start us, length us, event | category | flops | bytes accessed | tf_op | source)
XLA Modules:
  0.0 119.2 jit_solution(8793629300626866274)
XLA Ops:
  2.6 3.4 %pack_rows.3 = bf16[8,128,1024]{2,1,0:T(8,128)(2,1)} custom-call(s32[1]{0:T(128)} %bitcast.2.place, s32[8,16]{1,0:T(8,128)S(1)} %get-tuple-element.122.ids, s32[8,16]{1,0:T(8,128)S(1)} %get-tuple-element.123.starts_ref, bf16[64,16,1024]{2,1,0:T(8,128)(2,1)} %obs.3), custom_call_target="tpu_custom_call" | custom-call | flops 1000000000 | bytes 4194304 | tf_op jit(solution)/shard_map/pack_rows/pallas_call | solution.py:63
  6.0 6.1 %all-to-all-start.1 = ((bf16[8,128,1024]{2,1,0:T(8,128)(2,1)}), bf16[8,128,1024]{2,1,0:T(8,128)(2,1)}, u32[]{:S(2)}, u32[]{:S(2)}) async-start(bf16[8,128,1024]{2,1,0:T(8,128)(2,1)} %pack_rows.3), calls=%async_computation.1 | async-start | bytes 4194304 | tf_op jit(solution)/shard_map/all_to_all | solution.py:309
  12.7 2.8 %masked_rows.1 = (bf16[8,16,1024]{2,1,0:T(8,128)(2,1)}, bf16[8,16,1024]{2,1,0:T(8,128)(2,1)}, bf16[8,16,1024]{2,1,0:T(8,128)(2,1)}, bf16[8,16,1024]{2,1,0:T(8,12...) custom-call(s32[1]{0:T(128)} %bitcast.2.place, ...), custom_call_target="tpu_custom_call" | custom-call | flops 100000000 | bytes 6291456 | tf_op jit(solution)/shard_map/masked_rows/pallas_call | solution.py:98
  15.6 1.7 %collective-permute-start = (bf16[8,16,1024]{2,1,0:T(8,128)(2,1)}, bf16[8,16,1024]{2,1,0:T(8,128)(2,1)S(1)}, u32[]{:S(2)}, u32[]{:S(2)}) collective-permute-start(bf16[8,16,1024]{2,1,0:T(8,128)(2,1)} %get-tuple-element.74), channel_id=1, source_target_pairs={{0,1},{1,2},{2,3},{3,0},{4,5},{5,6},{6,7},{7,4},{8,9},{9,10},{10,1... | collective-permute-start | bytes 786440 | tf_op jit(solution)/shard_map/ppermute | solution.py:328
  17.3 3.3 %collective-permute-start.1 = (bf16[8,16,1024]{2,1,0:T(8,128)(2,1)}, bf16[8,16,1024]{2,1,0:T(8,128)(2,1)S(1)}, u32[]{:S(2)}, u32[]{:S(2)}) collective-permute-start(bf16[8,16,1024]{2,1,0:T(8,128)(2,1)} %get-tuple-element.75), channel_id=1, source_target_pairs={{0,2},{1,3},{2,0},{3,1},{4,6},{5,7},{6,4},{7,5},{8,10},{9,11},{10,... | collective-permute-start | bytes 786440 | tf_op jit(solution)/shard_map/ppermute | solution.py:328
  22.5 1.7 %collective-permute-start.4 = (bf16[8,16,1024]{2,1,0:T(8,128)(2,1)}, bf16[8,16,1024]{2,1,0:T(8,128)(2,1)S(1)}, u32[]{:S(2)}, u32[]{:S(2)}) collective-permute-start(bf16[8,16,1024]{2,1,0:T(8,128)(2,1)} %get-tuple-element.78), channel_id=1, source_target_pairs={{0,5},{1,6},{2,7},{3,4},{4,9},{5,10},{6,11},{7,8},{8,13},{9,14},{1... | collective-permute-start | bytes 786440 | tf_op jit(solution)/shard_map/ppermute | solution.py:328
  25.1 1.2 %collective-permute-done.refs_1_ = bf16[8,16,1024]{2,1,0:T(8,128)(2,1)S(1)} collective-permute-done((bf16[8,16,1024]{2,1,0:T(8,128)(2,1)}, bf16[8,16,1024]{2,1,0:T(8,128)(2,1)S(1)}, u32[]{:S(2)}, u32[]{:S(2)}) %collective-permute-start) | collective-permute-done | bytes 262176 | tf_op jit(solution)/shard_map/ppermute | solution.py:328
  26.4 2.4 %collective-permute-start.5 = (bf16[8,16,1024]{2,1,0:T(8,128)(2,1)}, bf16[8,16,1024]{2,1,0:T(8,128)(2,1)}, u32[]{:S(2)}, u32[]{:S(2)}) collective-permute-start(bf16[8,16,1024]{2,1,0:T(8,128)(2,1)} %get-tuple-element.79), channel_id=1, source_target_pairs={{0,6},{1,7},{2,4},{3,5},{4,10},{5,11},{6,8},{7,9},{8,14},{9,15},{1... | collective-permute-start | bytes 786440 | tf_op jit(solution)/shard_map/ppermute | solution.py:328
  28.8 12.4 %collective-permute-done.1.refs_2_ = bf16[8,16,1024]{2,1,0:T(8,128)(2,1)S(1)} collective-permute-done((bf16[8,16,1024]{2,1,0:T(8,128)(2,1)}, bf16[8,16,1024]{2,1,0:T(8,128)(2,1)S(1)}, u32[]{:S(2)}, u32[]{:S(2)}) %collective-permute-start.1) | collective-permute-done | bytes 262176 | tf_op jit(solution)/shard_map/ppermute | solution.py:328
  41.2 2.7 %collective-permute-start.7 = (bf16[8,16,1024]{2,1,0:T(8,128)(2,1)}, bf16[8,16,1024]{2,1,0:T(8,128)(2,1)}, u32[]{:S(2)}, u32[]{:S(2)}) collective-permute-start(bf16[8,16,1024]{2,1,0:T(8,128)(2,1)} %get-tuple-element.81), channel_id=1, source_target_pairs={{0,8},{1,9},{2,10},{3,11},{4,12},{5,13},{6,14},{7,15},{8,0},{9,1},... | collective-permute-start | bytes 786440 | tf_op jit(solution)/shard_map/ppermute | solution.py:328
  44.7 5.1 %collective-permute-start.8 = (bf16[8,16,1024]{2,1,0:T(8,128)(2,1)}, bf16[8,16,1024]{2,1,0:T(8,128)(2,1)}, u32[]{:S(2)}, u32[]{:S(2)}) collective-permute-start(bf16[8,16,1024]{2,1,0:T(8,128)(2,1)} %get-tuple-element.82), channel_id=1, source_target_pairs={{0,9},{1,10},{2,11},{3,8},{4,13},{5,14},{6,15},{7,12},{8,1},{9,2},... | collective-permute-start | bytes 786440 | tf_op jit(solution)/shard_map/ppermute | solution.py:328
  52.1 21.7 %conditional.1 = (bf16[8,2,16,512]{3,2,1,0:T(8,128)(2,1)}) conditional(s32[]{:T(128)} %convert_element_type.14, (bf16[1024,1024]{1,0:T(8,128)(2,1)}, s32[640,1]{0,1:T(1,128)S(1)}, bf16[1024,2048]{1,0:T(8,128)(2,1)}, bf16[512,2048]{1,0:T(8,128)(2,1)}, f32[1,2048]{1,0:T(1,128)S(1)}) %tuple.31, (s32[]{:T(128)}, s32[8,16]{1,0:T(8,128)S(1)}, ...), branch_computations={%region_6.7_spmd, %region_7.8_spmd} | conditional | flops 31000002560 | bytes 18974588 | solution.py:358
  52.3 21.3 %burn_in.2 = bf16[8,2,16,512]{3,2,1,0:T(8,128)(2,1)} custom-call(bf16[1024,1024]{1,0:T(8,128)(2,1)} %get-tuple-element.36.refs_0_, s32[640,1]{1,0:T(8,128)S(1)} %copy.20.refs_1_, bf16[1024,2048]{1,0:T(8,128)(2,1)} %get-tuple-element.38.refs_2_, bf16[512,2048]{1,0:T(8,128)(2,1)} %get-tuple-element.39.refs_3_, f32[1,2048]{1,0:T(1,128)S(1)} %get-tuple-element.40.refs_4_), custom_call_target="tpu_custom_call" | custom-call | flops 30000001024 | bytes 8388608 | tf_op jit(solution)/shard_map/cond/branch_0_fun/burn_in/pallas_call | solution.py:201
  73.8 6.3 %all-to-all-start.2 = ((bf16[8,2,16,512]{3,2,1,0:T(8,128)(2,1)}), bf16[8,2,16,512]{3,2,1,0:T(8,128)(2,1)S(1)}, u32[]{:S(2)}, u32[]{:S(2)}) async-start(bf16[8,2,16,512]{3,2,1,0:T(8,128)(2,1)} %get-tuple-element.132), calls=%async_computation.2 | async-start | bytes 524288 | tf_op jit(solution)/shard_map/all_to_all | solution.py:359
  80.1 1.8 %collective-permute-start.10 = (bf16[8,16,1024]{2,1,0:T(8,128)(2,1)}, bf16[8,16,1024]{2,1,0:T(8,128)(2,1)S(1)}, u32[]{:S(2)}, u32[]{:S(2)}) collective-permute-start(bf16[8,16,1024]{2,1,0:T(8,128)(2,1)} %get-tuple-element.84), channel_id=1, source_target_pairs={{0,11},{1,8},{2,9},{3,10},{4,15},{5,12},{6,13},{7,14},{8,3},{9,0},... | collective-permute-start | bytes 786440 | tf_op jit(solution)/shard_map/ppermute | solution.py:328
  81.9 2.1 %collective-permute-start.11 = (bf16[8,16,1024]{2,1,0:T(8,128)(2,1)}, bf16[8,16,1024]{2,1,0:T(8,128)(2,1)S(1)}, u32[]{:S(2)}, u32[]{:S(2)}) collective-permute-start(bf16[8,16,1024]{2,1,0:T(8,128)(2,1)} %get-tuple-element.85), channel_id=1, source_target_pairs={{0,12},{1,13},{2,14},{3,15},{4,0},{5,1},{6,2},{7,3},{8,4},{9,5},{1... | collective-permute-start | bytes 786440 | tf_op jit(solution)/shard_map/ppermute | solution.py:328
  84.2 3.9 %collective-permute-start.13 = (bf16[8,16,1024]{2,1,0:T(8,128)(2,1)}, bf16[8,16,1024]{2,1,0:T(8,128)(2,1)S(1)}, u32[]{:S(2)}, u32[]{:S(2)}) collective-permute-start(bf16[8,16,1024]{2,1,0:T(8,128)(2,1)} %get-tuple-element.87), channel_id=1, source_target_pairs={{0,14},{1,15},{2,12},{3,13},{4,2},{5,3},{6,0},{7,1},{8,6},{9,7},{1... | collective-permute-start | bytes 786440 | tf_op jit(solution)/shard_map/ppermute | solution.py:328
  88.1 1.6 %collective-permute-start.14 = (bf16[8,16,1024]{2,1,0:T(8,128)(2,1)}, bf16[8,16,1024]{2,1,0:T(8,128)(2,1)S(1)}, u32[]{:S(2)}, u32[]{:S(2)}) collective-permute-start(bf16[8,16,1024]{2,1,0:T(8,128)(2,1)} %get-tuple-element.88), channel_id=1, source_target_pairs={{0,15},{1,12},{2,13},{3,14},{4,3},{5,0},{6,1},{7,2},{8,7},{9,4},{1... | collective-permute-start | bytes 786440 | tf_op jit(solution)/shard_map/ppermute | solution.py:328
  90.9 4.3 %all-to-all-start.3 = ((bf16[16,8,1152]{2,1,0:T(8,128)(2,1)}), bf16[16,8,1152]{2,1,0:T(8,128)(2,1)S(1)}, u32[]{:S(2)}, u32[]{:S(2)}) async-start(bf16[16,8,1152]{2,1,0:T(8,128)(2,1)} %bitcast.9), calls=%async_computation.3 | async-start | bytes 589824 | tf_op jit(solution)/shard_map/all_to_all | solution.py:363
  95.2 8.4 %collective-permute-done.12.refs_13_ = bf16[8,16,1024]{2,1,0:T(8,128)(2,1)S(1)} collective-permute-done((bf16[8,16,1024]{2,1,0:T(8,128)(2,1)}, bf16[8,16,1024]{2,1,0:T(8,128)(2,1)S(1)}, u32[]{:S(2)}, u32[]{:S(2)}) %collective-permute-start.12) | collective-permute-done | bytes 262176 | tf_op jit(solution)/shard_map/ppermute | solution.py:328
  103.7 7.4 %collective-permute-done.13.refs_14_ = bf16[8,16,1024]{2,1,0:T(8,128)(2,1)S(1)} collective-permute-done((bf16[8,16,1024]{2,1,0:T(8,128)(2,1)}, bf16[8,16,1024]{2,1,0:T(8,128)(2,1)S(1)}, u32[]{:S(2)}, u32[]{:S(2)}) %collective-permute-start.13) | collective-permute-done | bytes 262176 | tf_op jit(solution)/shard_map/ppermute | solution.py:328
  111.1 1.6 %collective-permute-done.14.refs_15_ = bf16[8,16,1024]{2,1,0:T(8,128)(2,1)S(1)} collective-permute-done((bf16[8,16,1024]{2,1,0:T(8,128)(2,1)}, bf16[8,16,1024]{2,1,0:T(8,128)(2,1)S(1)}, u32[]{:S(2)}, u32[]{:S(2)}) %collective-permute-start.14) | collective-permute-done | bytes 262176 | tf_op jit(solution)/shard_map/ppermute | solution.py:328
  112.7 3.4 %place_rows.1 = bf16[128,16,1024]{2,1,0:T(8,128)(2,1)} custom-call(s32[16]{0:T(128)S(1)} %fusion.22.blocks, bf16[8,16,1024]{2,1,0:T(8,128)(2,1)S(1)} %copy-done, bf16[8,16,1024]{2,1,0:T(8,128)(2,1)S(1)} %collective-permute-done.refs_1_, bf16[8,16,1024]{2,1,0:T(8,128)(2,1)S(1)} %collective-permute-done.1.refs_2_, ...), custom_call_target="tpu_custom_call" | custom-call | flops 1000000000 | bytes 8388608 | tf_op jit(solution)/shard_map/place_rows/pallas_call | solution.py:128
  116.1 1.5 %all-to-all-done.3 = bf16[16,8,1152]{2,1,0:T(8,128)(2,1)S(1)} async-done(((bf16[16,8,1152]{2,1,0:T(8,128)(2,1)}), bf16[16,8,1152]{2,1,0:T(8,128)(2,1)S(1)}, u32[]{:S(2)}, u32[]{:S(2)}) %all-to-all-start.3) | async-done | bytes 294944 | tf_op jit(solution)/shard_map/all_to_all | solution.py:363
  (72 shorter events, 10.8 us)
Async XLA Ops:
  6.0 46.0 %all-to-all-start.1 = ((bf16[8,128,1024]{2,1,0:T(8,128)(2,1)}), bf16[8,128,1024]{2,1,0:T(8,128)(2,1)}, u32[]{:S(2)}, u32[]{:S(2)}) async-start(bf16[8,128,1024]{2,1,0:T(8,128)(2,1)} %pack_rows.3), calls=%async_computation.1 | async-start | bytes 4194304 | tf_op jit(solution)/shard_map/all_to_all | solution.py:309
  12.1 12.9 %copy-start.11 = (s32[128]{0:T(128)S(1)}, s32[128]{0:T(128)}, u32[]{:S(2)}) copy-start(s32[128]{0:T(128)} %param.17) | copy-start | bytes 1540
  12.1 13.0 %copy-start.7 = (f32[2048]{0:T(1024)S(1)}, f32[2048]{0:T(1024)}, u32[]{:S(2)}) copy-start(f32[2048]{0:T(1024)} %param.13) | copy-start | bytes 24580
  12.2 13.0 %copy-start.10 = (f32[512]{0:T(512)S(1)}, f32[512]{0:T(512)}, u32[]{:S(2)}) copy-start(f32[512]{0:T(512)} %param.14) | copy-start | bytes 6148
  15.6 10.8 %collective-permute-start = (bf16[8,16,1024]{2,1,0:T(8,128)(2,1)}, bf16[8,16,1024]{2,1,0:T(8,128)(2,1)S(1)}, u32[]{:S(2)}, u32[]{:S(2)}) collective-permute-start(bf16[8,16,1024]{2,1,0:T(8,128)(2,1)} %get-tuple-element.74), channel_id=1, source_target_pairs={{0,1},{1,2},{2,3},{3,0},{4,5},{5,6},{6,7},{7,4},{8,9},{9,10},{10,1... | collective-permute-start | bytes 786440 | tf_op jit(solution)/shard_map/ppermute | solution.py:328
  17.3 23.9 %collective-permute-start.1 = (bf16[8,16,1024]{2,1,0:T(8,128)(2,1)}, bf16[8,16,1024]{2,1,0:T(8,128)(2,1)S(1)}, u32[]{:S(2)}, u32[]{:S(2)}) collective-permute-start(bf16[8,16,1024]{2,1,0:T(8,128)(2,1)} %get-tuple-element.75), channel_id=1, source_target_pairs={{0,2},{1,3},{2,0},{3,1},{4,6},{5,7},{6,4},{7,5},{8,10},{9,11},{10,... | collective-permute-start | bytes 786440 | tf_op jit(solution)/shard_map/ppermute | solution.py:328
  20.6 20.6 %collective-permute-start.2 = (bf16[8,16,1024]{2,1,0:T(8,128)(2,1)}, bf16[8,16,1024]{2,1,0:T(8,128)(2,1)S(1)}, u32[]{:S(2)}, u32[]{:S(2)}) collective-permute-start(bf16[8,16,1024]{2,1,0:T(8,128)(2,1)} %get-tuple-element.76), channel_id=1, source_target_pairs={{0,3},{1,0},{2,1},{3,2},{4,7},{5,4},{6,5},{7,6},{8,11},{9,8},{10,9... | collective-permute-start | bytes 786440 | tf_op jit(solution)/shard_map/ppermute | solution.py:328
  21.3 22.7 %collective-permute-start.3 = (bf16[8,16,1024]{2,1,0:T(8,128)(2,1)}, bf16[8,16,1024]{2,1,0:T(8,128)(2,1)S(1)}, u32[]{:S(2)}, u32[]{:S(2)}) collective-permute-start(bf16[8,16,1024]{2,1,0:T(8,128)(2,1)} %get-tuple-element.77), channel_id=1, source_target_pairs={{0,4},{1,5},{2,6},{3,7},{4,8},{5,9},{6,10},{7,11},{8,12},{9,13},{1... | collective-permute-start | bytes 786440 | tf_op jit(solution)/shard_map/ppermute | solution.py:328
  22.5 27.3 %collective-permute-start.4 = (bf16[8,16,1024]{2,1,0:T(8,128)(2,1)}, bf16[8,16,1024]{2,1,0:T(8,128)(2,1)S(1)}, u32[]{:S(2)}, u32[]{:S(2)}) collective-permute-start(bf16[8,16,1024]{2,1,0:T(8,128)(2,1)} %get-tuple-element.78), channel_id=1, source_target_pairs={{0,5},{1,6},{2,7},{3,4},{4,9},{5,10},{6,11},{7,8},{8,13},{9,14},{1... | collective-permute-start | bytes 786440 | tf_op jit(solution)/shard_map/ppermute | solution.py:328
  26.4 53.7 %collective-permute-start.5 = (bf16[8,16,1024]{2,1,0:T(8,128)(2,1)}, bf16[8,16,1024]{2,1,0:T(8,128)(2,1)}, u32[]{:S(2)}, u32[]{:S(2)}) collective-permute-start(bf16[8,16,1024]{2,1,0:T(8,128)(2,1)} %get-tuple-element.79), channel_id=1, source_target_pairs={{0,6},{1,7},{2,4},{3,5},{4,10},{5,11},{6,8},{7,9},{8,14},{9,15},{1... | collective-permute-start | bytes 786440 | tf_op jit(solution)/shard_map/ppermute | solution.py:328
  41.2 40.7 %collective-permute-start.6 = (bf16[8,16,1024]{2,1,0:T(8,128)(2,1)}, bf16[8,16,1024]{2,1,0:T(8,128)(2,1)}, u32[]{:S(2)}, u32[]{:S(2)}) collective-permute-start(bf16[8,16,1024]{2,1,0:T(8,128)(2,1)} %get-tuple-element.80), channel_id=1, source_target_pairs={{0,7},{1,4},{2,5},{3,6},{4,11},{5,8},{6,9},{7,10},{8,15},{9,12},{1... | collective-permute-start | bytes 786440 | tf_op jit(solution)/shard_map/ppermute | solution.py:328
  41.2 42.8 %collective-permute-start.7 = (bf16[8,16,1024]{2,1,0:T(8,128)(2,1)}, bf16[8,16,1024]{2,1,0:T(8,128)(2,1)}, u32[]{:S(2)}, u32[]{:S(2)}) collective-permute-start(bf16[8,16,1024]{2,1,0:T(8,128)(2,1)} %get-tuple-element.81), channel_id=1, source_target_pairs={{0,8},{1,9},{2,10},{3,11},{4,12},{5,13},{6,14},{7,15},{8,0},{9,1},... | collective-permute-start | bytes 786440 | tf_op jit(solution)/shard_map/ppermute | solution.py:328
  44.7 39.5 %collective-permute-start.8 = (bf16[8,16,1024]{2,1,0:T(8,128)(2,1)}, bf16[8,16,1024]{2,1,0:T(8,128)(2,1)}, u32[]{:S(2)}, u32[]{:S(2)}) collective-permute-start(bf16[8,16,1024]{2,1,0:T(8,128)(2,1)} %get-tuple-element.82), channel_id=1, source_target_pairs={{0,9},{1,10},{2,11},{3,8},{4,13},{5,14},{6,15},{7,12},{8,1},{9,2},... | collective-permute-start | bytes 786440 | tf_op jit(solution)/shard_map/ppermute | solution.py:328
  50.5 37.6 %collective-permute-start.9 = (bf16[8,16,1024]{2,1,0:T(8,128)(2,1)}, bf16[8,16,1024]{2,1,0:T(8,128)(2,1)}, u32[]{:S(2)}, u32[]{:S(2)}) collective-permute-start(bf16[8,16,1024]{2,1,0:T(8,128)(2,1)} %get-tuple-element.83), channel_id=1, source_target_pairs={{0,10},{1,11},{2,8},{3,9},{4,14},{5,15},{6,12},{7,13},{8,2},{9,3},... | collective-permute-start | bytes 786440 | tf_op jit(solution)/shard_map/ppermute | solution.py:328
  73.8 38.9 %copy-start = (bf16[8,16,1024]{2,1,0:T(8,128)(2,1)S(1)}, bf16[8,16,1024]{2,1,0:T(8,128)(2,1)}, u32[]{:S(2)}) copy-start(bf16[8,16,1024]{2,1,0:T(8,128)(2,1)} %get-tuple-element.73.refs_0_) | copy-start | bytes 786436
  73.8 38.9 %copy-start.2 = (bf16[8,16,1024]{2,1,0:T(8,128)(2,1)S(1)}, bf16[8,16,1024]{2,1,0:T(8,128)(2,1)}, u32[]{:S(2)}) copy-start(bf16[8,16,1024]{2,1,0:T(8,128)(2,1)} %copy-done.1) | copy-start | bytes 786436
  73.8 38.9 %copy-start.4 = (bf16[8,16,1024]{2,1,0:T(8,128)(2,1)S(1)}, bf16[8,16,1024]{2,1,0:T(8,128)(2,1)}, u32[]{:S(2)}) copy-start(bf16[8,16,1024]{2,1,0:T(8,128)(2,1)} %copy-done.3) | copy-start | bytes 786436
  73.8 16.1 %all-to-all-start.2 = ((bf16[8,2,16,512]{3,2,1,0:T(8,128)(2,1)}), bf16[8,2,16,512]{3,2,1,0:T(8,128)(2,1)S(1)}, u32[]{:S(2)}, u32[]{:S(2)}) async-start(bf16[8,2,16,512]{3,2,1,0:T(8,128)(2,1)} %get-tuple-element.132), calls=%async_computation.2 | async-start | bytes 524288 | tf_op jit(solution)/shard_map/all_to_all | solution.py:359
  80.1 15.2 %collective-permute-start.10 = (bf16[8,16,1024]{2,1,0:T(8,128)(2,1)}, bf16[8,16,1024]{2,1,0:T(8,128)(2,1)S(1)}, u32[]{:S(2)}, u32[]{:S(2)}) collective-permute-start(bf16[8,16,1024]{2,1,0:T(8,128)(2,1)} %get-tuple-element.84), channel_id=1, source_target_pairs={{0,11},{1,8},{2,9},{3,10},{4,15},{5,12},{6,13},{7,14},{8,3},{9,0},... | collective-permute-start | bytes 786440 | tf_op jit(solution)/shard_map/ppermute | solution.py:328
  81.9 13.3 %collective-permute-start.11 = (bf16[8,16,1024]{2,1,0:T(8,128)(2,1)}, bf16[8,16,1024]{2,1,0:T(8,128)(2,1)S(1)}, u32[]{:S(2)}, u32[]{:S(2)}) collective-permute-start(bf16[8,16,1024]{2,1,0:T(8,128)(2,1)} %get-tuple-element.85), channel_id=1, source_target_pairs={{0,12},{1,13},{2,14},{3,15},{4,0},{5,1},{6,2},{7,3},{8,4},{9,5},{1... | collective-permute-start | bytes 786440 | tf_op jit(solution)/shard_map/ppermute | solution.py:328
  84.0 19.6 %collective-permute-start.12 = (bf16[8,16,1024]{2,1,0:T(8,128)(2,1)}, bf16[8,16,1024]{2,1,0:T(8,128)(2,1)S(1)}, u32[]{:S(2)}, u32[]{:S(2)}) collective-permute-start(bf16[8,16,1024]{2,1,0:T(8,128)(2,1)} %get-tuple-element.86), channel_id=1, source_target_pairs={{0,13},{1,14},{2,15},{3,12},{4,1},{5,2},{6,3},{7,0},{8,5},{9,6},{1... | collective-permute-start | bytes 786440 | tf_op jit(solution)/shard_map/ppermute | solution.py:328
  84.2 26.9 %collective-permute-start.13 = (bf16[8,16,1024]{2,1,0:T(8,128)(2,1)}, bf16[8,16,1024]{2,1,0:T(8,128)(2,1)S(1)}, u32[]{:S(2)}, u32[]{:S(2)}) collective-permute-start(bf16[8,16,1024]{2,1,0:T(8,128)(2,1)} %get-tuple-element.87), channel_id=1, source_target_pairs={{0,14},{1,15},{2,12},{3,13},{4,2},{5,3},{6,0},{7,1},{8,6},{9,7},{1... | collective-permute-start | bytes 786440 | tf_op jit(solution)/shard_map/ppermute | solution.py:328
  88.1 24.5 %collective-permute-start.14 = (bf16[8,16,1024]{2,1,0:T(8,128)(2,1)}, bf16[8,16,1024]{2,1,0:T(8,128)(2,1)S(1)}, u32[]{:S(2)}, u32[]{:S(2)}) collective-permute-start(bf16[8,16,1024]{2,1,0:T(8,128)(2,1)} %get-tuple-element.88), channel_id=1, source_target_pairs={{0,15},{1,12},{2,13},{3,14},{4,3},{5,0},{6,1},{7,2},{8,7},{9,4},{1... | collective-permute-start | bytes 786440 | tf_op jit(solution)/shard_map/ppermute | solution.py:328
  90.9 26.7 %all-to-all-start.3 = ((bf16[16,8,1152]{2,1,0:T(8,128)(2,1)}), bf16[16,8,1152]{2,1,0:T(8,128)(2,1)S(1)}, u32[]{:S(2)}, u32[]{:S(2)}) async-start(bf16[16,8,1152]{2,1,0:T(8,128)(2,1)} %bitcast.9), calls=%async_computation.3 | async-start | bytes 589824 | tf_op jit(solution)/shard_map/all_to_all | solution.py:363
  (3 other events, 8.1 us)

commit v4 on v3

v4 whole, which is shorter than its diff:
```python
import functools

import jax
import jax.numpy as jnp
from jax import lax
from jax.experimental import pallas as pl
from jax.experimental.pallas import tpu as pltpu
from jax.sharding import Mesh
from jax.sharding import PartitionSpec as P

STEPS = 128
BURN = 40
UNROLL = 80
ROOM = 128
EP = ("ep_0", "ep_1")
IMPORTANCE = 0.6
MIB = 1024 * 1024
SMEM = pl.BlockSpec(memory_space=pltpu.SMEM)
VMEM = pl.BlockSpec(memory_space=pltpu.VMEM)
HBM = pl.BlockSpec(memory_space=pltpu.HBM)


def sigmoid(x):
    return 0.5 * jnp.tanh(0.5 * x) + 0.5


def iota(shape, dim):
    return lax.broadcasted_iota(jnp.int32, shape, dim)


def one_hot(hit):
    return jnp.where(hit, 1.0, 0.0).astype(jnp.bfloat16)


def f32_dot(a, b):
    return jnp.dot(a, b, preferred_element_type=jnp.float32)


def pack_kernel(base, place, ids, starts_ref, obs, out, crowded, rows_of, packed, sem):
    shards, count = starts_ref.shape
    shard_steps = obs.shape[1]
    lanes = count * shard_steps
    spread = one_hot(iota((count, lanes), 1) // shard_steps == iota((count, lanes), 0))
    starts = f32_dot(starts_ref[...].astype(jnp.bfloat16), spread).astype(jnp.int32)
    step = place[0] * shard_steps + iota((shards, lanes), 1) % shard_steps
    within = ((step - starts) & (STEPS - 1)) < BURN
    before = one_hot(iota((lanes, lanes), 0) < iota((lanes, lanes), 1))
    slot = f32_dot(one_hot(within), before).astype(jnp.int32) - base
    slot = jnp.where(within, slot, -1)
    for k in range(shards):
        for i in range(count):
            rows_of[k, i * shard_steps : (i + 1) * shard_steps, :] = obs[ids[k, i]]
        hot = one_hot(iota((ROOM, lanes), 0) == slot[k : k + 1, :])
        packed[k] = f32_dot(hot, rows_of[k]).astype(jnp.bfloat16)
        pltpu.make_async_copy(packed.at[k], out.at[k], sem.at[k]).start()
    most = jnp.zeros((shards, lanes // 2), jnp.float32)
    for shard in range(shards):
        held = ((step + (shard * shard_steps) - starts) & (STEPS - 1)) < BURN
        some = jnp.where(held, 1.0, 0.0)
        most = jnp.maximum(most, f32_dot(some.astype(jnp.bfloat16), jnp.ones((lanes, lanes // 2), jnp.bfloat16)))
    crowded[0] = (jnp.max(most) > ROOM).astype(jnp.int32)
    for k in range(shards):
        pltpu.make_async_copy(packed.at[k], out.at[k], sem.at[k]).wait()


def pack(base, place, ids, starts, observations):
    shards, count = ids.shape
    _, shard_steps, width = observations.shape
    return pl.pallas_call(
        functools.partial(pack_kernel, base),
        out_shape=(
            jax.ShapeDtypeStruct((shards, ROOM, width), jnp.bfloat16),
            jax.ShapeDtypeStruct((1,), jnp.int32),
        ),
        in_specs=[SMEM, SMEM, VMEM, VMEM],
        out_specs=(HBM, SMEM),
        scratch_shapes=[
            pltpu.VMEM((shards, count * shard_steps, width), jnp.bfloat16),
            pltpu.VMEM((shards, ROOM, width), jnp.bfloat16),
            pltpu.SemaphoreType.DMA((shards,)),
        ],
        compiler_params=pltpu.CompilerParams(vmem_limit_bytes=24 * MIB),
        cost_estimate=pl.CostEstimate(flops=10**9, bytes_accessed=4 * MIB, transcendentals=0),
        name="pack_rows",
    )(place, ids, starts, observations)


def block_at(here, grid, n, sign):
    along, across = grid
    first = lax.rem(here[1] + (along + sign * (n // across)), along)
    return first * across + lax.rem(here[2] + (across + sign * (n % across)), across)


def masked_kernel(grid, place, ids, starts, obs, *refs):
    outs, (held, sem) = refs[:-2], refs[-2:]
    count, shard_steps, width = outs[0].shape
    step = place[0] * shard_steps + iota((shard_steps, width), 0)
    copies = [pltpu.make_async_copy(held.at[n], out, sem.at[n]) for n, out in enumerate(outs)]
    for n in range(len(outs)):
        block = block_at(place, grid, n, 1)
        for i in range(count):
            g = block * count + i
            keep = ((step - starts[g] - BURN) & (STEPS - 1)) < UNROLL
            held[n, i] = jnp.where(keep, obs[ids[g]], jnp.zeros((), jnp.bfloat16))
        copies[n].start()
    for copy in copies:
        copy.wait()


def masked(grid, place, ids, starts, observations):
    _, shard_steps, width = observations.shape
    learners = grid[0] * grid[1]
    block = (ids.shape[0] // learners, shard_steps, width)
    return pl.pallas_call(
        functools.partial(masked_kernel, grid),
        out_shape=[jax.ShapeDtypeStruct(block, jnp.bfloat16)] * learners,
        in_specs=[SMEM, SMEM, SMEM, VMEM],
        out_specs=[HBM] * learners,
        scratch_shapes=[
            pltpu.VMEM((learners, *block), jnp.bfloat16),
            pltpu.SemaphoreType.DMA((learners,)),
        ],
        compiler_params=pltpu.CompilerParams(vmem_limit_bytes=60 * MIB),
        cost_estimate=pl.CostEstimate(flops=10**8, bytes_accessed=6 * MIB, transcendentals=0),
        name="masked_rows",
    )(place, ids, starts, observations)


def place_kernel(grid, sources, place, *refs):
    rows, (out, sem) = refs[: len(sources)], refs[-2:]
    count = rows[0].shape[0]
    copies = [
        pltpu.make_async_copy(
            block, out.at[pl.ds(block_at(place, grid, n, -1) * count, count)], sem.at[m]
        )
        for m, (n, block) in enumerate(zip(sources, rows))
    ]
    for copy in copies:
        copy.start()
    for copy in copies:
        copy.wait()


def placed(grid, sources, place, rows):
    count, shard_steps, width = rows[0].shape
    return pl.pallas_call(
        functools.partial(place_kernel, grid, sources),
        out_shape=jax.ShapeDtypeStruct((grid[0] * grid[1] * count, shard_steps, width), jnp.bfloat16),
        in_specs=[SMEM] + [VMEM] * len(rows),
        out_specs=HBM,
        scratch_shapes=[pltpu.SemaphoreType.DMA((len(rows),))],
        compiler_params=pltpu.CompilerParams(vmem_limit_bytes=8 * MIB),
        cost_estimate=pl.CostEstimate(flops=10**9, bytes_accessed=8 * MIB, transcendentals=0),
        name="place_rows",
    )(place, *rows)


def burn_in_kernel(
    place, crowded, rows_hbm, more_hbm, win_hbm, wh_hbm, bias_ref, starts_ref, out_ref, xs, hot, x, proj, win, wh, pair, sem, out_sem
):
    copies, _, count, hidden_width = out_ref.shape
    shards = starts_ref.shape[0]
    shard_steps = STEPS // shards
    rows_copy = pltpu.make_async_copy(rows_hbm, xs, sem.at[0])
    rows_copy.start()
    win_copy = pltpu.make_async_copy(win_hbm, win, sem.at[2])
    wh_copy = pltpu.make_async_copy(wh_hbm, wh, sem.at[3])
    win_copy.start()
    wh_copy.start()

    mine = jnp.where(iota((shards, count), 0) == place[0], starts_ref[...], 0).astype(jnp.float32)
    mine = jnp.sum(mine, axis=0, keepdims=True)
    diagonal = iota((count, count), 0) == iota((count, count), 1)
    own = jnp.sum(jnp.where(diagonal, mine, 0.0), axis=1, keepdims=True).astype(jnp.int32)
    lane = iota((count, 128), 1)
    first = ((lane - own // shard_steps) & (shards - 1)) * shard_steps - own % shard_steps
    begin = jnp.maximum(first, 0)
    held = jnp.clip(jnp.minimum(first + shard_steps, BURN) - begin, 0, shard_steps)
    earlier = one_hot(iota((count, count), 1) < iota((count, count), 0))
    ahead = f32_dot(earlier, held.astype(jnp.float32).astype(jnp.bfloat16)).astype(jnp.int32)
    slot = iota((count, ROOM), 1)

    def select(base):
        for shard in range(shards):
            at = slice(shard, shard + 1)
            order = slot + base - ahead[:, at]
            step = jnp.where((order >= 0) & (order < held[:, at]), order + begin[:, at], -1)
            for t in range(BURN):
                hot[t * count : (t + 1) * count, shard * ROOM : (shard + 1) * ROOM] = one_hot(step == t)

    select(0)
    rows_copy.wait()
    x[...] = f32_dot(hot[...], xs[...]).astype(jnp.bfloat16)

    @pl.when(crowded[0] > 0)
    def _():
        more_copy = pltpu.make_async_copy(more_hbm, xs, sem.at[1])
        more_copy.start()
        select(ROOM)
        more_copy.wait()
        x[...] += f32_dot(hot[...], xs[...]).astype(jnp.bfloat16)

    win_copy.wait()
    proj[...] = f32_dot(x[...], win[...]) + bias_ref[...]
    wh_copy.wait()
    half = hidden_width // 2

    def step(t, state_pair):
        hiddens, cells = state_pair
        row = pl.ds(pl.multiple_of(t * count, count), count)
        blocks = [[pl.ds(gate * hidden_width + q * half, half) for gate in range(4)] for q in range(2)]
        sums = [[proj[row, block] for block in part] for part in blocks]
        for k in range(2):
            for q in range(2):
                for gate in range(4):
                    weight = wh[k * half : (k + 1) * half, blocks[q][gate]]
                    sums[q][gate] = sums[q][gate] + f32_dot(hiddens[k], weight)
        new_hiddens, new_cells = [], []
        for (ingate, forget, candidate, outgate), cell_state in zip(sums, cells):
            cell_state = sigmoid(forget) * cell_state + sigmoid(ingate) * jnp.tanh(candidate)
            new_cells.append(cell_state)
            new_hiddens.append((sigmoid(outgate) * jnp.tanh(cell_state)).astype(jnp.bfloat16))
        return (tuple(new_hiddens), tuple(new_cells))

    blank = ((jnp.zeros((count, half), jnp.bfloat16),) * 2, (jnp.zeros((count, half), jnp.float32),) * 2)
    hiddens, cells = lax.fori_loop(0, BURN, step, blank, unroll=8)
    pair[0] = jnp.concatenate(hiddens, axis=1)
    pair[1] = jnp.concatenate(cells, axis=1).astype(jnp.bfloat16)
    out_copies = [pltpu.make_async_copy(pair, out_ref.at[n], out_sem.at[n]) for n in range(copies)]
    for copy in out_copies:
        copy.start()
    for copy in out_copies:
        copy.wait()


def burn_in(place, crowded, rows, more, input_weight, hidden_weight, bias, starts):
    shards, count = starts.shape
    width = input_weight.shape[0]
    hidden_width = hidden_weight.shape[0]
    total = BURN * count
    return pl.pallas_call(
        burn_in_kernel,
        out_shape=jax.ShapeDtypeStruct((shards, 2, count, hidden_width), jnp.bfloat16),
        in_specs=[SMEM, SMEM, HBM, HBM, HBM, HBM, VMEM, VMEM],
        out_specs=HBM,
        scratch_shapes=[
            pltpu.VMEM((shards * ROOM, width), jnp.bfloat16),
            pltpu.VMEM((total, shards * ROOM), jnp.bfloat16),
            pltpu.VMEM((total, width), jnp.bfloat16),
            pltpu.VMEM((total, 4 * hidden_width), jnp.float32),
            pltpu.VMEM(input_weight.shape, jnp.bfloat16),
            pltpu.VMEM(hidden_weight.shape, jnp.bfloat16),
            pltpu.VMEM((2, count, hidden_width), jnp.bfloat16),
            pltpu.SemaphoreType.DMA((4,)),
            pltpu.SemaphoreType.DMA((shards,)),
        ],
        compiler_params=pltpu.CompilerParams(vmem_limit_bytes=58 * MIB),
        cost_estimate=pl.CostEstimate(
            flops=30_000_000_000, bytes_accessed=8 * MIB, transcendentals=0
        ),
        name="burn_in",
    )(place, crowded, rows, more, input_weight, hidden_weight, bias, starts)


def unwritten_kernel(out):
    del out


def unwritten(shape, dtype):
    return pl.pallas_call(
        unwritten_kernel,
        out_shape=jax.ShapeDtypeStruct(shape, dtype),
        out_specs=HBM,
        compiler_params=pltpu.CompilerParams(vmem_limit_bytes=60 * MIB),
        name="unwritten",
    )()


def order_kernel(pairs, rank, raw, out):
    shards, _, count, hidden_width = pairs.shape
    total = shards * count
    column = iota((total, total), 1)
    diagonal = column == iota((total, total), 0)
    rank_of = jnp.sum(jnp.where(diagonal, rank[...].astype(jnp.float32), 0.0), axis=1, keepdims=True)
    raw_of = jnp.sum(jnp.where(diagonal, raw[...], 0.0), axis=1, keepdims=True)
    hot = one_hot((column % count) * shards + column // count == rank_of.astype(jnp.int32))
    for n in range(2):
        state = pairs[:, n].reshape(total, hidden_width)
        out[:, n * hidden_width : (n + 1) * hidden_width] = f32_dot(hot, state).astype(jnp.bfloat16)
    lane = iota((total, 128), 1)
    tail = jnp.where(lane == 0, raw_of, jnp.where(lane == 1, jnp.max(raw_of), 0.0))
    out[:, 2 * hidden_width :] = tail.astype(jnp.bfloat16)


def ordered(pairs, rank, raw):
    total = rank.shape[1]
    return pl.pallas_call(
        order_kernel,
        out_shape=jax.ShapeDtypeStruct((total, 2 * pairs.shape[3] + 128), jnp.bfloat16),
        in_specs=[VMEM] * 3,
        out_specs=VMEM,
        compiler_params=pltpu.CompilerParams(vmem_limit_bytes=8 * MIB),
        cost_estimate=pl.CostEstimate(flops=10**8, bytes_accessed=MIB, transcendentals=0),
        name="learner_order",
    )(pairs, rank, raw)


def weights_kernel(received, out):
    total = received.shape[0]
    raw = received[...].astype(jnp.float32)
    lane = iota(raw.shape, 1)
    peak = jnp.max(jnp.where(lane == 1, raw, 0.0))
    weight = jnp.sum(jnp.where(lane == 0, raw, 0.0), axis=1, keepdims=True) / peak
    weight = jnp.where(iota((total, total), 0) == iota((total, total), 1), weight, 0.0)
    out[...] = jnp.sum(weight, axis=0, keepdims=True).astype(jnp.bfloat16)


def normalized(received):
    total, lanes = received.shape
    return pl.pallas_call(
        weights_kernel,
        grid=(1,),
        out_shape=jax.ShapeDtypeStruct((1, total), jnp.bfloat16),
        in_specs=[pl.BlockSpec((total, 128), lambda n: (0, lanes // 128 - 1))],
        out_specs=pl.BlockSpec((1, total), lambda n: (0, 0)),
        compiler_params=pltpu.CompilerParams(vmem_limit_bytes=4 * MIB),
        name="weights",
    )(received)[0]


def body(
    observations,
    input_weight,
    hidden_weight,
    gate_bias,
    forget_bias,
    episode_ids,
    start_steps,
    priorities,
):
    _, width = observations.shape[1:]
    seq_count = episode_ids.shape[0]
    hidden_width = hidden_weight.shape[0]
    shards = lax.axis_size("tm")
    learners = lax.axis_size(EP)
    place = jnp.stack([lax.axis_index(axis) for axis in ("tm", *EP)]).astype(jnp.int32)
    own_count = seq_count // shards
    per_learner = seq_count // learners

    index = jnp.arange(seq_count, dtype=jnp.int32)
    key = start_steps * seq_count + index
    rank = jnp.sum((key[None, :] < key[:, None]).astype(jnp.int32), axis=1)
    turn = jnp.arange(shards, dtype=jnp.int32)
    dealt = jnp.arange(own_count, dtype=jnp.int32)[None, :] * shards + turn[:, None]
    chosen = rank[None, None, :] == dealt[:, :, None]
    ids = jnp.sum(jnp.where(chosen, episode_ids, 0), axis=2)
    starts = jnp.sum(jnp.where(chosen, start_steps, 0), axis=2)

    def exchanged(base):
        sent, crowded = pack(base, place, ids, starts, observations)
        rows = lax.all_to_all(sent, "tm", split_axis=0, concat_axis=0, tiled=True)
        return rows.reshape(shards * ROOM, width), crowded

    grid = along, across = tuple(lax.axis_size(axis) for axis in EP)

    def hops(n):
        dx, dz = n // across, n % across
        return min(dx, along - dx) + min(dz, across - dz)

    late = [n for n in range(1, learners) if hops(n) == 1]
    order = sorted((n for n in range(1, learners) if n not in late), key=lambda n: (-hops(n), n)) + late
    rows_in, crowded = exchanged(0)
    sent_rows = masked(grid, place, episode_ids, start_steps, observations)
    moved_rows = [sent_rows[0]]
    for n in order:
        ring = [
            (i, (i // across + n // across) % along * across + (i + n) % across)
            for i in range(learners)
        ]
        moved_rows.append(lax.ppermute(sent_rows[n], EP, ring))

    blank = jnp.zeros((hidden_width,), jnp.float32)
    bias = (gate_bias + jnp.concatenate([blank, forget_bias, blank, blank]))[None, :]

    raw_weight = jnp.exp(-IMPORTANCE * jnp.log(priorities.astype(jnp.float32))).astype(jnp.bfloat16)
    raw_row = raw_weight.astype(jnp.float32)[None, :]
    bias, rank_row, raw_row = lax.optimization_barrier((bias, rank[None, :], raw_row))

    rows_in, again = lax.optimization_barrier((rows_in, crowded))
    more = lax.cond(
        again[0] > 0,
        lambda: exchanged(ROOM)[0],
        lambda: unwritten(rows_in.shape, rows_in.dtype),
    )
    pairs = burn_in(place, crowded, rows_in, more, input_weight, hidden_weight, bias, starts)
    pairs = lax.all_to_all(pairs, "tm", split_axis=0, concat_axis=0, tiled=True)
    rows = placed(grid, [0] + order, place, moved_rows)
    both = ordered(pairs, rank_row, raw_row)
    both = both.reshape(learners, per_learner, both.shape[1])
    both = lax.all_to_all(both, EP, split_axis=0, concat_axis=0, tiled=True)
    start_state = both[:, :, : 2 * hidden_width].reshape(seq_count, 2, hidden_width)
    weights = normalized(both.reshape(seq_count, both.shape[2]))
    return (rows, start_state, weights)


def solution(mesh):
    torus = Mesh(mesh.devices.reshape(mesh.shape["tm"], 4, 4), ("tm", "ep_0", "ep_1"))
    return jax.shard_map(
        body,
        mesh=torus,
        in_specs=(P(EP, "tm", None), P(), P(), P(), P(), P(EP), P(EP), P(EP)),
        out_specs=(P(EP, "tm", None), P(EP, None, None), P(EP)),
        check_vma=False,
    )
```

time: 121 us -> 113 us (0.934)
  waiting for transfers between devices: 32.6 us -> 24.6 us
  starting transfers between devices: 45.2 us -> 47.4 us
    ppermute x15, waiting for transfers between devices: 31.1 us -> 15.1 us  [body(): moved_rows.append(lax.ppermute(sent_rows[n], EP, ring))]
    all_to_all x1, waiting for transfers between devices: 0.01 us -> 7.53 us  [exchanged(): rows = lax.all_to_all(sent, 'tm', split_axis=0, concat_axis=0, tiled=True)]
    ppermute x15, starting transfers between devices: 28.5 us -> 31.6 us  [body(): moved_rows.append(lax.ppermute(sent_rows[n], EP, ring))]
    all_to_all x1, starting transfers between devices: 6.27 us -> 4.54 us  [body(): pairs = lax.all_to_all(pairs, 'tm', split_axis=0, concat_axis=0, tiled=True)]
    pallas_call x4 -> x5, Pallas kernels: 30.9 us -> 31.2 us  [the longest x1 20.9 us: burn_in(): pl.pallas_call(burn_in_kernel, out_shape=jax.ShapeDtypeStruct((shards, 2,...]
  transfers between devices with their start and end apart: 18 -> 18, of which waited for: 6 -> 6; matrix products, arithmetic and copies ran while one was open for 2% -> 1% of each run, Pallas kernels for 24% -> 25%
where the time goes in v4:
time: 113 us; the launch traced here: 111 us
  starting transfers between devices  47.4 us (42%)
  Pallas kernels  32.9 us (29%)
  waiting for transfers between devices  24.6 us (22%)
  other arithmetic  2.61 us (2%)
  local copies, waits for them, and re-layouts  2.24 us (2%)
  between operations  1.49 us (1%)
    ppermute x15, starting transfers between devices, body(): moved_rows.append(lax.ppermute(sent_rows[n], EP, ring))  31.6 us
    pallas_call x1, Pallas kernels, burn_in(): pl.pallas_call(burn_in_kernel, out_shape=jax.ShapeDtypeStruct((shards, 2,...  20.9 us
    ppermute x15, waiting for transfers between devices, body(): moved_rows.append(lax.ppermute(sent_rows[n], EP, ring))  15.1 us
    all_to_all x1, waiting for transfers between devices, exchanged(): rows = lax.all_to_all(sent, 'tm', split_axis=0, concat_axis=0, tiled=True)  7.53 us
    all_to_all x1, starting transfers between devices, exchanged(): rows = lax.all_to_all(sent, 'tm', split_axis=0, concat_axis=0, tiled=True)  6.1 us
    all_to_all x1, starting transfers between devices, body(): both = lax.all_to_all(both, EP, split_axis=0, concat_axis=0, tiled=True)  5.19 us
    all_to_all x1, starting transfers between devices, body(): pairs = lax.all_to_all(pairs, 'tm', split_axis=0, concat_axis=0, tiled=True)  4.54 us
    pallas_call x1, Pallas kernels, pack(): pl.pallas_call(functools.partial(pack_kernel, base), out_shape=(jax.Shape...  3.95 us
  transfers between devices with their start and end apart: 18, of which 6 were waited for; matrix products, arithmetic and copies ran while one was open for 1% of the time, Pallas kernels for 25%

profile of v4, /device:TPU:1, one launch (start us, length us, event | category | flops | bytes accessed | tf_op | source)
XLA Modules:
  0.0 111.3 jit_solution(8817445972337045063)
XLA Ops:
  1.6 1.1 fusion.1
  2.7 4.0 %pack_rows.3 = (bf16[8,128,1024]{2,1,0:T(8,128)(2,1)}, s32[1]{0:T(128)}) custom-call(s32[3]{0:T(128)S(1)} %pad_add_fusion.place, s32[8,16]{1,0:T(8,128)S(1)} %get-tuple-element.66.ids, s32[8,16]{1,0:T(8,128)S(1)} %get-tuple-element.65.starts_ref, bf16[64,16,1024]{2,1,0:T(8,128)(2,1)} %obs.3), custom_call_target="tpu_custom_call" | custom-call | flops 1000000000 | bytes 4194304 | tf_op jit(solution)/shard_map/pack_rows/pallas_call | solution.py:69
  6.6 6.1 %all-to-all-start.1 = ((bf16[8,128,1024]{2,1,0:T(8,128)(2,1)}), bf16[8,128,1024]{2,1,0:T(8,128)(2,1)}, u32[]{:S(2)}, u32[]{:S(2)}) async-start(bf16[8,128,1024]{2,1,0:T(8,128)(2,1)} %get-tuple-element.59), calls=%async_computation.1 | async-start | bytes 4194304 | tf_op jit(solution)/shard_map/all_to_all | solution.py:361
  12.8 3.0 %masked_rows.1 = (bf16[8,16,1024]{2,1,0:T(8,128)(2,1)}, bf16[8,16,1024]{2,1,0:T(8,128)(2,1)}, bf16[8,16,1024]{2,1,0:T(8,128)(2,1)}, bf16[8,16,1024]{2,1,0:T(8,12...) custom-call(s32[3]{0:T(128)S(1)} %pad_add_fusion.place, ...), custom_call_target="tpu_custom_call" | custom-call | flops 100000000 | bytes 6291456 | tf_op jit(solution)/shard_map/masked_rows/pallas_call | solution.py:114
  15.8 6.1 %collective-permute-start = (bf16[8,16,1024]{2,1,0:T(8,128)(2,1)}, bf16[8,16,1024]{2,1,0:T(8,128)(2,1)S(1)}, u32[]{:S(2)}, u32[]{:S(2)}) collective-permute-start(bf16[8,16,1024]{2,1,0:T(8,128)(2,1)} %get-tuple-element.43), channel_id=1, source_target_pairs={{0,10},{1,11},{2,8},{3,9},{4,14},{5,15},{6,12},{7,13},{8,2},{9,3},... | collective-permute-start | bytes 786440 | tf_op jit(solution)/shard_map/ppermute | solution.py:380
  21.9 2.5 %collective-permute-start.2 = (bf16[8,16,1024]{2,1,0:T(8,128)(2,1)}, bf16[8,16,1024]{2,1,0:T(8,128)(2,1)S(1)}, u32[]{:S(2)}, u32[]{:S(2)}) collective-permute-start(bf16[8,16,1024]{2,1,0:T(8,128)(2,1)} %get-tuple-element.45), channel_id=1, source_target_pairs={{0,9},{1,10},{2,11},{3,8},{4,13},{5,14},{6,15},{7,12},{8,1},{9,2},... | collective-permute-start | bytes 786440 | tf_op jit(solution)/shard_map/ppermute | solution.py:380
  24.4 2.6 %collective-permute-start.3 = (bf16[8,16,1024]{2,1,0:T(8,128)(2,1)}, bf16[8,16,1024]{2,1,0:T(8,128)(2,1)S(1)}, u32[]{:S(2)}, u32[]{:S(2)}) collective-permute-start(bf16[8,16,1024]{2,1,0:T(8,128)(2,1)} %get-tuple-element.46), channel_id=1, source_target_pairs={{0,11},{1,8},{2,9},{3,10},{4,15},{5,12},{6,13},{7,14},{8,3},{9,0},... | collective-permute-start | bytes 786440 | tf_op jit(solution)/shard_map/ppermute | solution.py:380
  27.0 3.9 %collective-permute-start.4 = (bf16[8,16,1024]{2,1,0:T(8,128)(2,1)}, bf16[8,16,1024]{2,1,0:T(8,128)(2,1)S(1)}, u32[]{:S(2)}, u32[]{:S(2)}) collective-permute-start(bf16[8,16,1024]{2,1,0:T(8,128)(2,1)} %get-tuple-element.47), channel_id=1, source_target_pairs={{0,14},{1,15},{2,12},{3,13},{4,2},{5,3},{6,0},{7,1},{8,6},{9,7},{1... | collective-permute-start | bytes 786440 | tf_op jit(solution)/shard_map/ppermute | solution.py:380
  31.5 7.5 %all-to-all-done.1 = bf16[8,128,1024]{2,1,0:T(8,128)(2,1)} async-done(((bf16[8,128,1024]{2,1,0:T(8,128)(2,1)}), bf16[8,128,1024]{2,1,0:T(8,128)(2,1)}, u32[]{:S(2)}, u32[]{:S(2)}) %all-to-all-start.1) | async-done | bytes 2097184 | tf_op jit(solution)/shard_map/all_to_all | solution.py:361
  39.8 1.3 %copy-done.2 = bf16[1024,1024]{1,0:T(8,128)(2,1)} copy-done((bf16[1024,1024]{1,0:T(8,128)(2,1)}, bf16[1024,1024]{1,0:T(8,128)(2,1)S(1)}, u32[]{:S(2)}) %copy-start.2) | copy-done | bytes 2097176
  41.1 3.6 %collective-permute-start.5 = (bf16[8,16,1024]{2,1,0:T(8,128)(2,1)}, bf16[8,16,1024]{2,1,0:T(8,128)(2,1)S(1)}, u32[]{:S(2)}, u32[]{:S(2)}) collective-permute-start(bf16[8,16,1024]{2,1,0:T(8,128)(2,1)} %get-tuple-element.48), channel_id=1, source_target_pairs={{0,2},{1,3},{2,0},{3,1},{4,6},{5,7},{6,4},{7,5},{8,10},{9,11},{10,... | collective-permute-start | bytes 786440 | tf_op jit(solution)/shard_map/ppermute | solution.py:380
  44.7 1.7 %collective-permute-start.6 = (bf16[8,16,1024]{2,1,0:T(8,128)(2,1)}, bf16[8,16,1024]{2,1,0:T(8,128)(2,1)S(1)}, u32[]{:S(2)}, u32[]{:S(2)}) collective-permute-start(bf16[8,16,1024]{2,1,0:T(8,128)(2,1)} %get-tuple-element.49), channel_id=1, source_target_pairs={{0,5},{1,6},{2,7},{3,4},{4,9},{5,10},{6,11},{7,8},{8,13},{9,14},{1... | collective-permute-start | bytes 786440 | tf_op jit(solution)/shard_map/ppermute | solution.py:380
  46.3 3.3 %collective-permute-done.2.refs_3_ = bf16[8,16,1024]{2,1,0:T(8,128)(2,1)S(1)} collective-permute-done((bf16[8,16,1024]{2,1,0:T(8,128)(2,1)}, bf16[8,16,1024]{2,1,0:T(8,128)(2,1)S(1)}, u32[]{:S(2)}, u32[]{:S(2)}) %collective-permute-start.2) | collective-permute-done | bytes 262176 | tf_op jit(solution)/shard_map/ppermute | solution.py:380
  49.6 9.4 %collective-permute-done.3.refs_4_ = bf16[8,16,1024]{2,1,0:T(8,128)(2,1)S(1)} collective-permute-done((bf16[8,16,1024]{2,1,0:T(8,128)(2,1)}, bf16[8,16,1024]{2,1,0:T(8,128)(2,1)S(1)}, u32[]{:S(2)}, u32[]{:S(2)}) %collective-permute-start.3) | collective-permute-done | bytes 262176 | tf_op jit(solution)/shard_map/ppermute | solution.py:380
  59.2 20.9 %burn_in.1 = bf16[8,2,16,512]{3,2,1,0:T(8,128)(2,1)} custom-call(s32[3]{0:T(128)S(1)} %pad_add_fusion.place, s32[1]{0:T(128)} %get-tuple-element.61.crowded, bf16[1024,1024]{1,0:T(8,128)(2,1)} %bitcast.4.rows_hbm, bf16[1024,1024]{1,0:T(8,128)(2,1)} %copy-done.2, bf16[1024,2048]{1,0:T(8,128)(2,1)} %win_hbm.1, bf16[512,2048]{1,0:T(8,128)(2,1)} %wh_hbm.1, ...), custom_call_target="tpu_custom_call" | custom-call | flops 30000001024 | bytes 8388608 | tf_op jit(solution)/shard_map/burn_in/pallas_call | solution.py:241
  80.1 4.5 %all-to-all-start.2 = ((bf16[8,2,16,512]{3,2,1,0:T(8,128)(2,1)}), bf16[8,2,16,512]{3,2,1,0:T(8,128)(2,1)S(1)}, u32[]{:S(2)}, u32[]{:S(2)}) async-start(bf16[8,2,16,512]{3,2,1,0:T(8,128)(2,1)} %burn_in.1), calls=%async_computation.2 | async-start | bytes 524288 | tf_op jit(solution)/shard_map/all_to_all | solution.py:396
  84.6 5.8 %collective-permute-start.10 = (bf16[8,16,1024]{2,1,0:T(8,128)(2,1)}, bf16[8,16,1024]{2,1,0:T(8,128)(2,1)S(1)}, u32[]{:S(2)}, u32[]{:S(2)}) collective-permute-start(bf16[8,16,1024]{2,1,0:T(8,128)(2,1)} %get-tuple-element.53), channel_id=1, source_target_pairs={{0,15},{1,12},{2,13},{3,14},{4,3},{5,0},{6,1},{7,2},{8,7},{9,4},{1... | collective-permute-start | bytes 786440 | tf_op jit(solution)/shard_map/ppermute | solution.py:380
  90.5 2.7 %collective-permute-start.12 = (bf16[8,16,1024]{2,1,0:T(8,128)(2,1)}, bf16[8,16,1024]{2,1,0:T(8,128)(2,1)}, u32[]{:S(2)}, u32[]{:S(2)}) collective-permute-start(bf16[8,16,1024]{2,1,0:T(8,128)(2,1)} %get-tuple-element.55), channel_id=1, source_target_pairs={{0,3},{1,0},{2,1},{3,2},{4,7},{5,4},{6,5},{7,6},{8,11},{9,8},{10,9... | collective-permute-start | bytes 786440 | tf_op jit(solution)/shard_map/ppermute | solution.py:380
  93.2 1.6 %collective-permute-start.13 = (bf16[8,16,1024]{2,1,0:T(8,128)(2,1)}, bf16[8,16,1024]{2,1,0:T(8,128)(2,1)}, u32[]{:S(2)}, u32[]{:S(2)}) collective-permute-start(bf16[8,16,1024]{2,1,0:T(8,128)(2,1)} %get-tuple-element.56), channel_id=1, source_target_pairs={{0,4},{1,5},{2,6},{3,7},{4,8},{5,9},{6,10},{7,11},{8,12},{9,13},{1... | collective-permute-start | bytes 786440 | tf_op jit(solution)/shard_map/ppermute | solution.py:380
  94.8 1.1 collective-permute-start.14
  96.9 5.2 %all-to-all-start.3 = ((bf16[16,8,1152]{2,1,0:T(8,128)(2,1)}), bf16[16,8,1152]{2,1,0:T(8,128)(2,1)S(1)}, u32[]{:S(2)}, u32[]{:S(2)}) async-start(bf16[16,8,1152]{2,1,0:T(8,128)(2,1)} %bitcast.9), calls=%async_computation.3 | async-start | bytes 589824 | tf_op jit(solution)/shard_map/all_to_all | solution.py:400
  102.1 1.7 %collective-permute-done.12.refs_13_ = bf16[8,16,1024]{2,1,0:T(8,128)(2,1)} collective-permute-done((bf16[8,16,1024]{2,1,0:T(8,128)(2,1)}, bf16[8,16,1024]{2,1,0:T(8,128)(2,1)}, u32[]{:S(2)}, u32[]{:S(2)}) %collective-permute-start.12) | collective-permute-done | bytes 262176 | tf_op jit(solution)/shard_map/ppermute | solution.py:380
  104.4 3.3 %place_rows.1 = bf16[128,16,1024]{2,1,0:T(8,128)(2,1)} custom-call(s32[3]{0:T(128)S(1)} %pad_add_fusion.place, bf16[8,16,1024]{2,1,0:T(8,128)(2,1)S(1)} %copy-done, bf16[8,16,1024]{2,1,0:T(8,128)(2,1)S(1)} %collective-permute-done.refs_1_, bf16[8,16,1024]{2,1,0:T(8,128)(2,1)S(1)} %collective-permute-done.1.refs_2_, ...), custom_call_target="tpu_custom_call" | custom-call | flops 1000000000 | bytes 8388608 | tf_op jit(solution)/shard_map/place_rows/pallas_call | solution.py:146
  107.7 2.0 %all-to-all-done.3 = bf16[16,8,1152]{2,1,0:T(8,128)(2,1)S(1)} async-done(((bf16[16,8,1152]{2,1,0:T(8,128)(2,1)}), bf16[16,8,1152]{2,1,0:T(8,128)(2,1)S(1)}, u32[]{:S(2)}, u32[]{:S(2)}) %all-to-all-start.3) | async-done | bytes 294944 | tf_op jit(solution)/shard_map/all_to_all | solution.py:400
  (44 shorter events, 4.9 us)
Async XLA Ops:
  6.6 6.1 %copy-start.1 = (bf16[64,16,1024]{2,1,0:T(8,128)(2,1)S(1)}, bf16[64,16,1024]{2,1,0:T(8,128)(2,1)}, u32[]{:S(2)}) copy-start(bf16[64,16,1024]{2,1,0:T(8,128)(2,1)} %obs.3) | copy-start | bytes 6291460
  6.6 32.4 %all-to-all-start.1 = ((bf16[8,128,1024]{2,1,0:T(8,128)(2,1)}), bf16[8,128,1024]{2,1,0:T(8,128)(2,1)}, u32[]{:S(2)}, u32[]{:S(2)}) async-start(bf16[8,128,1024]{2,1,0:T(8,128)(2,1)} %get-tuple-element.59), calls=%async_computation.1 | async-start | bytes 4194304 | tf_op jit(solution)/shard_map/all_to_all | solution.py:361
  12.7 18.1 %copy-start.5 = (s32[128]{0:T(128)S(1)}, s32[128]{0:T(128)}, u32[]{:S(2)}) copy-start(s32[128]{0:T(128)} %param.17) | copy-start | bytes 1540
  12.8 18.2 %copy-start.3 = (f32[2048]{0:T(1024)S(1)}, f32[2048]{0:T(1024)}, u32[]{:S(2)}) copy-start(f32[2048]{0:T(1024)} %param.13) | copy-start | bytes 24580
  12.8 18.2 %copy-start.4 = (f32[512]{0:T(512)S(1)}, f32[512]{0:T(512)}, u32[]{:S(2)}) copy-start(f32[512]{0:T(512)} %param.14) | copy-start | bytes 6148
  15.8 24.0 %collective-permute-start = (bf16[8,16,1024]{2,1,0:T(8,128)(2,1)}, bf16[8,16,1024]{2,1,0:T(8,128)(2,1)S(1)}, u32[]{:S(2)}, u32[]{:S(2)}) collective-permute-start(bf16[8,16,1024]{2,1,0:T(8,128)(2,1)} %get-tuple-element.43), channel_id=1, source_target_pairs={{0,10},{1,11},{2,8},{3,9},{4,14},{5,15},{6,12},{7,13},{8,2},{9,3},... | collective-permute-start | bytes 786440 | tf_op jit(solution)/shard_map/ppermute | solution.py:380
  21.9 22.7 %collective-permute-start.1 = (bf16[8,16,1024]{2,1,0:T(8,128)(2,1)}, bf16[8,16,1024]{2,1,0:T(8,128)(2,1)S(1)}, u32[]{:S(2)}, u32[]{:S(2)}) collective-permute-start(bf16[8,16,1024]{2,1,0:T(8,128)(2,1)} %get-tuple-element.44), channel_id=1, source_target_pairs={{0,6},{1,7},{2,4},{3,5},{4,10},{5,11},{6,8},{7,9},{8,14},{9,15},{1... | collective-permute-start | bytes 786440 | tf_op jit(solution)/shard_map/ppermute | solution.py:380
  21.9 27.7 %collective-permute-start.2 = (bf16[8,16,1024]{2,1,0:T(8,128)(2,1)}, bf16[8,16,1024]{2,1,0:T(8,128)(2,1)S(1)}, u32[]{:S(2)}, u32[]{:S(2)}) collective-permute-start(bf16[8,16,1024]{2,1,0:T(8,128)(2,1)} %get-tuple-element.45), channel_id=1, source_target_pairs={{0,9},{1,10},{2,11},{3,8},{4,13},{5,14},{6,15},{7,12},{8,1},{9,2},... | collective-permute-start | bytes 786440 | tf_op jit(solution)/shard_map/ppermute | solution.py:380
  24.4 34.7 %collective-permute-start.3 = (bf16[8,16,1024]{2,1,0:T(8,128)(2,1)}, bf16[8,16,1024]{2,1,0:T(8,128)(2,1)S(1)}, u32[]{:S(2)}, u32[]{:S(2)}) collective-permute-start(bf16[8,16,1024]{2,1,0:T(8,128)(2,1)} %get-tuple-element.46), channel_id=1, source_target_pairs={{0,11},{1,8},{2,9},{3,10},{4,15},{5,12},{6,13},{7,14},{8,3},{9,0},... | collective-permute-start | bytes 786440 | tf_op jit(solution)/shard_map/ppermute | solution.py:380
  27.0 32.1 %collective-permute-start.4 = (bf16[8,16,1024]{2,1,0:T(8,128)(2,1)}, bf16[8,16,1024]{2,1,0:T(8,128)(2,1)S(1)}, u32[]{:S(2)}, u32[]{:S(2)}) collective-permute-start(bf16[8,16,1024]{2,1,0:T(8,128)(2,1)} %get-tuple-element.47), channel_id=1, source_target_pairs={{0,14},{1,15},{2,12},{3,13},{4,2},{5,3},{6,0},{7,1},{8,6},{9,7},{1... | collective-permute-start | bytes 786440 | tf_op jit(solution)/shard_map/ppermute | solution.py:380
  39.7 1.3 %copy-start.2 = (bf16[1024,1024]{1,0:T(8,128)(2,1)}, bf16[1024,1024]{1,0:T(8,128)(2,1)S(1)}, u32[]{:S(2)}) copy-start(bf16[1024,1024]{1,0:T(8,128)(2,1)S(1)} %get-tuple-element.67.more_hbm) | copy-start | bytes 6291460
  41.1 43.6 %collective-permute-start.5 = (bf16[8,16,1024]{2,1,0:T(8,128)(2,1)}, bf16[8,16,1024]{2,1,0:T(8,128)(2,1)S(1)}, u32[]{:S(2)}, u32[]{:S(2)}) collective-permute-start(bf16[8,16,1024]{2,1,0:T(8,128)(2,1)} %get-tuple-element.48), channel_id=1, source_target_pairs={{0,2},{1,3},{2,0},{3,1},{4,6},{5,7},{6,4},{7,5},{8,10},{9,11},{10,... | collective-permute-start | bytes 786440 | tf_op jit(solution)/shard_map/ppermute | solution.py:380
  44.7 45.8 %collective-permute-start.6 = (bf16[8,16,1024]{2,1,0:T(8,128)(2,1)}, bf16[8,16,1024]{2,1,0:T(8,128)(2,1)S(1)}, u32[]{:S(2)}, u32[]{:S(2)}) collective-permute-start(bf16[8,16,1024]{2,1,0:T(8,128)(2,1)} %get-tuple-element.49), channel_id=1, source_target_pairs={{0,5},{1,6},{2,7},{3,4},{4,9},{5,10},{6,11},{7,8},{8,13},{9,14},{1... | collective-permute-start | bytes 786440 | tf_op jit(solution)/shard_map/ppermute | solution.py:380
  49.6 40.9 %collective-permute-start.7 = (bf16[8,16,1024]{2,1,0:T(8,128)(2,1)}, bf16[8,16,1024]{2,1,0:T(8,128)(2,1)S(1)}, u32[]{:S(2)}, u32[]{:S(2)}) collective-permute-start(bf16[8,16,1024]{2,1,0:T(8,128)(2,1)} %get-tuple-element.50), channel_id=1, source_target_pairs={{0,7},{1,4},{2,5},{3,6},{4,11},{5,8},{6,9},{7,10},{8,15},{9,12},{1... | collective-permute-start | bytes 786440 | tf_op jit(solution)/shard_map/ppermute | solution.py:380
  59.1 34.1 %collective-permute-start.8 = (bf16[8,16,1024]{2,1,0:T(8,128)(2,1)}, bf16[8,16,1024]{2,1,0:T(8,128)(2,1)S(1)}, u32[]{:S(2)}, u32[]{:S(2)}) collective-permute-start(bf16[8,16,1024]{2,1,0:T(8,128)(2,1)} %get-tuple-element.51), channel_id=1, source_target_pairs={{0,8},{1,9},{2,10},{3,11},{4,12},{5,13},{6,14},{7,15},{8,0},{9,1},... | collective-permute-start | bytes 786440 | tf_op jit(solution)/shard_map/ppermute | solution.py:380
  59.1 45.3 %copy-start = (bf16[8,16,1024]{2,1,0:T(8,128)(2,1)S(1)}, bf16[8,16,1024]{2,1,0:T(8,128)(2,1)}, u32[]{:S(2)}) copy-start(bf16[8,16,1024]{2,1,0:T(8,128)(2,1)} %get-tuple-element.42.refs_0_) | copy-start | bytes 786436
  59.1 35.7 %collective-permute-start.9 = (bf16[8,16,1024]{2,1,0:T(8,128)(2,1)}, bf16[8,16,1024]{2,1,0:T(8,128)(2,1)S(1)}, u32[]{:S(2)}, u32[]{:S(2)}) collective-permute-start(bf16[8,16,1024]{2,1,0:T(8,128)(2,1)} %get-tuple-element.52), channel_id=1, source_target_pairs={{0,13},{1,14},{2,15},{3,12},{4,1},{5,2},{6,3},{7,0},{8,5},{9,6},{1... | collective-permute-start | bytes 786440 | tf_op jit(solution)/shard_map/ppermute | solution.py:380
  80.1 15.8 %all-to-all-start.2 = ((bf16[8,2,16,512]{3,2,1,0:T(8,128)(2,1)}), bf16[8,2,16,512]{3,2,1,0:T(8,128)(2,1)S(1)}, u32[]{:S(2)}, u32[]{:S(2)}) async-start(bf16[8,2,16,512]{3,2,1,0:T(8,128)(2,1)} %burn_in.1), calls=%async_computation.2 | async-start | bytes 524288 | tf_op jit(solution)/shard_map/all_to_all | solution.py:396
  84.6 17.4 %collective-permute-start.10 = (bf16[8,16,1024]{2,1,0:T(8,128)(2,1)}, bf16[8,16,1024]{2,1,0:T(8,128)(2,1)S(1)}, u32[]{:S(2)}, u32[]{:S(2)}) collective-permute-start(bf16[8,16,1024]{2,1,0:T(8,128)(2,1)} %get-tuple-element.53), channel_id=1, source_target_pairs={{0,15},{1,12},{2,13},{3,14},{4,3},{5,0},{6,1},{7,2},{8,7},{9,4},{1... | collective-permute-start | bytes 786440 | tf_op jit(solution)/shard_map/ppermute | solution.py:380
  90.5 11.6 %collective-permute-start.11 = (bf16[8,16,1024]{2,1,0:T(8,128)(2,1)}, bf16[8,16,1024]{2,1,0:T(8,128)(2,1)}, u32[]{:S(2)}, u32[]{:S(2)}) collective-permute-start(bf16[8,16,1024]{2,1,0:T(8,128)(2,1)} %get-tuple-element.54), channel_id=1, source_target_pairs={{0,1},{1,2},{2,3},{3,0},{4,5},{5,6},{6,7},{7,4},{8,9},{9,10},{10,1... | collective-permute-start | bytes 786440 | tf_op jit(solution)/shard_map/ppermute | solution.py:380
  90.5 13.2 %collective-permute-start.12 = (bf16[8,16,1024]{2,1,0:T(8,128)(2,1)}, bf16[8,16,1024]{2,1,0:T(8,128)(2,1)}, u32[]{:S(2)}, u32[]{:S(2)}) collective-permute-start(bf16[8,16,1024]{2,1,0:T(8,128)(2,1)} %get-tuple-element.55), channel_id=1, source_target_pairs={{0,3},{1,0},{2,1},{3,2},{4,7},{5,4},{6,5},{7,6},{8,11},{9,8},{10,9... | collective-permute-start | bytes 786440 | tf_op jit(solution)/shard_map/ppermute | solution.py:380
  93.2 10.6 %collective-permute-start.13 = (bf16[8,16,1024]{2,1,0:T(8,128)(2,1)}, bf16[8,16,1024]{2,1,0:T(8,128)(2,1)}, u32[]{:S(2)}, u32[]{:S(2)}) collective-permute-start(bf16[8,16,1024]{2,1,0:T(8,128)(2,1)} %get-tuple-element.56), channel_id=1, source_target_pairs={{0,4},{1,5},{2,6},{3,7},{4,8},{5,9},{6,10},{7,11},{8,12},{9,13},{1... | collective-permute-start | bytes 786440 | tf_op jit(solution)/shard_map/ppermute | solution.py:380
  94.8 9.6 %collective-permute-start.14 = (bf16[8,16,1024]{2,1,0:T(8,128)(2,1)}, bf16[8,16,1024]{2,1,0:T(8,128)(2,1)}, u32[]{:S(2)}, u32[]{:S(2)}) collective-permute-start(bf16[8,16,1024]{2,1,0:T(8,128)(2,1)} %get-tuple-element.57), channel_id=1, source_target_pairs={{0,12},{1,13},{2,14},{3,15},{4,0},{5,1},{6,2},{7,3},{8,4},{9,5},{1... | collective-permute-start | bytes 786440 | tf_op jit(solution)/shard_map/ppermute | solution.py:380
  96.9 12.9 %all-to-all-start.3 = ((bf16[16,8,1152]{2,1,0:T(8,128)(2,1)}), bf16[16,8,1152]{2,1,0:T(8,128)(2,1)S(1)}, u32[]{:S(2)}, u32[]{:S(2)}) async-start(bf16[16,8,1152]{2,1,0:T(8,128)(2,1)} %bitcast.9), calls=%async_computation.3 | async-start | bytes 589824 | tf_op jit(solution)/shard_map/all_to_all | solution.py:400

commit v5 on v4

--- a/solution.py
+++ b/solution.py
@@ -36,53 +36,89 @@
     return jnp.dot(a, b, preferred_element_type=jnp.float32)
 
 
-def pack_kernel(base, place, ids, starts_ref, obs, out, crowded, rows_of, packed, sem):
-    shards, count = starts_ref.shape
+def pack_kernel(
+    base, place, ids_ref, starts_ref, obs_hbm, out, crowded, dealt, rank_ref, obs, ids_held, ids, rows_of, packed, sem, obs_sem
+):
+    obs_copy = pltpu.make_async_copy(obs_hbm, obs, obs_sem.at[0])
+    obs_copy.start()
+    shards, count = dealt.shape
+    total = shards * count
     shard_steps = obs.shape[1]
     lanes = count * shard_steps
+    row, column = iota((total, total), 0), iota((total, total), 1)
+
+    def upright(values):
+        return jnp.sum(jnp.where(row == column, values, 0.0), axis=1, keepdims=True)
+
+    start_row = starts_ref[...].astype(jnp.float32)
+    start_column = upright(start_row)
+    ahead = (start_row < start_column) | ((start_row == start_column) & (column < row))
+    rank_column = jnp.sum(jnp.where(ahead, 1.0, 0.0), axis=1, keepdims=True)
+    rank_row = jnp.sum(jnp.where(row == column, rank_column, 0.0), axis=0, keepdims=True)
+    rank_ref[...] = rank_row.astype(jnp.int32)
+    whole_rank = rank_column.astype(jnp.int32)
+    taker = (column % count) * shards + column // count
+    ids_row = jnp.where(whole_rank == taker, upright(ids_ref[...].astype(jnp.float32)), 0.0)
+    ids_held[...] = jnp.sum(ids_row, axis=0, keepdims=True).astype(jnp.int32)
+    ids_copy = pltpu.make_async_copy(ids_held, ids, obs_sem.at[1])
+    ids_copy.start()
+    to_shard = one_hot(iota((shards, total), 0) == rank_row.astype(jnp.int32) % shards)
+    to_place = jnp.where(iota((total, count), 1) == whole_rank // shards, start_column, 0.0)
+    dealt_starts = f32_dot(to_shard, to_place.astype(jnp.bfloat16))
+    dealt[...] = dealt_starts.astype(jnp.int32)
     spread = one_hot(iota((count, lanes), 1) // shard_steps == iota((count, lanes), 0))
-    starts = f32_dot(starts_ref[...].astype(jnp.bfloat16), spread).astype(jnp.int32)
+    starts = f32_dot(dealt_starts.astype(jnp.bfloat16), spread).astype(jnp.int32)
     step = place[0] * shard_steps + iota((shards, lanes), 1) % shard_steps
     within = ((step - starts) & (STEPS - 1)) < BURN
     before = one_hot(iota((lanes, lanes), 0) < iota((lanes, lanes), 1))
     slot = f32_dot(one_hot(within), before).astype(jnp.int32) - base
     slot = jnp.where(within, slot, -1)
-    for k in range(shards):
-        for i in range(count):
-            rows_of[k, i * shard_steps : (i + 1) * shard_steps, :] = obs[ids[k, i]]
-        hot = one_hot(iota((ROOM, lanes), 0) == slot[k : k + 1, :])
-        packed[k] = f32_dot(hot, rows_of[k]).astype(jnp.bfloat16)
-        pltpu.make_async_copy(packed.at[k], out.at[k], sem.at[k]).start()
     most = jnp.zeros((shards, lanes // 2), jnp.float32)
     for shard in range(shards):
         held = ((step + (shard * shard_steps) - starts) & (STEPS - 1)) < BURN
         some = jnp.where(held, 1.0, 0.0)
         most = jnp.maximum(most, f32_dot(some.astype(jnp.bfloat16), jnp.ones((lanes, lanes // 2), jnp.bfloat16)))
     crowded[0] = (jnp.max(most) > ROOM).astype(jnp.int32)
+    ids_copy.wait()
+    obs_copy.wait()
+    copies = [pltpu.make_async_copy(packed.at[k], out.at[k], sem.at[k]) for k in range(shards)]
     for k in range(shards):
-        pltpu.make_async_copy(packed.at[k], out.at[k], sem.at[k]).wait()
-
-
-def pack(base, place, ids, starts, observations):
-    shards, count = ids.shape
+        for i in range(count):
+            rows_of[k, i * shard_steps : (i + 1) * shard_steps, :] = obs[ids[0, k * count + i]]
+        hot = one_hot(iota((ROOM, lanes), 0) == slot[k : k + 1, :])
+        packed[k] = f32_dot(hot, rows_of[k]).astype(jnp.bfloat16)
+        copies[k].start()
+    for copy in copies:
+        copy.wait()
+
+
+def pack(base, place, shards, ids, starts, observations):
     _, shard_steps, width = observations.shape
+    total = ids.shape[0]
+    count = total // shards
     return pl.pallas_call(
         functools.partial(pack_kernel, base),
         out_shape=(
             jax.ShapeDtypeStruct((shards, ROOM, width), jnp.bfloat16),
             jax.ShapeDtypeStruct((1,), jnp.int32),
+            jax.ShapeDtypeStruct((shards, count), jnp.int32),
+            jax.ShapeDtypeStruct((1, total), jnp.int32),
         ),
-        in_specs=[SMEM, SMEM, VMEM, VMEM],
-        out_specs=(HBM, SMEM),
+        in_specs=[SMEM, VMEM, VMEM, HBM],
+        out_specs=(HBM, SMEM, VMEM, VMEM),
         scratch_shapes=[
+            pltpu.VMEM(observations.shape, jnp.bfloat16),
+            pltpu.VMEM((1, total), jnp.int32),
+            pltpu.SMEM((1, total), jnp.int32),
             pltpu.VMEM((shards, count * shard_steps, width), jnp.bfloat16),
             pltpu.VMEM((shards, ROOM, width), jnp.bfloat16),
             pltpu.SemaphoreType.DMA((shards,)),
+            pltpu.SemaphoreType.DMA((2,)),
         ],
-        compiler_params=pltpu.CompilerParams(vmem_limit_bytes=24 * MIB),
+        compiler_params=pltpu.CompilerParams(vmem_limit_bytes=58 * MIB),
         cost_estimate=pl.CostEstimate(flops=10**9, bytes_accessed=4 * MIB, transcendentals=0),
         name="pack_rows",
-    )(place, ids, starts, observations)
+    )(place, ids[None, :], starts[None, :], observations)
 
 
 def block_at(here, grid, n, sign):
@@ -344,22 +380,12 @@
     shards = lax.axis_size("tm")
     learners = lax.axis_size(EP)
     place = jnp.stack([lax.axis_index(axis) for axis in ("tm", *EP)]).astype(jnp.int32)
-    own_count = seq_count // shards
     per_learner = seq_count // learners
 
-    index = jnp.arange(seq_count, dtype=jnp.int32)
-    key = start_steps * seq_count + index
-    rank = jnp.sum((key[None, :] < key[:, None]).astype(jnp.int32), axis=1)
-    turn = jnp.arange(shards, dtype=jnp.int32)
-    dealt = jnp.arange(own_count, dtype=jnp.int32)[None, :] * shards + turn[:, None]
-    chosen = rank[None, None, :] == dealt[:, :, None]
-    ids = jnp.sum(jnp.where(chosen, episode_ids, 0), axis=2)
-    starts = jnp.sum(jnp.where(chosen, start_steps, 0), axis=2)
-
     def exchanged(base):
-        sent, crowded = pack(base, place, ids, starts, observations)
+        sent, *rest = pack(base, place, shards, episode_ids, start_steps, observations)
         rows = lax.all_to_all(sent, "tm", split_axis=0, concat_axis=0, tiled=True)
-        return rows.reshape(shards * ROOM, width), crowded
+        return rows.reshape(shards * ROOM, width), *rest
 
     grid = along, across = tuple(lax.axis_size(axis) for axis in EP)
 
@@ -369,7 +395,7 @@
 
     late = [n for n in range(1, learners) if hops(n) == 1]
     order = sorted((n for n in range(1, learners) if n not in late), key=lambda n: (-hops(n), n)) + late
-    rows_in, crowded = exchanged(0)
+    rows_in, crowded, starts, rank_row = exchanged(0)
     sent_rows = masked(grid, place, episode_ids, start_steps, observations)
     moved_rows = [sent_rows[0]]
     for n in order:
@@ -384,7 +410,7 @@
 
     raw_weight = jnp.exp(-IMPORTANCE * jnp.log(priorities.astype(jnp.float32))).astype(jnp.bfloat16)
     raw_row = raw_weight.astype(jnp.float32)[None, :]
-    bias, rank_row, raw_row = lax.optimization_barrier((bias, rank[None, :], raw_row))
+    bias, raw_row = lax.optimization_barrier((bias, raw_row))
 
     rows_in, again = lax.optimization_barrier((rows_in, crowded))
     more = lax.cond(

time: 113 us -> 111 us (0.982)
  other arithmetic: 2.61 us -> 0.67 us
    ppermute x15, waiting for transfers between devices: 15.1 us -> 13.8 us  [body(): moved_rows.append(lax.ppermute(sent_rows[n], EP, ring))]
    reduce_sum x2 -> x0, other arithmetic: 1.26 us -> none  [the longest x1 1.09 us: body(): starts = jnp.sum(jnp.where(chosen, start_steps, 0), axis=2)]
  transfers between devices with their start and end apart: 18 -> 18, of which waited for: 6 -> 6; matrix products, arithmetic and copies ran while one was open for 1% -> 1% of each run, Pallas kernels for 25% -> 26%
where the time goes in v5:
time: 111 us; the launch traced here: 110 us
  starting transfers between devices  48.4 us (44%)
  Pallas kernels  33.2 us (30%)
  waiting for transfers between devices  23.7 us (21%)
  local copies, waits for them, and re-layouts  2.27 us (2%)
  between operations  1.51 us (1%)
    ppermute x15, starting transfers between devices, body(): moved_rows.append(lax.ppermute(sent_rows[n], EP, ring))  32 us
    pallas_call x1, Pallas kernels, burn_in(): pl.pallas_call(burn_in_kernel, out_shape=jax.ShapeDtypeStruct((shards, 2,...  20.9 us
    ppermute x15, waiting for transfers between devices, body(): moved_rows.append(lax.ppermute(sent_rows[n], EP, ring))  13.8 us
    all_to_all x1, waiting for transfers between devices, exchanged(): rows = lax.all_to_all(sent, 'tm', split_axis=0, concat_axis=0, tiled=True)  7.79 us
    all_to_all x1, starting transfers between devices, exchanged(): rows = lax.all_to_all(sent, 'tm', split_axis=0, concat_axis=0, tiled=True)  6.1 us
    all_to_all x1, starting transfers between devices, body(): both = lax.all_to_all(both, EP, split_axis=0, concat_axis=0, tiled=True)  5.19 us
    all_to_all x1, starting transfers between devices, body(): pairs = lax.all_to_all(pairs, 'tm', split_axis=0, concat_axis=0, tiled=True)  5.11 us
    pallas_call x1, Pallas kernels, pack(): pl.pallas_call(functools.partial(pack_kernel, base), out_shape=(jax.Shape...  4.51 us
  transfers between devices with their start and end apart: 18, of which 6 were waited for; matrix products, arithmetic and copies ran while one was open for 1% of the time, Pallas kernels for 26%

profile of v5, /device:TPU:1, one launch (start us, length us, event | category | flops | bytes accessed | tf_op | source)
XLA Modules:
  0.0 109.7 jit_solution(12854806888023356949)
XLA Ops:
  0.7 4.5 %pack_rows.3 = (bf16[8,128,1024]{2,1,0:T(8,128)(2,1)}, s32[1]{0:T(128)}, s32[8,16]{1,0:T(8,128)}, s32[1,128]{1,0:T(1,128)}) custom-call(s32[3]{0:T(128)S(1)} %pad_add_fusion.place, s32[1,128]{1,0:T(1,128)} %bitcast.20, s32[1,128]{1,0:T(1,128)} %bitcast.22, bf16[64,16,1024]{2,1,0:T(8,128)(2,1)} %obs_hbm.1), custom_call_target="tpu_custom_call" | custom-call | flops 1000000000 | bytes 4194304 | tf_op jit(solution)/shard_map/pack_rows/pallas_call | solution.py:99
  5.3 6.1 %all-to-all-start.1 = ((bf16[8,128,1024]{2,1,0:T(8,128)(2,1)}), bf16[8,128,1024]{2,1,0:T(8,128)(2,1)}, u32[]{:S(2)}, u32[]{:S(2)}) async-start(bf16[8,128,1024]{2,1,0:T(8,128)(2,1)} %get-tuple-element.60), calls=%async_computation.1 | async-start | bytes 4194304 | tf_op jit(solution)/shard_map/all_to_all | solution.py:387
  11.4 2.7 %masked_rows.1 = (bf16[8,16,1024]{2,1,0:T(8,128)(2,1)}, bf16[8,16,1024]{2,1,0:T(8,128)(2,1)}, bf16[8,16,1024]{2,1,0:T(8,128)(2,1)}, bf16[8,16,1024]{2,1,0:T(8,12...) custom-call(s32[3]{0:T(128)S(1)} %pad_add_fusion.place, ...), custom_call_target="tpu_custom_call" | custom-call | flops 100000000 | bytes 6291456 | tf_op jit(solution)/shard_map/masked_rows/pallas_call | solution.py:150
  14.2 6.1 %collective-permute-start = (bf16[8,16,1024]{2,1,0:T(8,128)(2,1)}, bf16[8,16,1024]{2,1,0:T(8,128)(2,1)S(1)}, u32[]{:S(2)}, u32[]{:S(2)}) collective-permute-start(bf16[8,16,1024]{2,1,0:T(8,128)(2,1)} %get-tuple-element.44), channel_id=1, source_target_pairs={{0,10},{1,11},{2,8},{3,9},{4,14},{5,15},{6,12},{7,13},{8,2},{9,3},... | collective-permute-start | bytes 786440 | tf_op jit(solution)/shard_map/ppermute | solution.py:406
  20.3 2.5 %collective-permute-start.2 = (bf16[8,16,1024]{2,1,0:T(8,128)(2,1)}, bf16[8,16,1024]{2,1,0:T(8,128)(2,1)S(1)}, u32[]{:S(2)}, u32[]{:S(2)}) collective-permute-start(bf16[8,16,1024]{2,1,0:T(8,128)(2,1)} %get-tuple-element.46), channel_id=1, source_target_pairs={{0,9},{1,10},{2,11},{3,8},{4,13},{5,14},{6,15},{7,12},{8,1},{9,2},... | collective-permute-start | bytes 786440 | tf_op jit(solution)/shard_map/ppermute | solution.py:406
  22.8 2.6 %collective-permute-start.3 = (bf16[8,16,1024]{2,1,0:T(8,128)(2,1)}, bf16[8,16,1024]{2,1,0:T(8,128)(2,1)S(1)}, u32[]{:S(2)}, u32[]{:S(2)}) collective-permute-start(bf16[8,16,1024]{2,1,0:T(8,128)(2,1)} %get-tuple-element.47), channel_id=1, source_target_pairs={{0,11},{1,8},{2,9},{3,10},{4,15},{5,12},{6,13},{7,14},{8,3},{9,0},... | collective-permute-start | bytes 786440 | tf_op jit(solution)/shard_map/ppermute | solution.py:406
  25.4 3.9 %collective-permute-start.4 = (bf16[8,16,1024]{2,1,0:T(8,128)(2,1)}, bf16[8,16,1024]{2,1,0:T(8,128)(2,1)S(1)}, u32[]{:S(2)}, u32[]{:S(2)}) collective-permute-start(bf16[8,16,1024]{2,1,0:T(8,128)(2,1)} %get-tuple-element.48), channel_id=1, source_target_pairs={{0,14},{1,15},{2,12},{3,13},{4,2},{5,3},{6,0},{7,1},{8,6},{9,7},{1... | collective-permute-start | bytes 786440 | tf_op jit(solution)/shard_map/ppermute | solution.py:406
  29.9 7.8 %all-to-all-done.1 = bf16[8,128,1024]{2,1,0:T(8,128)(2,1)} async-done(((bf16[8,128,1024]{2,1,0:T(8,128)(2,1)}), bf16[8,128,1024]{2,1,0:T(8,128)(2,1)}, u32[]{:S(2)}, u32[]{:S(2)}) %all-to-all-start.1) | async-done | bytes 2097184 | tf_op jit(solution)/shard_map/all_to_all | solution.py:387
  38.4 1.3 %copy-done.3 = bf16[1024,1024]{1,0:T(8,128)(2,1)} copy-done((bf16[1024,1024]{1,0:T(8,128)(2,1)}, bf16[1024,1024]{1,0:T(8,128)(2,1)S(1)}, u32[]{:S(2)}) %copy-start.3) | copy-done | bytes 2097176
  39.7 3.6 %collective-permute-start.5 = (bf16[8,16,1024]{2,1,0:T(8,128)(2,1)}, bf16[8,16,1024]{2,1,0:T(8,128)(2,1)S(1)}, u32[]{:S(2)}, u32[]{:S(2)}) collective-permute-start(bf16[8,16,1024]{2,1,0:T(8,128)(2,1)} %get-tuple-element.49), channel_id=1, source_target_pairs={{0,2},{1,3},{2,0},{3,1},{4,6},{5,7},{6,4},{7,5},{8,10},{9,11},{10,... | collective-permute-start | bytes 786440 | tf_op jit(solution)/shard_map/ppermute | solution.py:406
  43.3 1.7 %collective-permute-start.6 = (bf16[8,16,1024]{2,1,0:T(8,128)(2,1)}, bf16[8,16,1024]{2,1,0:T(8,128)(2,1)S(1)}, u32[]{:S(2)}, u32[]{:S(2)}) collective-permute-start(bf16[8,16,1024]{2,1,0:T(8,128)(2,1)} %get-tuple-element.50), channel_id=1, source_target_pairs={{0,5},{1,6},{2,7},{3,4},{4,9},{5,10},{6,11},{7,8},{8,13},{9,14},{1... | collective-permute-start | bytes 786440 | tf_op jit(solution)/shard_map/ppermute | solution.py:406
  45.0 2.5 %collective-permute-done.2.refs_3_ = bf16[8,16,1024]{2,1,0:T(8,128)(2,1)S(1)} collective-permute-done((bf16[8,16,1024]{2,1,0:T(8,128)(2,1)}, bf16[8,16,1024]{2,1,0:T(8,128)(2,1)S(1)}, u32[]{:S(2)}, u32[]{:S(2)}) %collective-permute-start.2) | collective-permute-done | bytes 262176 | tf_op jit(solution)/shard_map/ppermute | solution.py:406
  47.8 9.0 %collective-permute-done.3.refs_4_ = bf16[8,16,1024]{2,1,0:T(8,128)(2,1)S(1)} collective-permute-done((bf16[8,16,1024]{2,1,0:T(8,128)(2,1)}, bf16[8,16,1024]{2,1,0:T(8,128)(2,1)S(1)}, u32[]{:S(2)}, u32[]{:S(2)}) %collective-permute-start.3) | collective-permute-done | bytes 262176 | tf_op jit(solution)/shard_map/ppermute | solution.py:406
  56.9 20.9 %burn_in.1 = bf16[8,2,16,512]{3,2,1,0:T(8,128)(2,1)} custom-call(s32[3]{0:T(128)S(1)} %pad_add_fusion.place, s32[1]{0:T(128)} %get-tuple-element.62.crowded, bf16[1024,1024]{1,0:T(8,128)(2,1)} %bitcast.8.rows_hbm, bf16[1024,1024]{1,0:T(8,128)(2,1)} %copy-done.3, bf16[1024,2048]{1,0:T(8,128)(2,1)} %win_hbm.1, bf16[512,2048]{1,0:T(8,128)(2,1)} %wh_hbm.1, ...), custom_call_target="tpu_custom_call" | custom-call | flops 30000001024 | bytes 8388608 | tf_op jit(solution)/shard_map/burn_in/pallas_call | solution.py:277
  77.8 5.1 %all-to-all-start.2 = ((bf16[8,2,16,512]{3,2,1,0:T(8,128)(2,1)}), bf16[8,2,16,512]{3,2,1,0:T(8,128)(2,1)S(1)}, u32[]{:S(2)}, u32[]{:S(2)}) async-start(bf16[8,2,16,512]{3,2,1,0:T(8,128)(2,1)} %burn_in.1), calls=%async_computation.2 | async-start | bytes 524288 | tf_op jit(solution)/shard_map/all_to_all | solution.py:422
  82.9 5.9 %collective-permute-start.10 = (bf16[8,16,1024]{2,1,0:T(8,128)(2,1)}, bf16[8,16,1024]{2,1,0:T(8,128)(2,1)S(1)}, u32[]{:S(2)}, u32[]{:S(2)}) collective-permute-start(bf16[8,16,1024]{2,1,0:T(8,128)(2,1)} %get-tuple-element.54), channel_id=1, source_target_pairs={{0,15},{1,12},{2,13},{3,14},{4,3},{5,0},{6,1},{7,2},{8,7},{9,4},{1... | collective-permute-start | bytes 786440 | tf_op jit(solution)/shard_map/ppermute | solution.py:406
  88.8 2.7 %collective-permute-start.12 = (bf16[8,16,1024]{2,1,0:T(8,128)(2,1)}, bf16[8,16,1024]{2,1,0:T(8,128)(2,1)}, u32[]{:S(2)}, u32[]{:S(2)}) collective-permute-start(bf16[8,16,1024]{2,1,0:T(8,128)(2,1)} %get-tuple-element.56), channel_id=1, source_target_pairs={{0,3},{1,0},{2,1},{3,2},{4,7},{5,4},{6,5},{7,6},{8,11},{9,8},{10,9... | collective-permute-start | bytes 786440 | tf_op jit(solution)/shard_map/ppermute | solution.py:406
  91.5 1.5 %collective-permute-start.13 = (bf16[8,16,1024]{2,1,0:T(8,128)(2,1)}, bf16[8,16,1024]{2,1,0:T(8,128)(2,1)}, u32[]{:S(2)}, u32[]{:S(2)}) collective-permute-start(bf16[8,16,1024]{2,1,0:T(8,128)(2,1)} %get-tuple-element.57), channel_id=1, source_target_pairs={{0,4},{1,5},{2,6},{3,7},{4,8},{5,9},{6,10},{7,11},{8,12},{9,13},{1... | collective-permute-start | bytes 786440 | tf_op jit(solution)/shard_map/ppermute | solution.py:406
  93.1 1.1 %collective-permute-start.14 = (bf16[8,16,1024]{2,1,0:T(8,128)(2,1)}, bf16[8,16,1024]{2,1,0:T(8,128)(2,1)}, u32[]{:S(2)}, u32[]{:S(2)}) collective-permute-start(bf16[8,16,1024]{2,1,0:T(8,128)(2,1)} %get-tuple-element.58), channel_id=1, source_target_pairs={{0,12},{1,13},{2,14},{3,15},{4,0},{5,1},{6,2},{7,3},{8,4},{9,5},{1... | collective-permute-start | bytes 786440 | tf_op jit(solution)/shard_map/ppermute | solution.py:406
  94.2 1.0 learner_order.1
  95.2 5.2 %all-to-all-start.3 = ((bf16[16,8,1152]{2,1,0:T(8,128)(2,1)}), bf16[16,8,1152]{2,1,0:T(8,128)(2,1)S(1)}, u32[]{:S(2)}, u32[]{:S(2)}) async-start(bf16[16,8,1152]{2,1,0:T(8,128)(2,1)} %bitcast.12), calls=%async_computation.3 | async-start | bytes 589824 | tf_op jit(solution)/shard_map/all_to_all | solution.py:426
  100.4 1.6 %collective-permute-done.12.refs_13_ = bf16[8,16,1024]{2,1,0:T(8,128)(2,1)} collective-permute-done((bf16[8,16,1024]{2,1,0:T(8,128)(2,1)}, bf16[8,16,1024]{2,1,0:T(8,128)(2,1)}, u32[]{:S(2)}, u32[]{:S(2)}) %collective-permute-start.12) | collective-permute-done | bytes 262176 | tf_op jit(solution)/shard_map/ppermute | solution.py:406
  102.7 3.3 %place_rows.1 = bf16[128,16,1024]{2,1,0:T(8,128)(2,1)} custom-call(s32[3]{0:T(128)S(1)} %pad_add_fusion.place, bf16[8,16,1024]{2,1,0:T(8,128)(2,1)S(1)} %copy-done, bf16[8,16,1024]{2,1,0:T(8,128)(2,1)S(1)} %collective-permute-done.refs_1_, bf16[8,16,1024]{2,1,0:T(8,128)(2,1)S(1)} %collective-permute-done.1.refs_2_, ...), custom_call_target="tpu_custom_call" | custom-call | flops 1000000000 | bytes 8388608 | tf_op jit(solution)/shard_map/place_rows/pallas_call | solution.py:182
  106.0 2.1 %all-to-all-done.3 = bf16[16,8,1152]{2,1,0:T(8,128)(2,1)S(1)} async-done(((bf16[16,8,1152]{2,1,0:T(8,128)(2,1)}), bf16[16,8,1152]{2,1,0:T(8,128)(2,1)S(1)}, u32[]{:S(2)}, u32[]{:S(2)}) %all-to-all-start.3) | async-done | bytes 294944 | tf_op jit(solution)/shard_map/all_to_all | solution.py:426
  (45 shorter events, 3.4 us)
Async XLA Ops:
  5.2 6.1 %copy-start.2 = (bf16[64,16,1024]{2,1,0:T(8,128)(2,1)S(1)}, bf16[64,16,1024]{2,1,0:T(8,128)(2,1)}, u32[]{:S(2)}) copy-start(bf16[64,16,1024]{2,1,0:T(8,128)(2,1)} %obs_hbm.1) | copy-start | bytes 6291460
  5.3 32.4 %all-to-all-start.1 = ((bf16[8,128,1024]{2,1,0:T(8,128)(2,1)}), bf16[8,128,1024]{2,1,0:T(8,128)(2,1)}, u32[]{:S(2)}, u32[]{:S(2)}) async-start(bf16[8,128,1024]{2,1,0:T(8,128)(2,1)} %get-tuple-element.60), calls=%async_computation.1 | async-start | bytes 4194304 | tf_op jit(solution)/shard_map/all_to_all | solution.py:387
  11.4 17.9 %copy-start.8 = (s32[128]{0:T(128)S(1)}, s32[128]{0:T(128)}, u32[]{:S(2)}) copy-start(s32[128]{0:T(128)} %param.17) | copy-start | bytes 1540
  11.4 17.9 %copy-start.4 = (f32[2048]{0:T(1024)S(1)}, f32[2048]{0:T(1024)}, u32[]{:S(2)}) copy-start(f32[2048]{0:T(1024)} %param.13) | copy-start | bytes 24580
  11.4 17.9 %copy-start.5 = (f32[512]{0:T(512)S(1)}, f32[512]{0:T(512)}, u32[]{:S(2)}) copy-start(f32[512]{0:T(512)} %param.14) | copy-start | bytes 6148
  14.2 24.2 %collective-permute-start = (bf16[8,16,1024]{2,1,0:T(8,128)(2,1)}, bf16[8,16,1024]{2,1,0:T(8,128)(2,1)S(1)}, u32[]{:S(2)}, u32[]{:S(2)}) collective-permute-start(bf16[8,16,1024]{2,1,0:T(8,128)(2,1)} %get-tuple-element.44), channel_id=1, source_target_pairs={{0,10},{1,11},{2,8},{3,9},{4,14},{5,15},{6,12},{7,13},{8,2},{9,3},... | collective-permute-start | bytes 786440 | tf_op jit(solution)/shard_map/ppermute | solution.py:406
  20.3 23.0 %collective-permute-start.1 = (bf16[8,16,1024]{2,1,0:T(8,128)(2,1)}, bf16[8,16,1024]{2,1,0:T(8,128)(2,1)S(1)}, u32[]{:S(2)}, u32[]{:S(2)}) collective-permute-start(bf16[8,16,1024]{2,1,0:T(8,128)(2,1)} %get-tuple-element.45), channel_id=1, source_target_pairs={{0,6},{1,7},{2,4},{3,5},{4,10},{5,11},{6,8},{7,9},{8,14},{9,15},{1... | collective-permute-start | bytes 786440 | tf_op jit(solution)/shard_map/ppermute | solution.py:406
  20.3 27.1 %collective-permute-start.2 = (bf16[8,16,1024]{2,1,0:T(8,128)(2,1)}, bf16[8,16,1024]{2,1,0:T(8,128)(2,1)S(1)}, u32[]{:S(2)}, u32[]{:S(2)}) collective-permute-start(bf16[8,16,1024]{2,1,0:T(8,128)(2,1)} %get-tuple-element.46), channel_id=1, source_target_pairs={{0,9},{1,10},{2,11},{3,8},{4,13},{5,14},{6,15},{7,12},{8,1},{9,2},... | collective-permute-start | bytes 786440 | tf_op jit(solution)/shard_map/ppermute | solution.py:406
  22.8 34.1 %collective-permute-start.3 = (bf16[8,16,1024]{2,1,0:T(8,128)(2,1)}, bf16[8,16,1024]{2,1,0:T(8,128)(2,1)S(1)}, u32[]{:S(2)}, u32[]{:S(2)}) collective-permute-start(bf16[8,16,1024]{2,1,0:T(8,128)(2,1)} %get-tuple-element.47), channel_id=1, source_target_pairs={{0,11},{1,8},{2,9},{3,10},{4,15},{5,12},{6,13},{7,14},{8,3},{9,0},... | collective-permute-start | bytes 786440 | tf_op jit(solution)/shard_map/ppermute | solution.py:406
  25.4 31.5 %collective-permute-start.4 = (bf16[8,16,1024]{2,1,0:T(8,128)(2,1)}, bf16[8,16,1024]{2,1,0:T(8,128)(2,1)S(1)}, u32[]{:S(2)}, u32[]{:S(2)}) collective-permute-start(bf16[8,16,1024]{2,1,0:T(8,128)(2,1)} %get-tuple-element.48), channel_id=1, source_target_pairs={{0,14},{1,15},{2,12},{3,13},{4,2},{5,3},{6,0},{7,1},{8,6},{9,7},{1... | collective-permute-start | bytes 786440 | tf_op jit(solution)/shard_map/ppermute | solution.py:406
  39.7 43.2 %collective-permute-start.5 = (bf16[8,16,1024]{2,1,0:T(8,128)(2,1)}, bf16[8,16,1024]{2,1,0:T(8,128)(2,1)S(1)}, u32[]{:S(2)}, u32[]{:S(2)}) collective-permute-start(bf16[8,16,1024]{2,1,0:T(8,128)(2,1)} %get-tuple-element.49), channel_id=1, source_target_pairs={{0,2},{1,3},{2,0},{3,1},{4,6},{5,7},{6,4},{7,5},{8,10},{9,11},{10,... | collective-permute-start | bytes 786440 | tf_op jit(solution)/shard_map/ppermute | solution.py:406
  43.3 45.5 %collective-permute-start.6 = (bf16[8,16,1024]{2,1,0:T(8,128)(2,1)}, bf16[8,16,1024]{2,1,0:T(8,128)(2,1)S(1)}, u32[]{:S(2)}, u32[]{:S(2)}) collective-permute-start(bf16[8,16,1024]{2,1,0:T(8,128)(2,1)} %get-tuple-element.50), channel_id=1, source_target_pairs={{0,5},{1,6},{2,7},{3,4},{4,9},{5,10},{6,11},{7,8},{8,13},{9,14},{1... | collective-permute-start | bytes 786440 | tf_op jit(solution)/shard_map/ppermute | solution.py:406
  47.5 41.4 %collective-permute-start.7 = (bf16[8,16,1024]{2,1,0:T(8,128)(2,1)}, bf16[8,16,1024]{2,1,0:T(8,128)(2,1)S(1)}, u32[]{:S(2)}, u32[]{:S(2)}) collective-permute-start(bf16[8,16,1024]{2,1,0:T(8,128)(2,1)} %get-tuple-element.51), channel_id=1, source_target_pairs={{0,7},{1,4},{2,5},{3,6},{4,11},{5,8},{6,9},{7,10},{8,15},{9,12},{1... | collective-permute-start | bytes 786440 | tf_op jit(solution)/shard_map/ppermute | solution.py:406
  56.9 34.7 %collective-permute-start.8 = (bf16[8,16,1024]{2,1,0:T(8,128)(2,1)}, bf16[8,16,1024]{2,1,0:T(8,128)(2,1)S(1)}, u32[]{:S(2)}, u32[]{:S(2)}) collective-permute-start(bf16[8,16,1024]{2,1,0:T(8,128)(2,1)} %get-tuple-element.52), channel_id=1, source_target_pairs={{0,8},{1,9},{2,10},{3,11},{4,12},{5,13},{6,14},{7,15},{8,0},{9,1},... | collective-permute-start | bytes 786440 | tf_op jit(solution)/shard_map/ppermute | solution.py:406
  56.9 36.2 %collective-permute-start.9 = (bf16[8,16,1024]{2,1,0:T(8,128)(2,1)}, bf16[8,16,1024]{2,1,0:T(8,128)(2,1)S(1)}, u32[]{:S(2)}, u32[]{:S(2)}) collective-permute-start(bf16[8,16,1024]{2,1,0:T(8,128)(2,1)} %get-tuple-element.53), channel_id=1, source_target_pairs={{0,13},{1,14},{2,15},{3,12},{4,1},{5,2},{6,3},{7,0},{8,5},{9,6},{1... | collective-permute-start | bytes 786440 | tf_op jit(solution)/shard_map/ppermute | solution.py:406
  56.9 37.3 %copy-start.1 = (s32[1,128]{1,0:T(1,128)S(1)}, s32[1,128]{1,0:T(1,128)}, u32[]{:S(2)}) copy-start(s32[1,128]{1,0:T(1,128)} %get-tuple-element.65.rank) | copy-start | bytes 1540
  56.9 45.8 %copy-start = (bf16[8,16,1024]{2,1,0:T(8,128)(2,1)S(1)}, bf16[8,16,1024]{2,1,0:T(8,128)(2,1)}, u32[]{:S(2)}) copy-start(bf16[8,16,1024]{2,1,0:T(8,128)(2,1)} %get-tuple-element.43.refs_0_) | copy-start | bytes 786436
  77.8 16.4 %all-to-all-start.2 = ((bf16[8,2,16,512]{3,2,1,0:T(8,128)(2,1)}), bf16[8,2,16,512]{3,2,1,0:T(8,128)(2,1)S(1)}, u32[]{:S(2)}, u32[]{:S(2)}) async-start(bf16[8,2,16,512]{3,2,1,0:T(8,128)(2,1)} %burn_in.1), calls=%async_computation.2 | async-start | bytes 524288 | tf_op jit(solution)/shard_map/all_to_all | solution.py:422
  82.9 17.5 %collective-permute-start.10 = (bf16[8,16,1024]{2,1,0:T(8,128)(2,1)}, bf16[8,16,1024]{2,1,0:T(8,128)(2,1)S(1)}, u32[]{:S(2)}, u32[]{:S(2)}) collective-permute-start(bf16[8,16,1024]{2,1,0:T(8,128)(2,1)} %get-tuple-element.54), channel_id=1, source_target_pairs={{0,15},{1,12},{2,13},{3,14},{4,3},{5,0},{6,1},{7,2},{8,7},{9,4},{1... | collective-permute-start | bytes 786440 | tf_op jit(solution)/shard_map/ppermute | solution.py:406
  88.8 11.6 %collective-permute-start.11 = (bf16[8,16,1024]{2,1,0:T(8,128)(2,1)}, bf16[8,16,1024]{2,1,0:T(8,128)(2,1)}, u32[]{:S(2)}, u32[]{:S(2)}) collective-permute-start(bf16[8,16,1024]{2,1,0:T(8,128)(2,1)} %get-tuple-element.55), channel_id=1, source_target_pairs={{0,1},{1,2},{2,3},{3,0},{4,5},{5,6},{6,7},{7,4},{8,9},{9,10},{10,1... | collective-permute-start | bytes 786440 | tf_op jit(solution)/shard_map/ppermute | solution.py:406
  88.8 13.2 %collective-permute-start.12 = (bf16[8,16,1024]{2,1,0:T(8,128)(2,1)}, bf16[8,16,1024]{2,1,0:T(8,128)(2,1)}, u32[]{:S(2)}, u32[]{:S(2)}) collective-permute-start(bf16[8,16,1024]{2,1,0:T(8,128)(2,1)} %get-tuple-element.56), channel_id=1, source_target_pairs={{0,3},{1,0},{2,1},{3,2},{4,7},{5,4},{6,5},{7,6},{8,11},{9,8},{10,9... | collective-permute-start | bytes 786440 | tf_op jit(solution)/shard_map/ppermute | solution.py:406
  91.5 10.5 %collective-permute-start.13 = (bf16[8,16,1024]{2,1,0:T(8,128)(2,1)}, bf16[8,16,1024]{2,1,0:T(8,128)(2,1)}, u32[]{:S(2)}, u32[]{:S(2)}) collective-permute-start(bf16[8,16,1024]{2,1,0:T(8,128)(2,1)} %get-tuple-element.57), channel_id=1, source_target_pairs={{0,4},{1,5},{2,6},{3,7},{4,8},{5,9},{6,10},{7,11},{8,12},{9,13},{1... | collective-permute-start | bytes 786440 | tf_op jit(solution)/shard_map/ppermute | solution.py:406
  93.1 9.6 %collective-permute-start.14 = (bf16[8,16,1024]{2,1,0:T(8,128)(2,1)}, bf16[8,16,1024]{2,1,0:T(8,128)(2,1)}, u32[]{:S(2)}, u32[]{:S(2)}) collective-permute-start(bf16[8,16,1024]{2,1,0:T(8,128)(2,1)} %get-tuple-element.58), channel_id=1, source_target_pairs={{0,12},{1,13},{2,14},{3,15},{4,0},{5,1},{6,2},{7,3},{8,4},{9,5},{1... | collective-permute-start | bytes 786440 | tf_op jit(solution)/shard_map/ppermute | solution.py:406
  95.2 12.9 %all-to-all-start.3 = ((bf16[16,8,1152]{2,1,0:T(8,128)(2,1)}), bf16[16,8,1152]{2,1,0:T(8,128)(2,1)S(1)}, u32[]{:S(2)}, u32[]{:S(2)}) async-start(bf16[16,8,1152]{2,1,0:T(8,128)(2,1)} %bitcast.12), calls=%async_computation.3 | async-start | bytes 589824 | tf_op jit(solution)/shard_map/all_to_all | solution.py:426
  (3 other events, 13.6 us)

commit v6 on v5

--- a/solution.py
+++ b/solution.py
@@ -192,17 +192,35 @@
 
 
 def burn_in_kernel(
-    place, crowded, rows_hbm, more_hbm, win_hbm, wh_hbm, bias_ref, starts_ref, out_ref, xs, hot, x, proj, win, wh, pair, sem, out_sem
+    place, crowded, rows_hbm, more_hbm, win_hbm, wh_hbm, bias_ref, forget_ref, starts_ref, out_ref, xs, hot, x, proj, win, wh, pair, sem, out_sem
 ):
     copies, _, count, hidden_width = out_ref.shape
     shards = starts_ref.shape[0]
     shard_steps = STEPS // shards
-    rows_copy = pltpu.make_async_copy(rows_hbm, xs, sem.at[0])
-    rows_copy.start()
-    win_copy = pltpu.make_async_copy(win_hbm, win, sem.at[2])
-    wh_copy = pltpu.make_async_copy(wh_hbm, wh, sem.at[3])
-    win_copy.start()
-    wh_copy.start()
+
+    def fetches(array, to, which):
+        pieces = sem.shape[1]
+        size = array.shape[0] // pieces
+        at = [pl.ds(n * size, size) for n in range(pieces)]
+        return [
+            pltpu.make_async_copy(array.at[at[n]], to.at[at[n]], sem.at[which, n])
+            for n in range(pieces)
+        ]
+
+    def start(copies):
+        for copy in copies:
+            copy.start()
+
+    def wait(copies):
+        for copy in copies:
+            copy.wait()
+
+    rows_copies = fetches(rows_hbm, xs, 0)
+    win_copies = fetches(win_hbm, win, 2)
+    wh_copies = fetches(wh_hbm, wh, 3)
+    start(rows_copies)
+    start(win_copies)
+    start(wh_copies)
 
     mine = jnp.where(iota((shards, count), 0) == place[0], starts_ref[...], 0).astype(jnp.float32)
     mine = jnp.sum(mine, axis=0, keepdims=True)
@@ -225,20 +243,23 @@
                 hot[t * count : (t + 1) * count, shard * ROOM : (shard + 1) * ROOM] = one_hot(step == t)
 
     select(0)
-    rows_copy.wait()
+    wait(rows_copies)
     x[...] = f32_dot(hot[...], xs[...]).astype(jnp.bfloat16)
 
     @pl.when(crowded[0] > 0)
     def _():
-        more_copy = pltpu.make_async_copy(more_hbm, xs, sem.at[1])
-        more_copy.start()
+        more_copies = fetches(more_hbm, xs, 1)
+        start(more_copies)
         select(ROOM)
-        more_copy.wait()
+        wait(more_copies)
         x[...] += f32_dot(hot[...], xs[...]).astype(jnp.bfloat16)
 
-    win_copy.wait()
-    proj[...] = f32_dot(x[...], win[...]) + bias_ref[...]
-    wh_copy.wait()
+    wait(win_copies)
+    bias = bias_ref[...]
+    forget_bias = bias[:, hidden_width : 2 * hidden_width] + forget_ref[...]
+    bias = jnp.concatenate([bias[:, :hidden_width], forget_bias, bias[:, 2 * hidden_width :]], axis=1)
+    proj[...] = f32_dot(x[...], win[...]) + bias
+    wait(wh_copies)
     half = hidden_width // 2
 
     def step(t, state_pair):
@@ -269,7 +290,7 @@
         copy.wait()
 
 
-def burn_in(place, crowded, rows, more, input_weight, hidden_weight, bias, starts):
+def burn_in(place, crowded, rows, more, input_weight, hidden_weight, gate_bias, forget_bias, starts):
     shards, count = starts.shape
     width = input_weight.shape[0]
     hidden_width = hidden_weight.shape[0]
@@ -277,7 +298,7 @@
     return pl.pallas_call(
         burn_in_kernel,
         out_shape=jax.ShapeDtypeStruct((shards, 2, count, hidden_width), jnp.bfloat16),
-        in_specs=[SMEM, SMEM, HBM, HBM, HBM, HBM, VMEM, VMEM],
+        in_specs=[SMEM, SMEM, HBM, HBM, HBM, HBM, VMEM, VMEM, VMEM],
         out_specs=HBM,
         scratch_shapes=[
             pltpu.VMEM((shards * ROOM, width), jnp.bfloat16),
@@ -287,7 +308,7 @@
             pltpu.VMEM(input_weight.shape, jnp.bfloat16),
             pltpu.VMEM(hidden_weight.shape, jnp.bfloat16),
             pltpu.VMEM((2, count, hidden_width), jnp.bfloat16),
-            pltpu.SemaphoreType.DMA((4,)),
+            pltpu.SemaphoreType.DMA((4, 8)),
             pltpu.SemaphoreType.DMA((shards,)),
         ],
         compiler_params=pltpu.CompilerParams(vmem_limit_bytes=58 * MIB),
@@ -295,7 +316,7 @@
             flops=30_000_000_000, bytes_accessed=8 * MIB, transcendentals=0
         ),
         name="burn_in",
-    )(place, crowded, rows, more, input_weight, hidden_weight, bias, starts)
+    )(place, crowded, rows, more, input_weight, hidden_weight, gate_bias[None, :], forget_bias[None, :], starts)
 
 
 def unwritten_kernel(out):
@@ -405,12 +426,8 @@
         ]
         moved_rows.append(lax.ppermute(sent_rows[n], EP, ring))
 
-    blank = jnp.zeros((hidden_width,), jnp.float32)
-    bias = (gate_bias + jnp.concatenate([blank, forget_bias, blank, blank]))[None, :]
-
     raw_weight = jnp.exp(-IMPORTANCE * jnp.log(priorities.astype(jnp.float32))).astype(jnp.bfloat16)
     raw_row = raw_weight.astype(jnp.float32)[None, :]
-    bias, raw_row = lax.optimization_barrier((bias, raw_row))
 
     rows_in, again = lax.optimization_barrier((rows_in, crowded))
     more = lax.cond(
@@ -418,7 +435,9 @@
         lambda: exchanged(ROOM)[0],
         lambda: unwritten(rows_in.shape, rows_in.dtype),
     )
-    pairs = burn_in(place, crowded, rows_in, more, input_weight, hidden_weight, bias, starts)
+    pairs = burn_in(
+        place, crowded, rows_in, more, input_weight, hidden_weight, gate_bias, forget_bias, starts
+    )
     pairs = lax.all_to_all(pairs, "tm", split_axis=0, concat_axis=0, tiled=True)
     rows = placed(grid, [0] + order, place, moved_rows)
     both = ordered(pairs, rank_row, raw_row)

time: 111 us -> 111 us (level)
  transfers between devices with their start and end apart: 18 -> 18, of which waited for: 6 -> 6; matrix products, arithmetic and copies ran while one was open for 1% -> 0% of each run, Pallas kernels for 26% -> 26%
where the time goes in v6:
time: 111 us; the launch traced here: 110 us
  starting transfers between devices  48.4 us (44%)
  Pallas kernels  33.4 us (30%)
  waiting for transfers between devices  24.3 us (22%)
  local copies, waits for them, and re-layouts  2.25 us (2%)
  between operations  1.48 us (1%)
    ppermute x15, starting transfers between devices, body(): moved_rows.append(lax.ppermute(sent_rows[n], EP, ring))  32 us
    pallas_call x1, Pallas kernels, burn_in(): pl.pallas_call(burn_in_kernel, out_shape=jax.ShapeDtypeStruct((shards, 2,...  21.1 us
    ppermute x15, waiting for transfers between devices, body(): moved_rows.append(lax.ppermute(sent_rows[n], EP, ring))  13.7 us
    all_to_all x1, waiting for transfers between devices, exchanged(): rows = lax.all_to_all(sent, 'tm', split_axis=0, concat_axis=0, tiled=True)  8.47 us
    all_to_all x1, starting transfers between devices, exchanged(): rows = lax.all_to_all(sent, 'tm', split_axis=0, concat_axis=0, tiled=True)  6.1 us
    all_to_all x1, starting transfers between devices, body(): both = lax.all_to_all(both, EP, split_axis=0, concat_axis=0, tiled=True)  5.16 us
    all_to_all x1, starting transfers between devices, body(): pairs = lax.all_to_all(pairs, 'tm', split_axis=0, concat_axis=0, tiled=True)  5.11 us
    pallas_call x1, Pallas kernels, pack(): pl.pallas_call(functools.partial(pack_kernel, base), out_shape=(jax.Shape...  4.51 us
  transfers between devices with their start and end apart: 18, of which 6 were waited for; matrix products, arithmetic and copies ran while one was open for 0% of the time, Pallas kernels for 26%

profile of v6, /device:TPU:1, one launch (start us, length us, event | category | flops | bytes accessed | tf_op | source)
XLA Modules:
  0.0 109.9 jit_solution(13400039786933231554)
XLA Ops:
  0.7 4.5 %pack_rows.3 = (bf16[8,128,1024]{2,1,0:T(8,128)(2,1)}, s32[1]{0:T(128)}, s32[8,16]{1,0:T(8,128)}, s32[1,128]{1,0:T(1,128)}) custom-call(s32[3]{0:T(128)S(1)} %pad_add_fusion.place, s32[1,128]{1,0:T(1,128)} %bitcast.20, s32[1,128]{1,0:T(1,128)} %bitcast.22, bf16[64,16,1024]{2,1,0:T(8,128)(2,1)} %obs_hbm.1), custom_call_target="tpu_custom_call" | custom-call | flops 1000000000 | bytes 4194304 | tf_op jit(solution)/shard_map/pack_rows/pallas_call | solution.py:99
  5.3 6.1 %all-to-all-start.1 = ((bf16[8,128,1024]{2,1,0:T(8,128)(2,1)}), bf16[8,128,1024]{2,1,0:T(8,128)(2,1)}, u32[]{:S(2)}, u32[]{:S(2)}) async-start(bf16[8,128,1024]{2,1,0:T(8,128)(2,1)} %get-tuple-element.58), calls=%async_computation.1 | async-start | bytes 4194304 | tf_op jit(solution)/shard_map/all_to_all | solution.py:408
  11.4 2.7 %masked_rows.1 = (bf16[8,16,1024]{2,1,0:T(8,128)(2,1)}, bf16[8,16,1024]{2,1,0:T(8,128)(2,1)}, bf16[8,16,1024]{2,1,0:T(8,128)(2,1)}, bf16[8,16,1024]{2,1,0:T(8,12...) custom-call(s32[3]{0:T(128)S(1)} %pad_add_fusion.place, ...), custom_call_target="tpu_custom_call" | custom-call | flops 100000000 | bytes 6291456 | tf_op jit(solution)/shard_map/masked_rows/pallas_call | solution.py:150
  14.1 6.1 %collective-permute-start = (bf16[8,16,1024]{2,1,0:T(8,128)(2,1)}, bf16[8,16,1024]{2,1,0:T(8,128)(2,1)S(1)}, u32[]{:S(2)}, u32[]{:S(2)}) collective-permute-start(bf16[8,16,1024]{2,1,0:T(8,128)(2,1)} %get-tuple-element.42), channel_id=1, source_target_pairs={{0,10},{1,11},{2,8},{3,9},{4,14},{5,15},{6,12},{7,13},{8,2},{9,3},... | collective-permute-start | bytes 786440 | tf_op jit(solution)/shard_map/ppermute | solution.py:427
  20.3 2.5 %collective-permute-start.2 = (bf16[8,16,1024]{2,1,0:T(8,128)(2,1)}, bf16[8,16,1024]{2,1,0:T(8,128)(2,1)S(1)}, u32[]{:S(2)}, u32[]{:S(2)}) collective-permute-start(bf16[8,16,1024]{2,1,0:T(8,128)(2,1)} %get-tuple-element.44), channel_id=1, source_target_pairs={{0,9},{1,10},{2,11},{3,8},{4,13},{5,14},{6,15},{7,12},{8,1},{9,2},... | collective-permute-start | bytes 786440 | tf_op jit(solution)/shard_map/ppermute | solution.py:427
  22.7 2.6 %collective-permute-start.3 = (bf16[8,16,1024]{2,1,0:T(8,128)(2,1)}, bf16[8,16,1024]{2,1,0:T(8,128)(2,1)S(1)}, u32[]{:S(2)}, u32[]{:S(2)}) collective-permute-start(bf16[8,16,1024]{2,1,0:T(8,128)(2,1)} %get-tuple-element.45), channel_id=1, source_target_pairs={{0,11},{1,8},{2,9},{3,10},{4,15},{5,12},{6,13},{7,14},{8,3},{9,0},... | collective-permute-start | bytes 786440 | tf_op jit(solution)/shard_map/ppermute | solution.py:427
  25.3 3.9 %collective-permute-start.4 = (bf16[8,16,1024]{2,1,0:T(8,128)(2,1)}, bf16[8,16,1024]{2,1,0:T(8,128)(2,1)S(1)}, u32[]{:S(2)}, u32[]{:S(2)}) collective-permute-start(bf16[8,16,1024]{2,1,0:T(8,128)(2,1)} %get-tuple-element.46), channel_id=1, source_target_pairs={{0,14},{1,15},{2,12},{3,13},{4,2},{5,3},{6,0},{7,1},{8,6},{9,7},{1... | collective-permute-start | bytes 786440 | tf_op jit(solution)/shard_map/ppermute | solution.py:427
  29.2 8.5 %all-to-all-done.1 = bf16[8,128,1024]{2,1,0:T(8,128)(2,1)} async-done(((bf16[8,128,1024]{2,1,0:T(8,128)(2,1)}), bf16[8,128,1024]{2,1,0:T(8,128)(2,1)}, u32[]{:S(2)}, u32[]{:S(2)}) %all-to-all-start.1) | async-done | bytes 2097184 | tf_op jit(solution)/shard_map/all_to_all | solution.py:408
  38.4 1.3 %copy-done.3 = bf16[1024,1024]{1,0:T(8,128)(2,1)} copy-done((bf16[1024,1024]{1,0:T(8,128)(2,1)}, bf16[1024,1024]{1,0:T(8,128)(2,1)S(1)}, u32[]{:S(2)}) %copy-start.3) | copy-done | bytes 2097176
  39.7 3.6 %collective-permute-start.5 = (bf16[8,16,1024]{2,1,0:T(8,128)(2,1)}, bf16[8,16,1024]{2,1,0:T(8,128)(2,1)S(1)}, u32[]{:S(2)}, u32[]{:S(2)}) collective-permute-start(bf16[8,16,1024]{2,1,0:T(8,128)(2,1)} %get-tuple-element.47), channel_id=1, source_target_pairs={{0,2},{1,3},{2,0},{3,1},{4,6},{5,7},{6,4},{7,5},{8,10},{9,11},{10,... | collective-permute-start | bytes 786440 | tf_op jit(solution)/shard_map/ppermute | solution.py:427
  43.3 1.7 %collective-permute-start.6 = (bf16[8,16,1024]{2,1,0:T(8,128)(2,1)}, bf16[8,16,1024]{2,1,0:T(8,128)(2,1)S(1)}, u32[]{:S(2)}, u32[]{:S(2)}) collective-permute-start(bf16[8,16,1024]{2,1,0:T(8,128)(2,1)} %get-tuple-element.48), channel_id=1, source_target_pairs={{0,5},{1,6},{2,7},{3,4},{4,9},{5,10},{6,11},{7,8},{8,13},{9,14},{1... | collective-permute-start | bytes 786440 | tf_op jit(solution)/shard_map/ppermute | solution.py:427
  45.0 2.5 %collective-permute-done.2.refs_3_ = bf16[8,16,1024]{2,1,0:T(8,128)(2,1)S(1)} collective-permute-done((bf16[8,16,1024]{2,1,0:T(8,128)(2,1)}, bf16[8,16,1024]{2,1,0:T(8,128)(2,1)S(1)}, u32[]{:S(2)}, u32[]{:S(2)}) %collective-permute-start.2) | collective-permute-done | bytes 262176 | tf_op jit(solution)/shard_map/ppermute | solution.py:427
  47.8 9.0 %collective-permute-done.3.refs_4_ = bf16[8,16,1024]{2,1,0:T(8,128)(2,1)S(1)} collective-permute-done((bf16[8,16,1024]{2,1,0:T(8,128)(2,1)}, bf16[8,16,1024]{2,1,0:T(8,128)(2,1)S(1)}, u32[]{:S(2)}, u32[]{:S(2)}) %collective-permute-start.3) | collective-permute-done | bytes 262176 | tf_op jit(solution)/shard_map/ppermute | solution.py:427
  56.8 21.1 %burn_in.1 = bf16[8,2,16,512]{3,2,1,0:T(8,128)(2,1)} custom-call(s32[3]{0:T(128)S(1)} %pad_add_fusion.place, s32[1]{0:T(128)} %get-tuple-element.60.crowded, bf16[1024,1024]{1,0:T(8,128)(2,1)} %bitcast.8.rows_hbm, bf16[1024,1024]{1,0:T(8,128)(2,1)} %copy-done.3, bf16[1024,2048]{1,0:T(8,128)(2,1)} %win_hbm.1, bf16[512,2048]{1,0:T(8,128)(2,1)} %wh_hbm.1, ...), custom_call_target="tpu_custom_call" | custom-call | flops 30000001024 | bytes 8388608 | tf_op jit(solution)/shard_map/burn_in/pallas_call | solution.py:298
  78.0 5.1 %all-to-all-start.2 = ((bf16[8,2,16,512]{3,2,1,0:T(8,128)(2,1)}), bf16[8,2,16,512]{3,2,1,0:T(8,128)(2,1)S(1)}, u32[]{:S(2)}, u32[]{:S(2)}) async-start(bf16[8,2,16,512]{3,2,1,0:T(8,128)(2,1)} %burn_in.1), calls=%async_computation.2 | async-start | bytes 524288 | tf_op jit(solution)/shard_map/all_to_all | solution.py:441
  83.1 5.9 %collective-permute-start.10 = (bf16[8,16,1024]{2,1,0:T(8,128)(2,1)}, bf16[8,16,1024]{2,1,0:T(8,128)(2,1)S(1)}, u32[]{:S(2)}, u32[]{:S(2)}) collective-permute-start(bf16[8,16,1024]{2,1,0:T(8,128)(2,1)} %get-tuple-element.52), channel_id=1, source_target_pairs={{0,15},{1,12},{2,13},{3,14},{4,3},{5,0},{6,1},{7,2},{8,7},{9,4},{1... | collective-permute-start | bytes 786440 | tf_op jit(solution)/shard_map/ppermute | solution.py:427
  89.0 2.7 %collective-permute-start.12 = (bf16[8,16,1024]{2,1,0:T(8,128)(2,1)}, bf16[8,16,1024]{2,1,0:T(8,128)(2,1)}, u32[]{:S(2)}, u32[]{:S(2)}) collective-permute-start(bf16[8,16,1024]{2,1,0:T(8,128)(2,1)} %get-tuple-element.54), channel_id=1, source_target_pairs={{0,3},{1,0},{2,1},{3,2},{4,7},{5,4},{6,5},{7,6},{8,11},{9,8},{10,9... | collective-permute-start | bytes 786440 | tf_op jit(solution)/shard_map/ppermute | solution.py:427
  91.7 1.6 %collective-permute-start.13 = (bf16[8,16,1024]{2,1,0:T(8,128)(2,1)}, bf16[8,16,1024]{2,1,0:T(8,128)(2,1)}, u32[]{:S(2)}, u32[]{:S(2)}) collective-permute-start(bf16[8,16,1024]{2,1,0:T(8,128)(2,1)} %get-tuple-element.55), channel_id=1, source_target_pairs={{0,4},{1,5},{2,6},{3,7},{4,8},{5,9},{6,10},{7,11},{8,12},{9,13},{1... | collective-permute-start | bytes 786440 | tf_op jit(solution)/shard_map/ppermute | solution.py:427
  93.3 1.1 %collective-permute-start.14 = (bf16[8,16,1024]{2,1,0:T(8,128)(2,1)}, bf16[8,16,1024]{2,1,0:T(8,128)(2,1)}, u32[]{:S(2)}, u32[]{:S(2)}) collective-permute-start(bf16[8,16,1024]{2,1,0:T(8,128)(2,1)} %get-tuple-element.56), channel_id=1, source_target_pairs={{0,12},{1,13},{2,14},{3,15},{4,0},{5,1},{6,2},{7,3},{8,4},{9,5},{1... | collective-permute-start | bytes 786440 | tf_op jit(solution)/shard_map/ppermute | solution.py:427
  94.4 1.0 learner_order.1
  95.4 5.2 %all-to-all-start.3 = ((bf16[16,8,1152]{2,1,0:T(8,128)(2,1)}), bf16[16,8,1152]{2,1,0:T(8,128)(2,1)S(1)}, u32[]{:S(2)}, u32[]{:S(2)}) async-start(bf16[16,8,1152]{2,1,0:T(8,128)(2,1)} %bitcast.13), calls=%async_computation.3 | async-start | bytes 589824 | tf_op jit(solution)/shard_map/all_to_all | solution.py:445
  100.6 1.6 %collective-permute-done.12.refs_13_ = bf16[8,16,1024]{2,1,0:T(8,128)(2,1)} collective-permute-done((bf16[8,16,1024]{2,1,0:T(8,128)(2,1)}, bf16[8,16,1024]{2,1,0:T(8,128)(2,1)}, u32[]{:S(2)}, u32[]{:S(2)}) %collective-permute-start.12) | collective-permute-done | bytes 262176 | tf_op jit(solution)/shard_map/ppermute | solution.py:427
  102.9 3.3 %place_rows.1 = bf16[128,16,1024]{2,1,0:T(8,128)(2,1)} custom-call(s32[3]{0:T(128)S(1)} %pad_add_fusion.place, bf16[8,16,1024]{2,1,0:T(8,128)(2,1)S(1)} %copy-done, bf16[8,16,1024]{2,1,0:T(8,128)(2,1)S(1)} %collective-permute-done.refs_1_, bf16[8,16,1024]{2,1,0:T(8,128)(2,1)S(1)} %collective-permute-done.1.refs_2_, ...), custom_call_target="tpu_custom_call" | custom-call | flops 1000000000 | bytes 8388608 | tf_op jit(solution)/shard_map/place_rows/pallas_call | solution.py:182
  106.2 2.1 %all-to-all-done.3 = bf16[16,8,1152]{2,1,0:T(8,128)(2,1)S(1)} async-done(((bf16[16,8,1152]{2,1,0:T(8,128)(2,1)}), bf16[16,8,1152]{2,1,0:T(8,128)(2,1)S(1)}, u32[]{:S(2)}, u32[]{:S(2)}) %all-to-all-start.3) | async-done | bytes 294944 | tf_op jit(solution)/shard_map/all_to_all | solution.py:445
  (38 shorter events, 2.8 us)
Async XLA Ops:
  5.2 6.1 %copy-start.2 = (bf16[64,16,1024]{2,1,0:T(8,128)(2,1)S(1)}, bf16[64,16,1024]{2,1,0:T(8,128)(2,1)}, u32[]{:S(2)}) copy-start(bf16[64,16,1024]{2,1,0:T(8,128)(2,1)} %obs_hbm.1) | copy-start | bytes 6291460
  5.2 6.1 %copy-start.4 = (s32[128]{0:T(128)S(1)}, s32[128]{0:T(128)}, u32[]{:S(2)}) copy-start(s32[128]{0:T(128)} %ids.1) | copy-start | bytes 1540
  5.3 6.1 %copy-start.5 = (s32[128]{0:T(128)S(1)}, s32[128]{0:T(128)}, u32[]{:S(2)}) copy-start(s32[128]{0:T(128)} %starts.1) | copy-start | bytes 1540
  5.3 32.4 %all-to-all-start.1 = ((bf16[8,128,1024]{2,1,0:T(8,128)(2,1)}), bf16[8,128,1024]{2,1,0:T(8,128)(2,1)}, u32[]{:S(2)}, u32[]{:S(2)}) async-start(bf16[8,128,1024]{2,1,0:T(8,128)(2,1)} %get-tuple-element.58), calls=%async_computation.1 | async-start | bytes 4194304 | tf_op jit(solution)/shard_map/all_to_all | solution.py:408
  14.1 24.3 %collective-permute-start = (bf16[8,16,1024]{2,1,0:T(8,128)(2,1)}, bf16[8,16,1024]{2,1,0:T(8,128)(2,1)S(1)}, u32[]{:S(2)}, u32[]{:S(2)}) collective-permute-start(bf16[8,16,1024]{2,1,0:T(8,128)(2,1)} %get-tuple-element.42), channel_id=1, source_target_pairs={{0,10},{1,11},{2,8},{3,9},{4,14},{5,15},{6,12},{7,13},{8,2},{9,3},... | collective-permute-start | bytes 786440 | tf_op jit(solution)/shard_map/ppermute | solution.py:427
  20.3 23.0 %collective-permute-start.1 = (bf16[8,16,1024]{2,1,0:T(8,128)(2,1)}, bf16[8,16,1024]{2,1,0:T(8,128)(2,1)S(1)}, u32[]{:S(2)}, u32[]{:S(2)}) collective-permute-start(bf16[8,16,1024]{2,1,0:T(8,128)(2,1)} %get-tuple-element.43), channel_id=1, source_target_pairs={{0,6},{1,7},{2,4},{3,5},{4,10},{5,11},{6,8},{7,9},{8,14},{9,15},{1... | collective-permute-start | bytes 786440 | tf_op jit(solution)/shard_map/ppermute | solution.py:427
  20.3 27.1 %collective-permute-start.2 = (bf16[8,16,1024]{2,1,0:T(8,128)(2,1)}, bf16[8,16,1024]{2,1,0:T(8,128)(2,1)S(1)}, u32[]{:S(2)}, u32[]{:S(2)}) collective-permute-start(bf16[8,16,1024]{2,1,0:T(8,128)(2,1)} %get-tuple-element.44), channel_id=1, source_target_pairs={{0,9},{1,10},{2,11},{3,8},{4,13},{5,14},{6,15},{7,12},{8,1},{9,2},... | collective-permute-start | bytes 786440 | tf_op jit(solution)/shard_map/ppermute | solution.py:427
  22.7 34.1 %collective-permute-start.3 = (bf16[8,16,1024]{2,1,0:T(8,128)(2,1)}, bf16[8,16,1024]{2,1,0:T(8,128)(2,1)S(1)}, u32[]{:S(2)}, u32[]{:S(2)}) collective-permute-start(bf16[8,16,1024]{2,1,0:T(8,128)(2,1)} %get-tuple-element.45), channel_id=1, source_target_pairs={{0,11},{1,8},{2,9},{3,10},{4,15},{5,12},{6,13},{7,14},{8,3},{9,0},... | collective-permute-start | bytes 786440 | tf_op jit(solution)/shard_map/ppermute | solution.py:427
  25.3 31.5 %collective-permute-start.4 = (bf16[8,16,1024]{2,1,0:T(8,128)(2,1)}, bf16[8,16,1024]{2,1,0:T(8,128)(2,1)S(1)}, u32[]{:S(2)}, u32[]{:S(2)}) collective-permute-start(bf16[8,16,1024]{2,1,0:T(8,128)(2,1)} %get-tuple-element.46), channel_id=1, source_target_pairs={{0,14},{1,15},{2,12},{3,13},{4,2},{5,3},{6,0},{7,1},{8,6},{9,7},{1... | collective-permute-start | bytes 786440 | tf_op jit(solution)/shard_map/ppermute | solution.py:427
  39.7 43.4 %collective-permute-start.5 = (bf16[8,16,1024]{2,1,0:T(8,128)(2,1)}, bf16[8,16,1024]{2,1,0:T(8,128)(2,1)S(1)}, u32[]{:S(2)}, u32[]{:S(2)}) collective-permute-start(bf16[8,16,1024]{2,1,0:T(8,128)(2,1)} %get-tuple-element.47), channel_id=1, source_target_pairs={{0,2},{1,3},{2,0},{3,1},{4,6},{5,7},{6,4},{7,5},{8,10},{9,11},{10,... | collective-permute-start | bytes 786440 | tf_op jit(solution)/shard_map/ppermute | solution.py:427
  43.3 45.7 %collective-permute-start.6 = (bf16[8,16,1024]{2,1,0:T(8,128)(2,1)}, bf16[8,16,1024]{2,1,0:T(8,128)(2,1)S(1)}, u32[]{:S(2)}, u32[]{:S(2)}) collective-permute-start(bf16[8,16,1024]{2,1,0:T(8,128)(2,1)} %get-tuple-element.48), channel_id=1, source_target_pairs={{0,5},{1,6},{2,7},{3,4},{4,9},{5,10},{6,11},{7,8},{8,13},{9,14},{1... | collective-permute-start | bytes 786440 | tf_op jit(solution)/shard_map/ppermute | solution.py:427
  47.4 41.6 %collective-permute-start.7 = (bf16[8,16,1024]{2,1,0:T(8,128)(2,1)}, bf16[8,16,1024]{2,1,0:T(8,128)(2,1)S(1)}, u32[]{:S(2)}, u32[]{:S(2)}) collective-permute-start(bf16[8,16,1024]{2,1,0:T(8,128)(2,1)} %get-tuple-element.49), channel_id=1, source_target_pairs={{0,7},{1,4},{2,5},{3,6},{4,11},{5,8},{6,9},{7,10},{8,15},{9,12},{1... | collective-permute-start | bytes 786440 | tf_op jit(solution)/shard_map/ppermute | solution.py:427
  56.8 34.9 %collective-permute-start.8 = (bf16[8,16,1024]{2,1,0:T(8,128)(2,1)}, bf16[8,16,1024]{2,1,0:T(8,128)(2,1)S(1)}, u32[]{:S(2)}, u32[]{:S(2)}) collective-permute-start(bf16[8,16,1024]{2,1,0:T(8,128)(2,1)} %get-tuple-element.50), channel_id=1, source_target_pairs={{0,8},{1,9},{2,10},{3,11},{4,12},{5,13},{6,14},{7,15},{8,0},{9,1},... | collective-permute-start | bytes 786440 | tf_op jit(solution)/shard_map/ppermute | solution.py:427
  56.8 36.4 %collective-permute-start.9 = (bf16[8,16,1024]{2,1,0:T(8,128)(2,1)}, bf16[8,16,1024]{2,1,0:T(8,128)(2,1)S(1)}, u32[]{:S(2)}, u32[]{:S(2)}) collective-permute-start(bf16[8,16,1024]{2,1,0:T(8,128)(2,1)} %get-tuple-element.51), channel_id=1, source_target_pairs={{0,13},{1,14},{2,15},{3,12},{4,1},{5,2},{6,3},{7,0},{8,5},{9,6},{1... | collective-permute-start | bytes 786440 | tf_op jit(solution)/shard_map/ppermute | solution.py:427
  56.8 37.6 %copy-start.6 = (s32[128]{0:T(128)S(1)}, s32[128]{0:T(128)}, u32[]{:S(2)}) copy-start(s32[128]{0:T(128)} %param.17) | copy-start | bytes 1540
  56.8 37.6 %copy-start.1 = (s32[1,128]{1,0:T(1,128)S(1)}, s32[1,128]{1,0:T(1,128)}, u32[]{:S(2)}) copy-start(s32[1,128]{1,0:T(1,128)} %get-tuple-element.62.rank) | copy-start | bytes 1540
  56.8 46.0 %copy-start = (bf16[8,16,1024]{2,1,0:T(8,128)(2,1)S(1)}, bf16[8,16,1024]{2,1,0:T(8,128)(2,1)}, u32[]{:S(2)}) copy-start(bf16[8,16,1024]{2,1,0:T(8,128)(2,1)} %get-tuple-element.41.refs_0_) | copy-start | bytes 786436
  78.0 16.4 %all-to-all-start.2 = ((bf16[8,2,16,512]{3,2,1,0:T(8,128)(2,1)}), bf16[8,2,16,512]{3,2,1,0:T(8,128)(2,1)S(1)}, u32[]{:S(2)}, u32[]{:S(2)}) async-start(bf16[8,2,16,512]{3,2,1,0:T(8,128)(2,1)} %burn_in.1), calls=%async_computation.2 | async-start | bytes 524288 | tf_op jit(solution)/shard_map/all_to_all | solution.py:441
  83.1 17.5 %collective-permute-start.10 = (bf16[8,16,1024]{2,1,0:T(8,128)(2,1)}, bf16[8,16,1024]{2,1,0:T(8,128)(2,1)S(1)}, u32[]{:S(2)}, u32[]{:S(2)}) collective-permute-start(bf16[8,16,1024]{2,1,0:T(8,128)(2,1)} %get-tuple-element.52), channel_id=1, source_target_pairs={{0,15},{1,12},{2,13},{3,14},{4,3},{5,0},{6,1},{7,2},{8,7},{9,4},{1... | collective-permute-start | bytes 786440 | tf_op jit(solution)/shard_map/ppermute | solution.py:427
  89.0 11.6 %collective-permute-start.11 = (bf16[8,16,1024]{2,1,0:T(8,128)(2,1)}, bf16[8,16,1024]{2,1,0:T(8,128)(2,1)}, u32[]{:S(2)}, u32[]{:S(2)}) collective-permute-start(bf16[8,16,1024]{2,1,0:T(8,128)(2,1)} %get-tuple-element.53), channel_id=1, source_target_pairs={{0,1},{1,2},{2,3},{3,0},{4,5},{5,6},{6,7},{7,4},{8,9},{9,10},{10,1... | collective-permute-start | bytes 786440 | tf_op jit(solution)/shard_map/ppermute | solution.py:427
  89.0 13.2 %collective-permute-start.12 = (bf16[8,16,1024]{2,1,0:T(8,128)(2,1)}, bf16[8,16,1024]{2,1,0:T(8,128)(2,1)}, u32[]{:S(2)}, u32[]{:S(2)}) collective-permute-start(bf16[8,16,1024]{2,1,0:T(8,128)(2,1)} %get-tuple-element.54), channel_id=1, source_target_pairs={{0,3},{1,0},{2,1},{3,2},{4,7},{5,4},{6,5},{7,6},{8,11},{9,8},{10,9... | collective-permute-start | bytes 786440 | tf_op jit(solution)/shard_map/ppermute | solution.py:427
  91.7 10.6 %collective-permute-start.13 = (bf16[8,16,1024]{2,1,0:T(8,128)(2,1)}, bf16[8,16,1024]{2,1,0:T(8,128)(2,1)}, u32[]{:S(2)}, u32[]{:S(2)}) collective-permute-start(bf16[8,16,1024]{2,1,0:T(8,128)(2,1)} %get-tuple-element.55), channel_id=1, source_target_pairs={{0,4},{1,5},{2,6},{3,7},{4,8},{5,9},{6,10},{7,11},{8,12},{9,13},{1... | collective-permute-start | bytes 786440 | tf_op jit(solution)/shard_map/ppermute | solution.py:427
  93.3 9.6 %collective-permute-start.14 = (bf16[8,16,1024]{2,1,0:T(8,128)(2,1)}, bf16[8,16,1024]{2,1,0:T(8,128)(2,1)}, u32[]{:S(2)}, u32[]{:S(2)}) collective-permute-start(bf16[8,16,1024]{2,1,0:T(8,128)(2,1)} %get-tuple-element.56), channel_id=1, source_target_pairs={{0,12},{1,13},{2,14},{3,15},{4,0},{5,1},{6,2},{7,3},{8,4},{9,5},{1... | collective-permute-start | bytes 786440 | tf_op jit(solution)/shard_map/ppermute | solution.py:427
  95.4 12.9 %all-to-all-start.3 = ((bf16[16,8,1152]{2,1,0:T(8,128)(2,1)}), bf16[16,8,1152]{2,1,0:T(8,128)(2,1)S(1)}, u32[]{:S(2)}, u32[]{:S(2)}) async-start(bf16[16,8,1152]{2,1,0:T(8,128)(2,1)} %bitcast.13), calls=%async_computation.3 | async-start | bytes 589824 | tf_op jit(solution)/shard_map/all_to_all | solution.py:445
  (1 other events, 1.3 us)

commit v7 on v6

--- a/solution.py
+++ b/solution.py
@@ -39,8 +39,13 @@
 def pack_kernel(
     base, place, ids_ref, starts_ref, obs_hbm, out, crowded, dealt, rank_ref, obs, ids_held, ids, rows_of, packed, sem, obs_sem
 ):
-    obs_copy = pltpu.make_async_copy(obs_hbm, obs, obs_sem.at[0])
-    obs_copy.start()
+    piece = obs.shape[0] // 8
+    pieces = [pl.ds(n * piece, piece) for n in range(8)]
+    obs_copies = [
+        pltpu.make_async_copy(obs_hbm.at[at], obs.at[at], obs_sem.at[n]) for n, at in enumerate(pieces)
+    ]
+    for copy in obs_copies:
+        copy.start()
     shards, count = dealt.shape
     total = shards * count
     shard_steps = obs.shape[1]
@@ -60,7 +65,7 @@
     taker = (column % count) * shards + column // count
     ids_row = jnp.where(whole_rank == taker, upright(ids_ref[...].astype(jnp.float32)), 0.0)
     ids_held[...] = jnp.sum(ids_row, axis=0, keepdims=True).astype(jnp.int32)
-    ids_copy = pltpu.make_async_copy(ids_held, ids, obs_sem.at[1])
+    ids_copy = pltpu.make_async_copy(ids_held, ids, obs_sem.at[8])
     ids_copy.start()
     to_shard = one_hot(iota((shards, total), 0) == rank_row.astype(jnp.int32) % shards)
     to_place = jnp.where(iota((total, count), 1) == whole_rank // shards, start_column, 0.0)
@@ -80,7 +85,8 @@
         most = jnp.maximum(most, f32_dot(some.astype(jnp.bfloat16), jnp.ones((lanes, lanes // 2), jnp.bfloat16)))
     crowded[0] = (jnp.max(most) > ROOM).astype(jnp.int32)
     ids_copy.wait()
-    obs_copy.wait()
+    for copy in obs_copies:
+        copy.wait()
     copies = [pltpu.make_async_copy(packed.at[k], out.at[k], sem.at[k]) for k in range(shards)]
     for k in range(shards):
         for i in range(count):
@@ -113,7 +119,7 @@
             pltpu.VMEM((shards, count * shard_steps, width), jnp.bfloat16),
             pltpu.VMEM((shards, ROOM, width), jnp.bfloat16),
             pltpu.SemaphoreType.DMA((shards,)),
-            pltpu.SemaphoreType.DMA((2,)),
+            pltpu.SemaphoreType.DMA((9,)),
         ],
         compiler_params=pltpu.CompilerParams(vmem_limit_bytes=58 * MIB),
         cost_estimate=pl.CostEstimate(flops=10**9, bytes_accessed=4 * MIB, transcendentals=0),

time: 111 us -> 111 us (level)
  no operation moved by 1% of the time
where the time goes in v7:
time: 111 us; the launch traced here: 110 us
  starting transfers between devices  48.4 us (44%)
  Pallas kernels  33.4 us (30%)
  waiting for transfers between devices  24.3 us (22%)
  local copies, waits for them, and re-layouts  2.25 us (2%)
  between operations  1.48 us (1%)
    ppermute x15, starting transfers between devices, body(): moved_rows.append(lax.ppermute(sent_rows[n], EP, ring))  32 us
    pallas_call x1, Pallas kernels, burn_in(): pl.pallas_call(burn_in_kernel, out_shape=jax.ShapeDtypeStruct((shards, 2,...  21.1 us
    ppermute x15, waiting for transfers between devices, body(): moved_rows.append(lax.ppermute(sent_rows[n], EP, ring))  13.8 us
    all_to_all x1, waiting for transfers between devices, exchanged(): rows = lax.all_to_all(sent, 'tm', split_axis=0, concat_axis=0, tiled=True)  8.47 us
    all_to_all x1, starting transfers between devices, exchanged(): rows = lax.all_to_all(sent, 'tm', split_axis=0, concat_axis=0, tiled=True)  6.1 us
    all_to_all x1, starting transfers between devices, body(): both = lax.all_to_all(both, EP, split_axis=0, concat_axis=0, tiled=True)  5.16 us
    all_to_all x1, starting transfers between devices, body(): pairs = lax.all_to_all(pairs, 'tm', split_axis=0, concat_axis=0, tiled=True)  5.11 us
    pallas_call x1, Pallas kernels, pack(): pl.pallas_call(functools.partial(pack_kernel, base), out_shape=(jax.Shape...  4.49 us
  transfers between devices with their start and end apart: 18, of which 6 were waited for; matrix products, arithmetic and copies ran while one was open for 0% of the time, Pallas kernels for 26%

profile of v7, /device:TPU:1, one launch (start us, length us, event | category | flops | bytes accessed | tf_op | source)
XLA Modules:
  0.0 109.8 jit_solution(11614487446578755732)
XLA Ops:
  0.7 4.5 %pack_rows.3 = (bf16[8,128,1024]{2,1,0:T(8,128)(2,1)}, s32[1]{0:T(128)}, s32[8,16]{1,0:T(8,128)}, s32[1,128]{1,0:T(1,128)}) custom-call(s32[3]{0:T(128)S(1)} %pad_add_fusion.place, s32[1,128]{1,0:T(1,128)} %bitcast.20, s32[1,128]{1,0:T(1,128)} %bitcast.22, bf16[64,16,1024]{2,1,0:T(8,128)(2,1)} %obs_hbm.1), custom_call_target="tpu_custom_call" | custom-call | flops 1000000000 | bytes 4194304 | tf_op jit(solution)/shard_map/pack_rows/pallas_call | solution.py:105
  5.2 6.1 %all-to-all-start.1 = ((bf16[8,128,1024]{2,1,0:T(8,128)(2,1)}), bf16[8,128,1024]{2,1,0:T(8,128)(2,1)}, u32[]{:S(2)}, u32[]{:S(2)}) async-start(bf16[8,128,1024]{2,1,0:T(8,128)(2,1)} %get-tuple-element.58), calls=%async_computation.1 | async-start | bytes 4194304 | tf_op jit(solution)/shard_map/all_to_all | solution.py:414
  11.4 2.7 %masked_rows.1 = (bf16[8,16,1024]{2,1,0:T(8,128)(2,1)}, bf16[8,16,1024]{2,1,0:T(8,128)(2,1)}, bf16[8,16,1024]{2,1,0:T(8,128)(2,1)}, bf16[8,16,1024]{2,1,0:T(8,12...) custom-call(s32[3]{0:T(128)S(1)} %pad_add_fusion.place, ...), custom_call_target="tpu_custom_call" | custom-call | flops 100000000 | bytes 6291456 | tf_op jit(solution)/shard_map/masked_rows/pallas_call | solution.py:156
  14.1 6.1 %collective-permute-start = (bf16[8,16,1024]{2,1,0:T(8,128)(2,1)}, bf16[8,16,1024]{2,1,0:T(8,128)(2,1)S(1)}, u32[]{:S(2)}, u32[]{:S(2)}) collective-permute-start(bf16[8,16,1024]{2,1,0:T(8,128)(2,1)} %get-tuple-element.42), channel_id=1, source_target_pairs={{0,10},{1,11},{2,8},{3,9},{4,14},{5,15},{6,12},{7,13},{8,2},{9,3},... | collective-permute-start | bytes 786440 | tf_op jit(solution)/shard_map/ppermute | solution.py:433
  20.2 2.5 %collective-permute-start.2 = (bf16[8,16,1024]{2,1,0:T(8,128)(2,1)}, bf16[8,16,1024]{2,1,0:T(8,128)(2,1)S(1)}, u32[]{:S(2)}, u32[]{:S(2)}) collective-permute-start(bf16[8,16,1024]{2,1,0:T(8,128)(2,1)} %get-tuple-element.44), channel_id=1, source_target_pairs={{0,9},{1,10},{2,11},{3,8},{4,13},{5,14},{6,15},{7,12},{8,1},{9,2},... | collective-permute-start | bytes 786440 | tf_op jit(solution)/shard_map/ppermute | solution.py:433
  22.7 2.6 %collective-permute-start.3 = (bf16[8,16,1024]{2,1,0:T(8,128)(2,1)}, bf16[8,16,1024]{2,1,0:T(8,128)(2,1)S(1)}, u32[]{:S(2)}, u32[]{:S(2)}) collective-permute-start(bf16[8,16,1024]{2,1,0:T(8,128)(2,1)} %get-tuple-element.45), channel_id=1, source_target_pairs={{0,11},{1,8},{2,9},{3,10},{4,15},{5,12},{6,13},{7,14},{8,3},{9,0},... | collective-permute-start | bytes 786440 | tf_op jit(solution)/shard_map/ppermute | solution.py:433
  25.3 3.9 %collective-permute-start.4 = (bf16[8,16,1024]{2,1,0:T(8,128)(2,1)}, bf16[8,16,1024]{2,1,0:T(8,128)(2,1)S(1)}, u32[]{:S(2)}, u32[]{:S(2)}) collective-permute-start(bf16[8,16,1024]{2,1,0:T(8,128)(2,1)} %get-tuple-element.46), channel_id=1, source_target_pairs={{0,14},{1,15},{2,12},{3,13},{4,2},{5,3},{6,0},{7,1},{8,6},{9,7},{1... | collective-permute-start | bytes 786440 | tf_op jit(solution)/shard_map/ppermute | solution.py:433
  29.2 8.5 %all-to-all-done.1 = bf16[8,128,1024]{2,1,0:T(8,128)(2,1)} async-done(((bf16[8,128,1024]{2,1,0:T(8,128)(2,1)}), bf16[8,128,1024]{2,1,0:T(8,128)(2,1)}, u32[]{:S(2)}, u32[]{:S(2)}) %all-to-all-start.1) | async-done | bytes 2097184 | tf_op jit(solution)/shard_map/all_to_all | solution.py:414
  38.4 1.3 %copy-done.3 = bf16[1024,1024]{1,0:T(8,128)(2,1)} copy-done((bf16[1024,1024]{1,0:T(8,128)(2,1)}, bf16[1024,1024]{1,0:T(8,128)(2,1)S(1)}, u32[]{:S(2)}) %copy-start.3) | copy-done | bytes 2097176
  39.7 3.6 %collective-permute-start.5 = (bf16[8,16,1024]{2,1,0:T(8,128)(2,1)}, bf16[8,16,1024]{2,1,0:T(8,128)(2,1)S(1)}, u32[]{:S(2)}, u32[]{:S(2)}) collective-permute-start(bf16[8,16,1024]{2,1,0:T(8,128)(2,1)} %get-tuple-element.47), channel_id=1, source_target_pairs={{0,2},{1,3},{2,0},{3,1},{4,6},{5,7},{6,4},{7,5},{8,10},{9,11},{10,... | collective-permute-start | bytes 786440 | tf_op jit(solution)/shard_map/ppermute | solution.py:433
  43.3 1.7 %collective-permute-start.6 = (bf16[8,16,1024]{2,1,0:T(8,128)(2,1)}, bf16[8,16,1024]{2,1,0:T(8,128)(2,1)S(1)}, u32[]{:S(2)}, u32[]{:S(2)}) collective-permute-start(bf16[8,16,1024]{2,1,0:T(8,128)(2,1)} %get-tuple-element.48), channel_id=1, source_target_pairs={{0,5},{1,6},{2,7},{3,4},{4,9},{5,10},{6,11},{7,8},{8,13},{9,14},{1... | collective-permute-start | bytes 786440 | tf_op jit(solution)/shard_map/ppermute | solution.py:433
  44.9 2.5 %collective-permute-done.2.refs_3_ = bf16[8,16,1024]{2,1,0:T(8,128)(2,1)S(1)} collective-permute-done((bf16[8,16,1024]{2,1,0:T(8,128)(2,1)}, bf16[8,16,1024]{2,1,0:T(8,128)(2,1)S(1)}, u32[]{:S(2)}, u32[]{:S(2)}) %collective-permute-start.2) | collective-permute-done | bytes 262176 | tf_op jit(solution)/shard_map/ppermute | solution.py:433
  47.8 9.0 %collective-permute-done.3.refs_4_ = bf16[8,16,1024]{2,1,0:T(8,128)(2,1)S(1)} collective-permute-done((bf16[8,16,1024]{2,1,0:T(8,128)(2,1)}, bf16[8,16,1024]{2,1,0:T(8,128)(2,1)S(1)}, u32[]{:S(2)}, u32[]{:S(2)}) %collective-permute-start.3) | collective-permute-done | bytes 262176 | tf_op jit(solution)/shard_map/ppermute | solution.py:433
  56.8 21.1 %burn_in.1 = bf16[8,2,16,512]{3,2,1,0:T(8,128)(2,1)} custom-call(s32[3]{0:T(128)S(1)} %pad_add_fusion.place, s32[1]{0:T(128)} %get-tuple-element.60.crowded, bf16[1024,1024]{1,0:T(8,128)(2,1)} %bitcast.8.rows_hbm, bf16[1024,1024]{1,0:T(8,128)(2,1)} %copy-done.3, bf16[1024,2048]{1,0:T(8,128)(2,1)} %win_hbm.1, bf16[512,2048]{1,0:T(8,128)(2,1)} %wh_hbm.1, ...), custom_call_target="tpu_custom_call" | custom-call | flops 30000001024 | bytes 8388608 | tf_op jit(solution)/shard_map/burn_in/pallas_call | solution.py:304
  78.0 5.1 %all-to-all-start.2 = ((bf16[8,2,16,512]{3,2,1,0:T(8,128)(2,1)}), bf16[8,2,16,512]{3,2,1,0:T(8,128)(2,1)S(1)}, u32[]{:S(2)}, u32[]{:S(2)}) async-start(bf16[8,2,16,512]{3,2,1,0:T(8,128)(2,1)} %burn_in.1), calls=%async_computation.2 | async-start | bytes 524288 | tf_op jit(solution)/shard_map/all_to_all | solution.py:447
  83.1 5.9 %collective-permute-start.10 = (bf16[8,16,1024]{2,1,0:T(8,128)(2,1)}, bf16[8,16,1024]{2,1,0:T(8,128)(2,1)S(1)}, u32[]{:S(2)}, u32[]{:S(2)}) collective-permute-start(bf16[8,16,1024]{2,1,0:T(8,128)(2,1)} %get-tuple-element.52), channel_id=1, source_target_pairs={{0,15},{1,12},{2,13},{3,14},{4,3},{5,0},{6,1},{7,2},{8,7},{9,4},{1... | collective-permute-start | bytes 786440 | tf_op jit(solution)/shard_map/ppermute | solution.py:433
  89.0 2.7 %collective-permute-start.12 = (bf16[8,16,1024]{2,1,0:T(8,128)(2,1)}, bf16[8,16,1024]{2,1,0:T(8,128)(2,1)}, u32[]{:S(2)}, u32[]{:S(2)}) collective-permute-start(bf16[8,16,1024]{2,1,0:T(8,128)(2,1)} %get-tuple-element.54), channel_id=1, source_target_pairs={{0,3},{1,0},{2,1},{3,2},{4,7},{5,4},{6,5},{7,6},{8,11},{9,8},{10,9... | collective-permute-start | bytes 786440 | tf_op jit(solution)/shard_map/ppermute | solution.py:433
  91.7 1.6 %collective-permute-start.13 = (bf16[8,16,1024]{2,1,0:T(8,128)(2,1)}, bf16[8,16,1024]{2,1,0:T(8,128)(2,1)}, u32[]{:S(2)}, u32[]{:S(2)}) collective-permute-start(bf16[8,16,1024]{2,1,0:T(8,128)(2,1)} %get-tuple-element.55), channel_id=1, source_target_pairs={{0,4},{1,5},{2,6},{3,7},{4,8},{5,9},{6,10},{7,11},{8,12},{9,13},{1... | collective-permute-start | bytes 786440 | tf_op jit(solution)/shard_map/ppermute | solution.py:433
  93.2 1.1 %collective-permute-start.14 = (bf16[8,16,1024]{2,1,0:T(8,128)(2,1)}, bf16[8,16,1024]{2,1,0:T(8,128)(2,1)}, u32[]{:S(2)}, u32[]{:S(2)}) collective-permute-start(bf16[8,16,1024]{2,1,0:T(8,128)(2,1)} %get-tuple-element.56), channel_id=1, source_target_pairs={{0,12},{1,13},{2,14},{3,15},{4,0},{5,1},{6,2},{7,3},{8,4},{9,5},{1... | collective-permute-start | bytes 786440 | tf_op jit(solution)/shard_map/ppermute | solution.py:433
  94.4 1.0 learner_order.1
  95.4 5.2 %all-to-all-start.3 = ((bf16[16,8,1152]{2,1,0:T(8,128)(2,1)}), bf16[16,8,1152]{2,1,0:T(8,128)(2,1)S(1)}, u32[]{:S(2)}, u32[]{:S(2)}) async-start(bf16[16,8,1152]{2,1,0:T(8,128)(2,1)} %bitcast.13), calls=%async_computation.3 | async-start | bytes 589824 | tf_op jit(solution)/shard_map/all_to_all | solution.py:451
  100.6 1.6 %collective-permute-done.12.refs_13_ = bf16[8,16,1024]{2,1,0:T(8,128)(2,1)} collective-permute-done((bf16[8,16,1024]{2,1,0:T(8,128)(2,1)}, bf16[8,16,1024]{2,1,0:T(8,128)(2,1)}, u32[]{:S(2)}, u32[]{:S(2)}) %collective-permute-start.12) | collective-permute-done | bytes 262176 | tf_op jit(solution)/shard_map/ppermute | solution.py:433
  102.9 3.3 %place_rows.1 = bf16[128,16,1024]{2,1,0:T(8,128)(2,1)} custom-call(s32[3]{0:T(128)S(1)} %pad_add_fusion.place, bf16[8,16,1024]{2,1,0:T(8,128)(2,1)S(1)} %copy-done, bf16[8,16,1024]{2,1,0:T(8,128)(2,1)S(1)} %collective-permute-done.refs_1_, bf16[8,16,1024]{2,1,0:T(8,128)(2,1)S(1)} %collective-permute-done.1.refs_2_, ...), custom_call_target="tpu_custom_call" | custom-call | flops 1000000000 | bytes 8388608 | tf_op jit(solution)/shard_map/place_rows/pallas_call | solution.py:188
  106.2 2.1 %all-to-all-done.3 = bf16[16,8,1152]{2,1,0:T(8,128)(2,1)S(1)} async-done(((bf16[16,8,1152]{2,1,0:T(8,128)(2,1)}), bf16[16,8,1152]{2,1,0:T(8,128)(2,1)S(1)}, u32[]{:S(2)}, u32[]{:S(2)}) %all-to-all-start.3) | async-done | bytes 294944 | tf_op jit(solution)/shard_map/all_to_all | solution.py:451
  (38 shorter events, 2.8 us)
Async XLA Ops:
  5.2 6.1 %copy-start.2 = (bf16[64,16,1024]{2,1,0:T(8,128)(2,1)S(1)}, bf16[64,16,1024]{2,1,0:T(8,128)(2,1)}, u32[]{:S(2)}) copy-start(bf16[64,16,1024]{2,1,0:T(8,128)(2,1)} %obs_hbm.1) | copy-start | bytes 6291460
  5.2 6.1 %copy-start.4 = (s32[128]{0:T(128)S(1)}, s32[128]{0:T(128)}, u32[]{:S(2)}) copy-start(s32[128]{0:T(128)} %ids.1) | copy-start | bytes 1540
  5.2 6.1 %copy-start.5 = (s32[128]{0:T(128)S(1)}, s32[128]{0:T(128)}, u32[]{:S(2)}) copy-start(s32[128]{0:T(128)} %starts.1) | copy-start | bytes 1540
  5.2 32.4 %all-to-all-start.1 = ((bf16[8,128,1024]{2,1,0:T(8,128)(2,1)}), bf16[8,128,1024]{2,1,0:T(8,128)(2,1)}, u32[]{:S(2)}, u32[]{:S(2)}) async-start(bf16[8,128,1024]{2,1,0:T(8,128)(2,1)} %get-tuple-element.58), calls=%async_computation.1 | async-start | bytes 4194304 | tf_op jit(solution)/shard_map/all_to_all | solution.py:414
  14.1 24.3 %collective-permute-start = (bf16[8,16,1024]{2,1,0:T(8,128)(2,1)}, bf16[8,16,1024]{2,1,0:T(8,128)(2,1)S(1)}, u32[]{:S(2)}, u32[]{:S(2)}) collective-permute-start(bf16[8,16,1024]{2,1,0:T(8,128)(2,1)} %get-tuple-element.42), channel_id=1, source_target_pairs={{0,10},{1,11},{2,8},{3,9},{4,14},{5,15},{6,12},{7,13},{8,2},{9,3},... | collective-permute-start | bytes 786440 | tf_op jit(solution)/shard_map/ppermute | solution.py:433
  20.2 23.0 %collective-permute-start.1 = (bf16[8,16,1024]{2,1,0:T(8,128)(2,1)}, bf16[8,16,1024]{2,1,0:T(8,128)(2,1)S(1)}, u32[]{:S(2)}, u32[]{:S(2)}) collective-permute-start(bf16[8,16,1024]{2,1,0:T(8,128)(2,1)} %get-tuple-element.43), channel_id=1, source_target_pairs={{0,6},{1,7},{2,4},{3,5},{4,10},{5,11},{6,8},{7,9},{8,14},{9,15},{1... | collective-permute-start | bytes 786440 | tf_op jit(solution)/shard_map/ppermute | solution.py:433
  20.2 27.2 %collective-permute-start.2 = (bf16[8,16,1024]{2,1,0:T(8,128)(2,1)}, bf16[8,16,1024]{2,1,0:T(8,128)(2,1)S(1)}, u32[]{:S(2)}, u32[]{:S(2)}) collective-permute-start(bf16[8,16,1024]{2,1,0:T(8,128)(2,1)} %get-tuple-element.44), channel_id=1, source_target_pairs={{0,9},{1,10},{2,11},{3,8},{4,13},{5,14},{6,15},{7,12},{8,1},{9,2},... | collective-permute-start | bytes 786440 | tf_op jit(solution)/shard_map/ppermute | solution.py:433
  22.7 34.1 %collective-permute-start.3 = (bf16[8,16,1024]{2,1,0:T(8,128)(2,1)}, bf16[8,16,1024]{2,1,0:T(8,128)(2,1)S(1)}, u32[]{:S(2)}, u32[]{:S(2)}) collective-permute-start(bf16[8,16,1024]{2,1,0:T(8,128)(2,1)} %get-tuple-element.45), channel_id=1, source_target_pairs={{0,11},{1,8},{2,9},{3,10},{4,15},{5,12},{6,13},{7,14},{8,3},{9,0},... | collective-permute-start | bytes 786440 | tf_op jit(solution)/shard_map/ppermute | solution.py:433
  25.3 31.5 %collective-permute-start.4 = (bf16[8,16,1024]{2,1,0:T(8,128)(2,1)}, bf16[8,16,1024]{2,1,0:T(8,128)(2,1)S(1)}, u32[]{:S(2)}, u32[]{:S(2)}) collective-permute-start(bf16[8,16,1024]{2,1,0:T(8,128)(2,1)} %get-tuple-element.46), channel_id=1, source_target_pairs={{0,14},{1,15},{2,12},{3,13},{4,2},{5,3},{6,0},{7,1},{8,6},{9,7},{1... | collective-permute-start | bytes 786440 | tf_op jit(solution)/shard_map/ppermute | solution.py:433
  39.7 43.4 %collective-permute-start.5 = (bf16[8,16,1024]{2,1,0:T(8,128)(2,1)}, bf16[8,16,1024]{2,1,0:T(8,128)(2,1)S(1)}, u32[]{:S(2)}, u32[]{:S(2)}) collective-permute-start(bf16[8,16,1024]{2,1,0:T(8,128)(2,1)} %get-tuple-element.47), channel_id=1, source_target_pairs={{0,2},{1,3},{2,0},{3,1},{4,6},{5,7},{6,4},{7,5},{8,10},{9,11},{10,... | collective-permute-start | bytes 786440 | tf_op jit(solution)/shard_map/ppermute | solution.py:433
  43.3 45.7 %collective-permute-start.6 = (bf16[8,16,1024]{2,1,0:T(8,128)(2,1)}, bf16[8,16,1024]{2,1,0:T(8,128)(2,1)S(1)}, u32[]{:S(2)}, u32[]{:S(2)}) collective-permute-start(bf16[8,16,1024]{2,1,0:T(8,128)(2,1)} %get-tuple-element.48), channel_id=1, source_target_pairs={{0,5},{1,6},{2,7},{3,4},{4,9},{5,10},{6,11},{7,8},{8,13},{9,14},{1... | collective-permute-start | bytes 786440 | tf_op jit(solution)/shard_map/ppermute | solution.py:433
  47.4 41.6 %collective-permute-start.7 = (bf16[8,16,1024]{2,1,0:T(8,128)(2,1)}, bf16[8,16,1024]{2,1,0:T(8,128)(2,1)S(1)}, u32[]{:S(2)}, u32[]{:S(2)}) collective-permute-start(bf16[8,16,1024]{2,1,0:T(8,128)(2,1)} %get-tuple-element.49), channel_id=1, source_target_pairs={{0,7},{1,4},{2,5},{3,6},{4,11},{5,8},{6,9},{7,10},{8,15},{9,12},{1... | collective-permute-start | bytes 786440 | tf_op jit(solution)/shard_map/ppermute | solution.py:433
  56.8 34.9 %collective-permute-start.8 = (bf16[8,16,1024]{2,1,0:T(8,128)(2,1)}, bf16[8,16,1024]{2,1,0:T(8,128)(2,1)S(1)}, u32[]{:S(2)}, u32[]{:S(2)}) collective-permute-start(bf16[8,16,1024]{2,1,0:T(8,128)(2,1)} %get-tuple-element.50), channel_id=1, source_target_pairs={{0,8},{1,9},{2,10},{3,11},{4,12},{5,13},{6,14},{7,15},{8,0},{9,1},... | collective-permute-start | bytes 786440 | tf_op jit(solution)/shard_map/ppermute | solution.py:433
  56.8 36.4 %collective-permute-start.9 = (bf16[8,16,1024]{2,1,0:T(8,128)(2,1)}, bf16[8,16,1024]{2,1,0:T(8,128)(2,1)S(1)}, u32[]{:S(2)}, u32[]{:S(2)}) collective-permute-start(bf16[8,16,1024]{2,1,0:T(8,128)(2,1)} %get-tuple-element.51), channel_id=1, source_target_pairs={{0,13},{1,14},{2,15},{3,12},{4,1},{5,2},{6,3},{7,0},{8,5},{9,6},{1... | collective-permute-start | bytes 786440 | tf_op jit(solution)/shard_map/ppermute | solution.py:433
  56.8 37.6 %copy-start.6 = (s32[128]{0:T(128)S(1)}, s32[128]{0:T(128)}, u32[]{:S(2)}) copy-start(s32[128]{0:T(128)} %param.17) | copy-start | bytes 1540
  56.8 37.6 %copy-start.1 = (s32[1,128]{1,0:T(1,128)S(1)}, s32[1,128]{1,0:T(1,128)}, u32[]{:S(2)}) copy-start(s32[1,128]{1,0:T(1,128)} %get-tuple-element.62.rank) | copy-start | bytes 1540
  56.8 46.0 %copy-start = (bf16[8,16,1024]{2,1,0:T(8,128)(2,1)S(1)}, bf16[8,16,1024]{2,1,0:T(8,128)(2,1)}, u32[]{:S(2)}) copy-start(bf16[8,16,1024]{2,1,0:T(8,128)(2,1)} %get-tuple-element.41.refs_0_) | copy-start | bytes 786436
  78.0 16.4 %all-to-all-start.2 = ((bf16[8,2,16,512]{3,2,1,0:T(8,128)(2,1)}), bf16[8,2,16,512]{3,2,1,0:T(8,128)(2,1)S(1)}, u32[]{:S(2)}, u32[]{:S(2)}) async-start(bf16[8,2,16,512]{3,2,1,0:T(8,128)(2,1)} %burn_in.1), calls=%async_computation.2 | async-start | bytes 524288 | tf_op jit(solution)/shard_map/all_to_all | solution.py:447
  83.1 17.5 %collective-permute-start.10 = (bf16[8,16,1024]{2,1,0:T(8,128)(2,1)}, bf16[8,16,1024]{2,1,0:T(8,128)(2,1)S(1)}, u32[]{:S(2)}, u32[]{:S(2)}) collective-permute-start(bf16[8,16,1024]{2,1,0:T(8,128)(2,1)} %get-tuple-element.52), channel_id=1, source_target_pairs={{0,15},{1,12},{2,13},{3,14},{4,3},{5,0},{6,1},{7,2},{8,7},{9,4},{1... | collective-permute-start | bytes 786440 | tf_op jit(solution)/shard_map/ppermute | solution.py:433
  89.0 11.6 %collective-permute-start.11 = (bf16[8,16,1024]{2,1,0:T(8,128)(2,1)}, bf16[8,16,1024]{2,1,0:T(8,128)(2,1)}, u32[]{:S(2)}, u32[]{:S(2)}) collective-permute-start(bf16[8,16,1024]{2,1,0:T(8,128)(2,1)} %get-tuple-element.53), channel_id=1, source_target_pairs={{0,1},{1,2},{2,3},{3,0},{4,5},{5,6},{6,7},{7,4},{8,9},{9,10},{10,1... | collective-permute-start | bytes 786440 | tf_op jit(solution)/shard_map/ppermute | solution.py:433
  89.0 13.2 %collective-permute-start.12 = (bf16[8,16,1024]{2,1,0:T(8,128)(2,1)}, bf16[8,16,1024]{2,1,0:T(8,128)(2,1)}, u32[]{:S(2)}, u32[]{:S(2)}) collective-permute-start(bf16[8,16,1024]{2,1,0:T(8,128)(2,1)} %get-tuple-element.54), channel_id=1, source_target_pairs={{0,3},{1,0},{2,1},{3,2},{4,7},{5,4},{6,5},{7,6},{8,11},{9,8},{10,9... | collective-permute-start | bytes 786440 | tf_op jit(solution)/shard_map/ppermute | solution.py:433
  91.7 10.5 %collective-permute-start.13 = (bf16[8,16,1024]{2,1,0:T(8,128)(2,1)}, bf16[8,16,1024]{2,1,0:T(8,128)(2,1)}, u32[]{:S(2)}, u32[]{:S(2)}) collective-permute-start(bf16[8,16,1024]{2,1,0:T(8,128)(2,1)} %get-tuple-element.55), channel_id=1, source_target_pairs={{0,4},{1,5},{2,6},{3,7},{4,8},{5,9},{6,10},{7,11},{8,12},{9,13},{1... | collective-permute-start | bytes 786440 | tf_op jit(solution)/shard_map/ppermute | solution.py:433
  93.2 9.6 %collective-permute-start.14 = (bf16[8,16,1024]{2,1,0:T(8,128)(2,1)}, bf16[8,16,1024]{2,1,0:T(8,128)(2,1)}, u32[]{:S(2)}, u32[]{:S(2)}) collective-permute-start(bf16[8,16,1024]{2,1,0:T(8,128)(2,1)} %get-tuple-element.56), channel_id=1, source_target_pairs={{0,12},{1,13},{2,14},{3,15},{4,0},{5,1},{6,2},{7,3},{8,4},{9,5},{1... | collective-permute-start | bytes 786440 | tf_op jit(solution)/shard_map/ppermute | solution.py:433
  95.4 12.9 %all-to-all-start.3 = ((bf16[16,8,1152]{2,1,0:T(8,128)(2,1)}), bf16[16,8,1152]{2,1,0:T(8,128)(2,1)S(1)}, u32[]{:S(2)}, u32[]{:S(2)}) async-start(bf16[16,8,1152]{2,1,0:T(8,128)(2,1)} %bitcast.13), calls=%async_computation.3 | async-start | bytes 589824 | tf_op jit(solution)/shard_map/all_to_all | solution.py:451
  (1 other events, 1.3 us)
